TPU v7x, 32 devices: a whole 2x2x4 slice. The times are simulated.
32 devices in a mesh: dp: 8 (over y, x, core), shard: 4 (over z).
Axes of the slice: x: 2, y: 2, z: 4, core: 2. Of those that a mesh axis runs over, the one named last changes fastest.
Arguments:
- tokens: bfloat16 [8, 1024, 2048], P('dp', 'shard'), may hold values from -6 to 6
- block_order: int32 [8, 8], P('dp'), may hold values from 0 to 7, as said below
- attn_gain: float32 [2048], P('shard'), may hold values from 0.1 to 1.9
- w_query: float32 [2048, 2048], P('shard'), may hold values from -0.125 to 0.125
- w_key: float32 [2048, 256], P('shard'), may hold values from -0.125 to 0.125
- w_value: float32 [2048, 256], P('shard'), may hold values from -0.125 to 0.125
- w_out: float32 [2048, 2048], P('shard'), may hold values from -0.75 to 0.75
- mlp_gain: float32 [2048], P('shard'), may hold values from 0.1 to 1.9
- w_gate: float32 [2048, 5632], P('shard'), may hold values from -0.125 to 0.125
- w_up: float32 [2048, 5632], P('shard'), may hold values from -0.125 to 0.125
- w_down: float32 [5632, 2048], P('shard'), may hold values from -0.078125 to 0.078125
- cotangent: bfloat16 [8, 1024, 2048], P('dp', 'shard'), may hold values from -6 to 6
Outputs:
- block_out: bfloat16 [8, 1024, 2048], P('dp', 'shard')
- tokens_grad: float32 [8, 1024, 2048], P('dp', 'shard')
- attn_gain_grad: float32 [2048], P('shard')
- w_query_grad: float32 [2048, 2048], P('shard')
- w_key_grad: float32 [2048, 256], P('shard')
- w_value_grad: float32 [2048, 256], P('shard')
- w_out_grad: float32 [2048, 2048], P('shard')
- mlp_gain_grad: float32 [2048], P('shard')
- w_gate_grad: float32 [2048, 5632], P('shard')
- w_up_grad: float32 [2048, 5632], P('shard')
- w_down_grad: float32 [5632, 2048], P('shard')
Inputs may be any that keep to these rules, and one draw needn't show every extreme that they name: `block_order`: in each row every number of 0 to 7 appears once, and entries 2 j and 2 j + 1 of a row add up to 7.
All inputs are finite; a program needn't handle non-finite values.
Results may differ from a plain program's by a relative error of at most 0.023.
Values may be sent and summed in bfloat16 or wider, within the bound.
A program may use at most 448 MiB of HBM per device.

v0:
```python
import functools

import jax
import jax.numpy as jnp
from jax import lax
from jax.experimental import pallas as pl
from jax.sharding import PartitionSpec as P

HEAD_DIM = 64
EPSILON = 1e-05
ROPE_BASE = 10000.0
MASKED = -1e30
LOW = jnp.bfloat16
FULL = jnp.float32
EXTRA = 32


def contract(left, right, left_dim, right_dim):
    return lax.dot_general(
        left, right, (((left_dim,), (right_dim,)), ((), ())), preferred_element_type=FULL
    )


def shift(value, amount):
    count = lax.axis_size("shard")
    pairs = [(i, (i + amount) % count) for i in range(count)]
    return lax.ppermute(value, "shard", pairs)


def plane_parts(value):
    count = lax.axis_size("shard")
    return [value] + [shift(value, k) for k in range(1, count)]


def assemble(parts, axis=0):
    count = lax.axis_size("shard")
    rank = lax.axis_index("shard")
    rows = parts[0].shape[axis]
    shape = list(parts[0].shape)
    shape[axis] = rows * count
    whole = jnp.zeros(shape, parts[0].dtype)
    for k, part in enumerate(parts):
        place = lax.rem(rank - k + count, count)
        whole = lax.dynamic_update_slice_in_dim(whole, part, place * rows, axis)
    return whole


def plane_send(value):
    count = lax.axis_size("shard")
    rank = lax.axis_index("shard")
    rows = value.shape[0] // count
    parts = []
    for k in range(count):
        target = lax.rem(rank + k, count)
        piece = lax.dynamic_slice_in_dim(value, target * rows, rows, 0)
        parts.append(shift(piece, k) if k else piece)
    return parts


def plane_sum(parts):
    total = parts[0].astype(FULL)
    for part in parts[1:]:
        total = total + part.astype(FULL)
    return total.astype(LOW)


def rope(values, cosine, sine):
    half = values.shape[-2] // 2
    front, back = values[..., :half, :], values[..., half:, :]
    return jnp.concatenate([front * cosine - back * sine, back * cosine + front * sine], axis=-2)


def places_of(table, plane, rows, span):
    blocks = rows // span
    count = table.shape[1] // blocks
    grouped = table.reshape(table.shape[0], count, blocks)
    picked = lax.dynamic_slice_in_dim(grouped, plane, 1, 1)[:, 0]
    within = jnp.arange(span, dtype=jnp.int32)
    return (picked[:, :, None] * span + within[None, None, :]).reshape(table.shape[0], rows)


def spread_kernel(lanes, planes, unit, piece_ref, gate_ref, up_ref):
    for which, out_ref in enumerate((gate_ref, up_ref)):
        for p in range(planes):
            for d in range(lanes):
                start = (which * planes + p) * unit
                place = (p * lanes + d) * unit
                out_ref[:, place : place + unit] = piece_ref[d, :, start : start + unit].astype(FULL)


def spread_mlp(pieces, planes, unit):
    lanes, rows, cols = pieces.shape
    block = min(64, rows)
    full = jax.ShapeDtypeStruct((rows, lanes * planes * unit), FULL)
    spec = pl.BlockSpec((block, lanes * planes * unit), lambda i: (i, 0))
    return pl.pallas_call(
        functools.partial(spread_kernel, lanes, planes, unit),
        out_shape=(full, full),
        grid=(rows // block,),
        in_specs=[pl.BlockSpec((lanes, block, cols), lambda i: (0, i, 0))],
        out_specs=(spec, spec),
        cost_estimate=pl.CostEstimate(
            flops=0, bytes_accessed=lanes * rows * cols * 6, transcendentals=0
        ),
    )(pieces)


def gather_kernel(lanes, head_cols, out_cols, sharing, piece_ref, q_ref, k_ref, v_ref, o_ref):
    first_key, first_value = head_cols, head_cols + HEAD_DIM
    first_out = head_cols + 2 * HEAD_DIM
    for d in range(lanes):
        q_ref[:, d * head_cols : (d + 1) * head_cols] = piece_ref[d, :, :head_cols].astype(FULL)
        o_ref[:, d * out_cols : (d + 1) * out_cols] = piece_ref[d, :, first_out:].astype(FULL)
    for h in range(lanes // sharing):
        for start, out_ref in ((first_key, k_ref), (first_value, v_ref)):
            total = None
            for d in range(h * sharing, (h + 1) * sharing):
                part = piece_ref[d, :, start : start + HEAD_DIM].astype(FULL)
                total = part if total is None else total + part
            out_ref[:, h * HEAD_DIM : (h + 1) * HEAD_DIM] = total


def spread_attn(pieces, rows, head_cols, out_cols, kv_heads):
    lanes, _, cols = pieces.shape
    widths = (lanes * head_cols, kv_heads * HEAD_DIM, kv_heads * HEAD_DIM, lanes * out_cols)
    return pl.pallas_call(
        functools.partial(gather_kernel, lanes, head_cols, out_cols, lanes // kv_heads),
        out_shape=tuple(jax.ShapeDtypeStruct((rows, w), FULL) for w in widths),
        grid=(rows // EXTRA,),
        in_specs=[pl.BlockSpec((lanes, EXTRA, cols), lambda i: (0, i, 0))],
        out_specs=tuple(pl.BlockSpec((EXTRA, w), lambda i: (i, 0)) for w in widths),
        cost_estimate=pl.CostEstimate(
            flops=0, bytes_accessed=lanes * rows * cols * 6, transcendentals=0
        ),
    )(pieces)


def norm_back(upstream, normed, row_scale, gain):
    scaled = upstream * gain
    gain_grad = jnp.sum(upstream * normed, axis=0)
    mean = jnp.mean(scaled * normed, axis=-1, keepdims=True)
    return row_scale * (scaled - normed * mean), gain_grad


def on_device(
    tokens,
    block_order,
    attn_gain,
    w_query,
    w_key,
    w_value,
    w_out,
    mlp_gain,
    w_gate,
    w_up,
    w_down,
    cotangent,
):
    planes = lax.axis_size("shard")
    plane = lax.axis_index("shard")
    lanes = lax.axis_size("dp")
    lane = lax.axis_index("dp")
    rows = tokens.shape[1]
    width = tokens.shape[2]
    span = rows // 2
    seqs = lanes
    total_rows = seqs * rows
    own_width = width // planes
    heads = w_query.shape[1] // HEAD_DIM
    kv_heads = w_key.shape[1] // HEAD_DIM
    own_heads = heads // lanes
    head_cols = own_heads * HEAD_DIM
    kv_head = (lane * own_heads * kv_heads) // heads
    out_cols = w_out.shape[1] // lanes
    ff_rows = w_down.shape[0]
    unit = ff_rows // lanes
    own_ff = unit * planes
    scale = HEAD_DIM ** (-0.5)

    inputs = lax.all_gather(tokens[0], "dp", axis=0, tiled=True)
    upstream = lax.all_gather(cotangent[0], "dp", axis=0, tiled=True)
    table = lax.all_gather(block_order[0], "dp", axis=0, tiled=False)

    def columns(weight, start, count):
        return lax.dynamic_slice_in_dim(weight, start, count, 1).astype(LOW)

    attn_piece = jnp.concatenate(
        [
            columns(w_query, lane * head_cols, head_cols),
            columns(w_key, kv_head * HEAD_DIM, HEAD_DIM),
            columns(w_value, kv_head * HEAD_DIM, HEAD_DIM),
            columns(w_out, lane * out_cols, out_cols),
        ],
        axis=1,
    )
    piece_cols = attn_piece.shape[1]
    gain_rows = jnp.stack([attn_gain, mlp_gain]).astype(LOW)
    gain_rows = jnp.pad(gain_rows, ((0, EXTRA - 2), (0, piece_cols - own_width)))
    attn_parts = plane_parts(jnp.concatenate([attn_piece, gain_rows], axis=0))
    attn_mat = assemble([part[:own_width] for part in attn_parts])
    gains = assemble([part[own_width : own_width + 2, :own_width] for part in attn_parts], 1)
    gain_one, gain_two = gains[0].astype(FULL), gains[1].astype(FULL)
    qkv_cols = head_cols + 2 * HEAD_DIM
    qkv_mat = attn_mat[:, :qkv_cols]
    out_mat = attn_mat[:, qkv_cols:]

    mlp_piece = jnp.concatenate(
        [
            columns(weight, p * ff_rows + lane * unit, unit)
            for weight in (w_gate, w_up)
            for p in range(planes)
        ],
        axis=1,
    )
    mlp_parts = plane_parts(mlp_piece)
    mlp_mat = assemble(mlp_parts)
    down_piece = lax.dynamic_slice_in_dim(w_down, lane * unit, unit, 0).astype(LOW)
    down_parts = plane_parts(down_piece)
    down_mat = assemble(down_parts)

    first_row = lane * head_cols
    owner = first_row // own_width
    row_piece = lax.dynamic_slice_in_dim(w_out, first_row - owner * own_width, head_cols, 0).astype(
        LOW
    )
    out_rows = jnp.where(owner == plane, row_piece, jnp.zeros_like(row_piece))
    for k in range(1, planes):
        pairs = []
        for d in range(lanes):
            source = (d * head_cols) // own_width
            pairs.append((d * planes + source, d * planes + (source + k) % planes))
        out_rows = out_rows + lax.ppermute(row_piece, ("dp", "shard"), pairs)

    query_places = places_of(table, plane, rows, span)
    frequency = ROPE_BASE ** (
        -(jnp.arange(HEAD_DIM // 2, dtype=FULL) * 2.0) / HEAD_DIM
    )
    angles = frequency[:, None] * query_places.reshape(-1).astype(FULL)[None, :]
    cosine, sine = jnp.cos(angles), jnp.sin(angles)

    wide = inputs.astype(FULL)
    scale_one = lax.rsqrt(jnp.mean(wide * wide, axis=-1, keepdims=True) + EPSILON)
    hidden_one = (wide * scale_one * gain_one).astype(LOW)
    qkv = contract(qkv_mat, hidden_one, 0, 1)
    query = rope(qkv[:head_cols].reshape(own_heads, HEAD_DIM, total_rows), cosine, sine)
    query = query.astype(LOW)
    key = rope(qkv[head_cols : head_cols + HEAD_DIM], cosine, sine).astype(LOW)
    value = qkv[head_cols + HEAD_DIM :].astype(LOW)
    kv_parts = plane_parts(jnp.concatenate([key, value], axis=0))
    key_places = jnp.concatenate(
        [places_of(table, lax.rem(plane - k + planes, planes), rows, span) for k in range(planes)],
        axis=1,
    )
    kv_all = jnp.stack(kv_parts, axis=0).reshape(planes, 2, HEAD_DIM, seqs, rows)
    kv_all = jnp.transpose(kv_all, (1, 3, 0, 4, 2)).reshape(2, seqs, planes * rows, HEAD_DIM)
    key_all, value_all = kv_all[0], kv_all[1]
    query_heads = jnp.transpose(
        query.reshape(own_heads, HEAD_DIM, seqs, rows), (2, 0, 3, 1)
    )
    visible = (key_places[:, :, None] <= query_places[:, None, :])[:, None]
    scores = (
        jnp.einsum("shqd,skd->shkq", query_heads, key_all, preferred_element_type=FULL) * scale
    )
    scores = jnp.where(visible, scores, MASKED)
    top = jnp.max(scores, axis=2, keepdims=True)
    weights = jnp.exp(scores - top)
    total = jnp.sum(weights, axis=2, keepdims=True)
    probability = weights / total
    log_total = top + jnp.log(total)
    attended = jnp.einsum(
        "shkq,skd->hdsq", probability.astype(LOW), value_all, preferred_element_type=FULL
    ).reshape(head_cols, total_rows)

    attended_all = lax.all_gather(attended.astype(LOW), "dp", axis=0, tiled=True)
    branch = contract(out_mat, attended_all, 0, 0)
    own_inputs = lax.dynamic_slice_in_dim(inputs, lane * out_cols, out_cols, 1)
    middle_part = (own_inputs.astype(FULL).T + branch).astype(LOW)
    middle = lax.all_gather(middle_part, "dp", axis=0, tiled=True)
    wide_two = middle.astype(FULL)
    scale_two = lax.rsqrt(jnp.mean(wide_two * wide_two, axis=0, keepdims=True) + EPSILON)
    hidden_two = (wide_two * scale_two * gain_two[:, None]).astype(LOW)
    both = contract(mlp_mat, hidden_two, 0, 0)
    gate_value, up_value = both[:own_ff], both[own_ff:]
    sigmoid = jax.nn.sigmoid(gate_value)
    silu = gate_value * sigmoid
    inner = (silu * up_value).astype(LOW)

    inner_grad = contract(down_mat, upstream, 1, 1)
    gate_grad = inner_grad * up_value * sigmoid * (1.0 + gate_value * (1.0 - sigmoid))
    up_grad = inner_grad * silu
    both_grad = jnp.concatenate([gate_grad.astype(LOW), up_grad.astype(LOW)], axis=0)
    hidden_two_grad = contract(both_grad, mlp_mat, 0, 1).astype(LOW)
    hidden_two_own = lax.psum_scatter(hidden_two_grad, "dp", scatter_dimension=0, tiled=True)
    mlp_grad = contract(hidden_two, both_grad, 1, 1).astype(LOW)
    down_grad = contract(inner, upstream, 1, 0).astype(LOW)
    mlp_sent = plane_send(mlp_grad)
    down_sent = plane_send(down_grad)
    partial_out = contract(inner, down_mat, 0, 0).astype(LOW)
    hidden_two_own = hidden_two_own.astype(FULL)
    middle_own = lax.dynamic_slice_in_dim(middle, lane * rows, rows, 1).astype(FULL).T
    scale_own = lax.rsqrt(jnp.mean(middle_own * middle_own, axis=-1, keepdims=True) + EPSILON)
    middle_norm_grad, gain_two_grad = norm_back(
        hidden_two_own, middle_own * scale_own, scale_own, gain_two
    )
    middle_grad = middle_norm_grad + cotangent[0].astype(FULL)
    middle_grad_low = middle_grad.astype(LOW)
    branch_grad = lax.all_gather(middle_grad_low, "dp", axis=0, tiled=True)

    partial_out, branch_grad = lax.optimization_barrier((partial_out, branch_grad))
    result = lax.psum_scatter(partial_out, "dp", scatter_dimension=0, tiled=True)
    block_out = (middle_own + result.astype(FULL)).astype(LOW)[None]

    attended_grad = contract(out_rows, branch_grad, 1, 1)
    attended_grad_low = attended_grad.astype(LOW)
    grad_heads = attended_grad_low.reshape(own_heads, HEAD_DIM, seqs, rows)
    delta = jnp.sum(
        (attended * attended_grad_low.astype(FULL)).reshape(own_heads, HEAD_DIM, seqs, rows), axis=1
    )
    delta = jnp.transpose(delta, (1, 0, 2))[:, :, None, :]
    grad_heads = jnp.transpose(grad_heads, (2, 0, 3, 1))
    scores = (
        jnp.einsum("shqd,skd->shkq", query_heads, key_all, preferred_element_type=FULL) * scale
    )
    probability = jnp.exp(jnp.where(visible, scores - log_total, MASKED))
    prob_grad = jnp.einsum("shqd,skd->shkq", grad_heads, value_all, preferred_element_type=FULL)
    score_grad = (probability * (prob_grad - delta)).astype(LOW)
    query_grad = (
        jnp.einsum("shkq,skd->hdsq", score_grad, key_all, preferred_element_type=FULL) * scale
    ).reshape(own_heads, HEAD_DIM, total_rows)
    key_grad = (
        jnp.einsum("shkq,shqd->dsk", score_grad, query_heads, preferred_element_type=FULL) * scale
    )
    value_grad = jnp.einsum(
        "shkq,shqd->dsk", probability.astype(LOW), grad_heads, preferred_element_type=FULL
    )

    kv_grad = jnp.concatenate([key_grad, value_grad], axis=0).astype(LOW)
    kv_grad = kv_grad.reshape(2 * HEAD_DIM, seqs, planes, rows)
    kv_own = kv_grad[:, :, 0].astype(FULL)
    for k in range(1, planes):
        part = shift(kv_grad[:, :, k], planes - k)
        kv_own = kv_own + part.astype(FULL)
    kv_own = kv_own.reshape(2 * HEAD_DIM, total_rows)
    query_lin = rope(query_grad, cosine, -sine).astype(LOW).reshape(head_cols, total_rows)
    key_lin = rope(kv_own[:HEAD_DIM], cosine, -sine).astype(LOW)
    qkv_lin = jnp.concatenate([query_lin, key_lin, kv_own[HEAD_DIM:].astype(LOW)], axis=0)
    hidden_one_part = contract(qkv_lin, qkv_mat, 0, 1)
    hidden_one_low = hidden_one_part.astype(LOW)
    hidden_one_grad = lax.psum_scatter(
        hidden_one_low, "dp", scatter_dimension=0, tiled=True
    ).astype(FULL)
    gain_one_grad = jnp.sum(hidden_one_low.astype(FULL) * (wide * scale_one), axis=0)
    own_tokens = tokens[0].astype(FULL)
    own_scale = lax.rsqrt(jnp.mean(own_tokens * own_tokens, axis=-1, keepdims=True) + EPSILON)
    input_norm_grad, _ = norm_back(
        hidden_one_grad, own_tokens * own_scale, own_scale, gain_one
    )
    tokens_grad = (middle_grad + input_norm_grad)[None]

    branch_cols = lax.dynamic_slice_in_dim(branch_grad, lane * out_cols, out_cols, 1)
    qkv_grad = contract(hidden_one, qkv_lin, 0, 1).astype(LOW)
    out_grad = contract(attended_all, branch_cols, 1, 0).astype(LOW)
    attn_grad = jnp.concatenate([qkv_grad, out_grad], axis=1).reshape(planes, own_width, -1)
    gain_grads = jnp.stack([gain_one_grad, gain_two_grad]).astype(LOW)
    gain_grads = jnp.transpose(gain_grads.reshape(2, planes, own_width), (1, 0, 2))
    gain_grads = jnp.pad(gain_grads, ((0, 0), (0, EXTRA - 2), (0, piece_cols - own_width)))
    attn_grad = jnp.concatenate([attn_grad, gain_grads], axis=1)
    attn_sent = plane_send(attn_grad.reshape(-1, piece_cols))

    mlp_all = lax.all_gather(plane_sum(mlp_sent), "dp", axis=0, tiled=False)
    down_all = lax.all_gather(plane_sum(down_sent), "dp", axis=0, tiled=True)
    attn_all = lax.all_gather(plane_sum(attn_sent), "dp", axis=0, tiled=False)

    gate_out, up_out = spread_mlp(mlp_all, planes, unit)
    query_out, key_out, value_out, out_out = spread_attn(
        attn_all, own_width, head_cols, out_cols, kv_heads
    )
    gain_own = jnp.sum(attn_all[:, own_width : own_width + 2, :own_width].astype(FULL), axis=0)
    return (
        block_out,
        tokens_grad,
        gain_own[0],
        query_out,
        key_out,
        value_out,
        out_out,
        gain_own[1],
        gate_out,
        up_out,
        down_all.astype(FULL),
    )


def solution(mesh):
    rows = P("shard", None)
    acts = P("dp", "shard", None)
    gain = P("shard")
    weights = (gain, rows, rows, rows, rows, gain, rows, rows, rows)

    return jax.shard_map(
        on_device,
        mesh=mesh,
        in_specs=(acts, P("dp", None)) + weights + (acts,),
        out_specs=(acts, acts) + weights,
        check_vma=False,
    )
```

profile of v0, /device:TPU:0, one launch (start us, length us, event | category | flops | bytes accessed | tf_op | source)
XLA Modules:
  0.0 1328.1 jit_solution(5816182491524188056)
XLA Ops:
  29.9 35.3 %collective-permute-done = bf16[544,640]{1,0:T(8,128)(2,1)} collective-permute-done((bf16[544,640]{1,0:T(8,128)(2,1)}, bf16[544,640]{1,0:T(8,128)(2,1)}, u32[]{:S(2)}, u32[]{:S(2)}) %collective-permute-start) | collective-permute-done | bytes 696352 | tf_op jit(solution)/shard_map/ppermute | solution.py:27
  65.9 13.1 collective-permute-done.1
  109.8 35.5 %collective-permute-done.4 = bf16[128,2048]{1,0:T(8,128)(2,1)S(1)} collective-permute-done((bf16[128,2048]{1,0:T(8,128)(2,1)S(1)}, bf16[128,2048]{1,0:T(8,128)(2,1)S(1)}, u32[]{:S(2)}, u32[]{:S(2)}) %collective-permute-start.4) | collective-permute-done | bytes 524320 | tf_op jit(solution)/shard_map/ppermute | solution.py:27
  154.1 15.1 %bitcast_reduce_fusion = (f32[8,4,256]{2,1,0:T(4,128)S(1)}, f32[8,1024,4,256]{3,1,2,0:T(8,128)}) fusion(pred[8,1024,256]{2,1,0:T(8,128)(4,1)S(1)} %broadcast_compare_fusion, bf16[4,32,8,256]{3,1,0,2:T(8,128)(2,1)} %bitcast.255, bf16[4,32,8,256]{3,1,0,2:T(8,128)(2,1)} %bitcast.253, bf16[8,1024,64,1]{1,2,0,3:T(8,128)(2,1)S(1)} %reshape.349), kind=kOutput, calls=%fused_computation.1 | convolution fusion | flops 1100996608 | bytes 37781504 | tf_op jit(solution)/shard_map/shqd,skd->shkq/dot_general | solution.py:262
  169.2 14.4 %fusion.2 = f32[8,4,256]{2,1,0:T(4,128)S(1)} fusion(f32[8,1024,4,256]{3,1,2,0:T(8,128)} %get-tuple-element.125, f32[8,4,256]{2,1,0:T(4,128)S(1)} %get-tuple-element.124, pred[8,1024,256]{2,1,0:T(8,128)(4,1)S(1)} %broadcast_compare_fusion), kind=kLoop, calls=%fused_computation.7 | loop fusion | flops 33546240 | bytes 35717120 | tf_op jit(solution)/shard_map/reduce_sum | solution.py:267
  183.6 15.8 %fusion.54 = f32[4,64,8,256]{3,1,0,2:T(8,128)} fusion(f32[8,1024,4,256]{3,1,2,0:T(8,128)} %get-tuple-element.125, f32[8,4,256]{2,1,0:T(4,128)S(1)} %fusion.2, f32[8,4,256]{2,1,0:T(4,128)S(1)} %get-tuple-element.124, pred[8,1024,256]{2,1,0:T(8,128)(4,1)S(1)} %broadcast_compare_fusion, bf16[8,1024,64,1]{1,2,0,3:T(8,128)(2,1)S(1)} %copy-done.21), kind=kOutput, calls=%fused_computation.87 | convolution fusion | flops 1115684864 | bytes 38862848 | tf_op jit(solution)/shard_map/shkq,skd->hdsq/dot_general | solution.py:270
  205.7 52.5 %all-gather.14.cloned.1.call-done = bf16[2048,2048]{1,0:T(8,128)(2,1)} async-done(((bf16[256,2048]{1,0:T(8,128)(2,1)}), bf16[2048,2048]{1,0:T(8,128)(2,1)}) %all-gather.14.cloned.1.call-update) | async-done | bytes 8388624 | tf_op jit(solution)/shard_map/all_gather | solution.py:274
  299.5 84.3 %collective-permute-done.10 = bf16[176,2048]{1,0:T(8,128)(2,1)S(1)} collective-permute-done((bf16[176,2048]{1,0:T(8,128)(2,1)}, bf16[176,2048]{1,0:T(8,128)(2,1)S(1)}, u32[]{:S(2)}, u32[]{:S(2)}) %collective-permute-start.10) | collective-permute-done | bytes 720928 | tf_op jit(solution)/shard_map/ppermute | solution.py:27
  384.7 27.2 %collective-permute-done.11 = bf16[176,2048]{1,0:T(8,128)(2,1)S(1)} collective-permute-done((bf16[176,2048]{1,0:T(8,128)(2,1)}, bf16[176,2048]{1,0:T(8,128)(2,1)S(1)}, u32[]{:S(2)}, u32[]{:S(2)}) %collective-permute-start.11) | collective-permute-done | bytes 720928 | tf_op jit(solution)/shard_map/ppermute | solution.py:27
  426.3 18.3 %fusion.33 = f32[1408,2048]{1,0:T(8,128)} fusion(bf16[2048,1408]{1,0:T(8,128)(2,1)} %constant_dynamic-update-slice_fusion.4, bf16[2048,2048]{1,0:T(8,128)(2,1)S(1)} %copy-done.1, f32[2048]{0:T(1024)S(1)} %bitcast.281, f32[2048]{0:T(1024)S(1)} %add_rsqrt_fusion), kind=kOutput, calls=%fused_computation.59 | convolution fusion | flops 11827937280 | bytes 25706496 | tf_op jit(solution)/shard_map/dot_general | solution.py:19
  444.7 15.1 %multiply_convert_fusion.2 = (bf16[704,2048]{1,0:T(8,128)(2,1)S(1)}, bf16[704,2048]{1,0:T(8,128)(2,1)S(1)}, bf16[704,2048]{1,0:T(8,128)(2,1)}) fusion(f32[1408,2048]{1,0:T(8,128)} %fusion.33, bf16[704,2048]{1,0:T(8,128)(2,1)} %constant_dynamic-update-slice_fusion, bf16[1,2048,2048]{2,1,0:T(8,128)(2,1)} %all-gather.24.cloned.1.call-done), kind=kOutput, calls=%fused_computation.37 | convolution fusion | flops 5927206912 | bytes 31457280 | tf_op jit(solution)/shard_map/dot_general | solution.py:19
  462.3 16.9 %convolution_convert_fusion.1 = bf16[2048,2048]{0,1:T(8,128)(2,1)} fusion(bf16[2048,1408]{1,0:T(8,128)(2,1)} %constant_dynamic-update-slice_fusion.4, bf16[704,2048]{1,0:T(8,128)(2,1)S(1)} %get-tuple-element.67, bf16[704,2048]{1,0:T(8,128)(2,1)S(1)} %get-tuple-element.66), kind=kOutput, calls=%fused_computation.30 | convolution fusion | flops 11826888704 | bytes 19922944 | tf_op jit(solution)/shard_map/dot_general | solution.py:19
  482.7 114.3 %reduce-scatter.4.cloned.1.call-done = bf16[256,2048]{0,1:T(8,128)(2,1)} async-done(((bf16[2048,2048]{0,1:T(8,128)(2,1)}), bf16[256,2048]{0,1:T(8,128)(2,1)}) %reduce-scatter.4.cloned.1.call-update) | async-done | bytes 1048592 | tf_op jit(solution)/shard_map/reduce_scatter | solution.py:293
  619.5 16.8 %collective-permute-done.24 = bf16[176,2048]{1,0:T(8,128)(2,1)} collective-permute-done((bf16[176,2048]{1,0:T(8,128)(2,1)}, bf16[176,2048]{1,0:T(8,128)(2,1)}, u32[]{:S(2)}, u32[]{:S(2)}) %collective-permute-start.24) | collective-permute-done | bytes 720928 | tf_op jit(solution)/shard_map/ppermute | solution.py:27
  636.3 13.5 %collective-permute-done.26 = bf16[176,2048]{1,0:T(8,128)(2,1)} collective-permute-done((bf16[176,2048]{1,0:T(8,128)(2,1)}, bf16[176,2048]{1,0:T(8,128)(2,1)}, u32[]{:S(2)}, u32[]{:S(2)}) %collective-permute-start.26) | collective-permute-done | bytes 720928 | tf_op jit(solution)/shard_map/ppermute | solution.py:27
  649.8 31.5 %collective-permute-done.25 = bf16[176,2048]{1,0:T(8,128)(2,1)} collective-permute-done((bf16[176,2048]{1,0:T(8,128)(2,1)S(1)}, bf16[176,2048]{1,0:T(8,128)(2,1)}, u32[]{:S(2)}, u32[]{:S(2)}) %collective-permute-start.25) | collective-permute-done | bytes 720928 | tf_op jit(solution)/shard_map/ppermute | solution.py:27
  684.5 17.6 %convolution_convert_fusion.2 = bf16[2048,1408]{1,0:T(8,128)(2,1)S(1)} fusion(bf16[704,2048]{1,0:T(8,128)(2,1)} %copy-done.40, bf16[704,2048]{1,0:T(8,128)(2,1)} %copy-done.39, bf16[2048,2048]{1,0:T(8,128)(2,1)} %all-gather.16.cloned.1.call-done, f32[2048]{0:T(1024)S(1)} %bitcast.284, f32[2048]{0:T(1024)S(1)} %add_rsqrt_fusion), kind=kOutput, calls=%fused_computation.31 | convolution fusion | flops 11842355200 | bytes 19939328 | tf_op jit(solution)/shard_map/dot_general | solution.py:19
  709.7 32.8 %collective-permute-done.21 = bf16[512,1408]{1,0:T(8,128)(2,1)} collective-permute-done((bf16[512,1408]{1,0:T(8,128)(2,1)}, bf16[512,1408]{1,0:T(8,128)(2,1)}, u32[]{:S(2)}, u32[]{:S(2)}) %collective-permute-start.21) | collective-permute-done | bytes 1441824 | tf_op jit(solution)/shard_map/ppermute | solution.py:27
  742.5 30.7 %collective-permute-done.23 = bf16[512,1408]{1,0:T(8,128)(2,1)} collective-permute-done((bf16[512,1408]{1,0:T(8,128)(2,1)}, bf16[512,1408]{1,0:T(8,128)(2,1)}, u32[]{:S(2)}, u32[]{:S(2)}) %collective-permute-start.23) | collective-permute-done | bytes 1441824 | tf_op jit(solution)/shard_map/ppermute | solution.py:27
  773.2 58.4 %collective-permute-done.22 = bf16[512,1408]{1,0:T(8,128)(2,1)} collective-permute-done((bf16[512,1408]{1,0:T(8,128)(2,1)}, bf16[512,1408]{1,0:T(8,128)(2,1)}, u32[]{:S(2)}, u32[]{:S(2)}) %collective-permute-start.22) | collective-permute-done | bytes 1441824 | tf_op jit(solution)/shard_map/ppermute | solution.py:27
  864.5 22.5 %collective-permute-done.13 = bf16[256,2048]{1,0:T(8,128)(2,1)} collective-permute-done((bf16[256,2048]{1,0:T(8,128)(2,1)S(1)}, bf16[256,2048]{1,0:T(8,128)(2,1)}, u32[]{:S(2)}, u32[]{:S(2)}) %collective-permute-start.13) | collective-permute-done | bytes 1048608 | tf_op jit(solution)/shard_map/ppermute | solution.py:232
  887.0 20.7 %collective-permute-done.12 = bf16[256,2048]{1,0:T(8,128)(2,1)} collective-permute-done((bf16[256,2048]{1,0:T(8,128)(2,1)S(1)}, bf16[256,2048]{1,0:T(8,128)(2,1)}, u32[]{:S(2)}, u32[]{:S(2)}) %collective-permute-start.12) | collective-permute-done | bytes 1048608 | tf_op jit(solution)/shard_map/ppermute | solution.py:232
  917.1 19.8 %fusion.12 = bf16[8,4,1024,256]{3,2,1,0:T(8,128)(2,1)} fusion(f32[8,1024,4,256]{3,1,2,0:T(8,128)} %get-tuple-element.125, f32[8,4,256]{2,1,0:T(4,128)S(1)} %copy.72, f32[8,4,256]{2,1,0:T(4,128)S(1)} %bitcast.294, pred[8,1024,256]{2,1,0:T(8,128)(4,1)S(1)} %broadcast_compare_fusion, bf16[8,1024,64,1]{1,2,0,3:T(8,128)(2,1)S(1)} %copy-done.22, ...), kind=kOutput, calls=%fused_computation.21 | convolution fusion | flops 1124073472 | bytes 54591488 | tf_op jit(solution)/shard_map/shqd,skd->shkq/dot_general | solution.py:325
  960.1 16.1 %fusion.59 = bf16[64,8,1024]{2,0,1:T(8,128)(2,1)} fusion(f32[8,1024,4,256]{3,1,2,0:T(8,128)} %get-tuple-element.125, f32[8,4,256]{2,1,0:T(4,128)S(1)} %bitcast.295, pred[8,1024,256]{2,1,0:T(8,128)(4,1)S(1)} %broadcast_compare_fusion, bf16[4,64,8,256]{3,2,1,0:T(8,128)(2,1)} %bitcast.268), kind=kOutput, calls=%fused_computation.97 | convolution fusion | flops 1107820544 | bytes 37781504 | tf_op jit(solution)/shard_map/shkq,shqd->dsk/dot_general | solution.py:333
  1003.7 23.6 %collective-permute-done.16 = bf16[128,8,256]{2,1,0:T(8,128)(2,1)S(1)} collective-permute-done((bf16[128,8,256]{2,1,0:T(8,128)(2,1)S(1)}, bf16[128,8,256]{2,1,0:T(8,128)(2,1)S(1)}, u32[]{:S(2)}, u32[]{:S(2)}) %collective-permute-start.16) | collective-permute-done | bytes 524320 | tf_op jit(solution)/shard_map/ppermute | solution.py:27
  1063.8 16.2 %collective-permute-done.18 = bf16[544,640]{1,0:T(8,128)(2,1)S(1)} collective-permute-done((bf16[544,640]{1,0:T(8,128)(2,1)S(1)}, bf16[544,640]{1,0:T(8,128)(2,1)S(1)}, u32[]{:S(2)}, u32[]{:S(2)}) %collective-permute-start.18) | collective-permute-done | bytes 696352 | tf_op jit(solution)/shard_map/ppermute | solution.py:27
  1080.0 14.6 %collective-permute-done.20 = bf16[544,640]{1,0:T(8,128)(2,1)S(1)} collective-permute-done((bf16[544,640]{1,0:T(8,128)(2,1)S(1)}, bf16[544,640]{1,0:T(8,128)(2,1)S(1)}, u32[]{:S(2)}, u32[]{:S(2)}) %collective-permute-start.20) | collective-permute-done | bytes 696352 | tf_op jit(solution)/shard_map/ppermute | solution.py:27
  1094.6 27.0 %collective-permute-done.19 = bf16[544,640]{1,0:T(8,128)(2,1)} collective-permute-done((bf16[544,640]{1,0:T(8,128)(2,1)S(1)}, bf16[544,640]{1,0:T(8,128)(2,1)}, u32[]{:S(2)}, u32[]{:S(2)}) %collective-permute-start.19) | collective-permute-done | bytes 696352 | tf_op jit(solution)/shard_map/ppermute | solution.py:27
  1135.4 13.8 %shard_map.204 = (f32[512,5632]{1,0:T(8,128)}, f32[512,5632]{1,0:T(8,128)}) custom-call(bf16[8,512,1408]{2,1,0:T(8,128)(2,1)} %bitcast.240), custom_call_target="tpu_custom_call" | custom-call | bytes 34603008 | tf_op jit(solution)/shard_map/pallas_call | solution.py:96
  1149.2 14.1 %all-gather.26.cloned.1.call-done = bf16[4352,640]{1,0:T(8,128)(2,1)} async-done(((bf16[544,640]{1,0:T(8,128)(2,1)}), bf16[4352,640]{1,0:T(8,128)(2,1)}) %all-gather.26.cloned.1.call-update) | async-done | bytes 5570576 | tf_op jit(solution)/shard_map/all_gather | solution.py:372
  1176.3 61.7 %reduce-scatter.8.cloned.1.call-done = bf16[256,2048]{0,1:T(8,128)(2,1)} async-done(((bf16[2048,2048]{0,1:T(8,128)(2,1)}), bf16[256,2048]{0,1:T(8,128)(2,1)}) %reduce-scatter.8.cloned.1.call-update) | async-done | bytes 1048592 | tf_op jit(solution)/shard_map/reduce_scatter | solution.py:349
  1239.7 73.1 %reduce-scatter.6.cloned.1.call-done = bf16[256,2048]{0,1:T(8,128)(2,1)} async-done(((bf16[2048,2048]{0,1:T(8,128)(2,1)}), bf16[256,2048]{0,1:T(8,128)(2,1)}) %reduce-scatter.6.cloned.1.call-update) | async-done | bytes 1048592 | tf_op jit(solution)/shard_map/reduce_scatter | solution.py:310
  (280 shorter events, 330.4 us)
Async XLA Ops:
  7.2 76.9 %all-gather.22.cloned.1.call-start = ((), (), s32[]{:S(2)}) async-start(), calls=%async_computation.10 | async-start | bytes 9437184 | tf_op jit(solution)/shard_map/all_gather | solution.py:180
  9.5 248.7 %all-gather.14.cloned.1.call-start = ((), (), s32[]{:S(2)}) async-start(), calls=%async_computation.3 | async-start | bytes 9437184 | tf_op jit(solution)/shard_map/all_gather | solution.py:274
  14.1 65.7 %collective-permute-start.2 = (bf16[544,640]{1,0:T(8,128)(2,1)}, bf16[544,640]{1,0:T(8,128)(2,1)}, u32[]{:S(2)}, u32[]{:S(2)}) collective-permute-start(bf16[544,640]{1,0:T(8,128)(2,1)} %fusion.81), channel_id=1, source_target_pairs={{0,3},{1,0},{2,1},{3,2},{4,7},{5,4},{6,5},{7,6},{8,11},{9,8},{10,9... | collective-permute-start | bytes 2088968 | tf_op jit(solution)/shard_map/ppermute | solution.py:27
  19.2 59.9 %collective-permute-start.1 = (bf16[544,640]{1,0:T(8,128)(2,1)}, bf16[544,640]{1,0:T(8,128)(2,1)}, u32[]{:S(2)}, u32[]{:S(2)}) collective-permute-start(bf16[544,640]{1,0:T(8,128)(2,1)} %fusion.81), channel_id=1, source_target_pairs={{0,2},{1,3},{2,0},{3,1},{4,6},{5,7},{6,4},{7,5},{8,10},{9,11},{10,... | collective-permute-start | bytes 2088968 | tf_op jit(solution)/shard_map/ppermute | solution.py:27
  19.2 46.1 %collective-permute-start = (bf16[544,640]{1,0:T(8,128)(2,1)}, bf16[544,640]{1,0:T(8,128)(2,1)}, u32[]{:S(2)}, u32[]{:S(2)}) collective-permute-start(bf16[544,640]{1,0:T(8,128)(2,1)} %fusion.81), channel_id=1, source_target_pairs={{0,1},{1,2},{2,3},{3,0},{4,5},{5,6},{6,7},{7,4},{8,9},{9,10},{10,1... | collective-permute-start | bytes 2088968 | tf_op jit(solution)/shard_map/ppermute | solution.py:27
  96.7 48.6 %collective-permute-start.4 = (bf16[128,2048]{1,0:T(8,128)(2,1)S(1)}, bf16[128,2048]{1,0:T(8,128)(2,1)S(1)}, u32[]{:S(2)}, u32[]{:S(2)}) collective-permute-start(bf16[128,2048]{1,0:T(8,128)(2,1)S(1)} %pad_maximum_fusion.6), channel_id=1, source_target_pairs={{0,2},{1,3},{2,0},{3,1},{4,6},{5,7},{6,4},{7,5},{8,10},{9,11},{10,... | collective-permute-start | bytes 1572872 | tf_op jit(solution)/shard_map/ppermute | solution.py:27
  100.3 45.1 %collective-permute-start.3 = (bf16[128,2048]{1,0:T(8,128)(2,1)S(1)}, bf16[128,2048]{1,0:T(8,128)(2,1)S(1)}, u32[]{:S(2)}, u32[]{:S(2)}) collective-permute-start(bf16[128,2048]{1,0:T(8,128)(2,1)S(1)} %pad_maximum_fusion.6), channel_id=1, source_target_pairs={{0,1},{1,2},{2,3},{3,0},{4,5},{5,6},{6,7},{7,4},{8,9},{9,10},{10,1... | collective-permute-start | bytes 1572872 | tf_op jit(solution)/shard_map/ppermute | solution.py:27
  205.6 215.0 %all-gather.16.cloned.1.call-start = ((), (), s32[]{:S(2)}) async-start(), calls=%async_computation.4 | async-start | bytes 9437184 | tf_op jit(solution)/shard_map/all_gather | solution.py:278
  265.5 179.2 %all-gather.24.cloned.1.call-start = ((), (), s32[]{:S(2)}) async-start(), calls=%async_computation.11 | async-start | bytes 9437184 | tf_op jit(solution)/shard_map/all_gather | solution.py:181
  266.0 330.9 %reduce-scatter.4.cloned.1.call-start = ((), (), s32[]{:S(2)}) async-start(), calls=%async_computation.5 | async-start | bytes 9437184 | tf_op jit(solution)/shard_map/reduce_scatter | solution.py:293
  281.2 131.7 %collective-permute-start.6 = (bf16[512,1408]{1,0:T(8,128)(2,1)}, bf16[512,1408]{1,0:T(8,128)(2,1)}, u32[]{:S(2)}, u32[]{:S(2)}) collective-permute-start(bf16[512,1408]{1,0:T(8,128)(2,1)} %concatenate.65), channel_id=1, source_target_pairs={{0,1},{1,2},{2,3},{3,0},{4,5},{5,6},{6,7},{7,4},{8,9},{9,10},{10,1... | collective-permute-start | bytes 4325384 | tf_op jit(solution)/shard_map/ppermute | solution.py:27
  282.6 101.3 %collective-permute-start.10 = (bf16[176,2048]{1,0:T(8,128)(2,1)}, bf16[176,2048]{1,0:T(8,128)(2,1)S(1)}, u32[]{:S(2)}, u32[]{:S(2)}) collective-permute-start(bf16[176,2048]{1,0:T(8,128)(2,1)} %get-tuple-element.63), channel_id=1, source_target_pairs={{0,2},{1,3},{2,0},{3,1},{4,6},{5,7},{6,4},{7,5},{8,10},{9,11},{10,... | collective-permute-start | bytes 2162696 | tf_op jit(solution)/shard_map/ppermute | solution.py:27
  284.0 131.4 %collective-permute-start.7 = (bf16[512,1408]{1,0:T(8,128)(2,1)}, bf16[512,1408]{1,0:T(8,128)(2,1)}, u32[]{:S(2)}, u32[]{:S(2)}) collective-permute-start(bf16[512,1408]{1,0:T(8,128)(2,1)} %concatenate.65), channel_id=1, source_target_pairs={{0,2},{1,3},{2,0},{3,1},{4,6},{5,7},{6,4},{7,5},{8,10},{9,11},{10,... | collective-permute-start | bytes 4325384 | tf_op jit(solution)/shard_map/ppermute | solution.py:27
  285.5 132.5 %collective-permute-start.8 = (bf16[512,1408]{1,0:T(8,128)(2,1)}, bf16[512,1408]{1,0:T(8,128)(2,1)}, u32[]{:S(2)}, u32[]{:S(2)}) collective-permute-start(bf16[512,1408]{1,0:T(8,128)(2,1)} %concatenate.65), channel_id=1, source_target_pairs={{0,3},{1,0},{2,1},{3,2},{4,7},{5,4},{6,5},{7,6},{8,11},{9,8},{10,9... | collective-permute-start | bytes 4325384 | tf_op jit(solution)/shard_map/ppermute | solution.py:27
  292.0 119.9 %collective-permute-start.11 = (bf16[176,2048]{1,0:T(8,128)(2,1)}, bf16[176,2048]{1,0:T(8,128)(2,1)S(1)}, u32[]{:S(2)}, u32[]{:S(2)}) collective-permute-start(bf16[176,2048]{1,0:T(8,128)(2,1)} %get-tuple-element.63), channel_id=1, source_target_pairs={{0,3},{1,0},{2,1},{3,2},{4,7},{5,4},{6,5},{7,6},{8,11},{9,8},{10,9... | collective-permute-start | bytes 2162696 | tf_op jit(solution)/shard_map/ppermute | solution.py:27
  479.2 378.9 %all-gather.18.cloned.1.call-start = ((), (), s32[]{:S(2)}) async-start(), calls=%async_computation.6 | async-start | bytes 9437184 | tf_op jit(solution)/shard_map/all_gather | solution.py:307
  602.7 523.6 %all-gather.20.cloned.1.call-start = ((), (), s32[]{:S(2)}) async-start(), calls=%async_computation.9 | async-start | bytes 6488064 | tf_op jit(solution)/shard_map/all_gather | solution.py:371
  616.6 33.2 %collective-permute-start.26 = (bf16[176,2048]{1,0:T(8,128)(2,1)}, bf16[176,2048]{1,0:T(8,128)(2,1)}, u32[]{:S(2)}, u32[]{:S(2)}) collective-permute-start(bf16[176,2048]{1,0:T(8,128)(2,1)} %get-tuple-element.85), channel_id=1, source_target_pairs={{0,3},{1,0},{2,1},{3,2},{4,7},{5,4},{6,5},{7,6},{8,11},{9,8},{10,9... | collective-permute-start | bytes 2162696 | tf_op jit(solution)/shard_map/ppermute | solution.py:27
  618.9 62.3 %collective-permute-start.25 = (bf16[176,2048]{1,0:T(8,128)(2,1)S(1)}, bf16[176,2048]{1,0:T(8,128)(2,1)}, u32[]{:S(2)}, u32[]{:S(2)}) collective-permute-start(bf16[176,2048]{1,0:T(8,128)(2,1)S(1)} %get-tuple-element.86), channel_id=1, source_target_pairs={{0,2},{1,3},{2,0},{3,1},{4,6},{5,7},{6,4},{7,5},{8,10},{9,11},{10,... | collective-permute-start | bytes 2162696 | tf_op jit(solution)/shard_map/ppermute | solution.py:27
  684.4 451.0 %all-gather.28.cloned.1.call-start = ((), (), s32[]{:S(2)}) async-start(), calls=%async_computation.13 | async-start | bytes 12976128 | tf_op jit(solution)/shard_map/all_gather | solution.py:370
  705.9 36.6 %collective-permute-start.21 = (bf16[512,1408]{1,0:T(8,128)(2,1)}, bf16[512,1408]{1,0:T(8,128)(2,1)}, u32[]{:S(2)}, u32[]{:S(2)}) collective-permute-start(bf16[512,1408]{1,0:T(8,128)(2,1)} %get-tuple-element.79), channel_id=1, source_target_pairs={{0,1},{1,2},{2,3},{3,0},{4,5},{5,6},{6,7},{7,4},{8,9},{9,10},{10,1... | collective-permute-start | bytes 4325384 | tf_op jit(solution)/shard_map/ppermute | solution.py:27
  705.9 67.3 %collective-permute-start.23 = (bf16[512,1408]{1,0:T(8,128)(2,1)}, bf16[512,1408]{1,0:T(8,128)(2,1)}, u32[]{:S(2)}, u32[]{:S(2)}) collective-permute-start(bf16[512,1408]{1,0:T(8,128)(2,1)} %get-tuple-element.80), channel_id=1, source_target_pairs={{0,3},{1,0},{2,1},{3,2},{4,7},{5,4},{6,5},{7,6},{8,11},{9,8},{10,9... | collective-permute-start | bytes 4325384 | tf_op jit(solution)/shard_map/ppermute | solution.py:27
  709.7 121.9 %collective-permute-start.22 = (bf16[512,1408]{1,0:T(8,128)(2,1)}, bf16[512,1408]{1,0:T(8,128)(2,1)}, u32[]{:S(2)}, u32[]{:S(2)}) collective-permute-start(bf16[512,1408]{1,0:T(8,128)(2,1)} %get-tuple-element.81), channel_id=1, source_target_pairs={{0,2},{1,3},{2,0},{3,1},{4,6},{5,7},{6,4},{7,5},{8,10},{9,11},{10,... | collective-permute-start | bytes 4325384 | tf_op jit(solution)/shard_map/ppermute | solution.py:27
  836.1 327.3 %all-gather.26.cloned.1.call-start = ((), (), s32[]{:S(2)}) async-start(), calls=%async_computation.12 | async-start | bytes 6266880 | tf_op jit(solution)/shard_map/all_gather | solution.py:372
  837.9 26.6 %collective-permute-start.14 = (bf16[256,2048]{1,0:T(8,128)(2,1)S(1)}, bf16[256,2048]{1,0:T(8,128)(2,1)}, u32[]{:S(2)}, u32[]{:S(2)}) collective-permute-start(bf16[256,2048]{1,0:T(8,128)(2,1)S(1)} %dynamic-slice_convert_fusion), channel_id=1, source_target_pairs={{0,3},{4,7},{9,8},{13,12},{18,17},{22,21},{27,26},{31,30}} | collective-permute-start | bytes 3145736 | tf_op jit(solution)/shard_map/ppermute | solution.py:232
  842.0 45.0 %collective-permute-start.13 = (bf16[256,2048]{1,0:T(8,128)(2,1)S(1)}, bf16[256,2048]{1,0:T(8,128)(2,1)}, u32[]{:S(2)}, u32[]{:S(2)}) collective-permute-start(bf16[256,2048]{1,0:T(8,128)(2,1)S(1)} %dynamic-slice_convert_fusion), channel_id=1, source_target_pairs={{0,2},{4,6},{9,11},{13,15},{18,16},{22,20},{27,25},{31,29}} | collective-permute-start | bytes 3145736 | tf_op jit(solution)/shard_map/ppermute | solution.py:232
  844.2 63.4 %collective-permute-start.12 = (bf16[256,2048]{1,0:T(8,128)(2,1)S(1)}, bf16[256,2048]{1,0:T(8,128)(2,1)}, u32[]{:S(2)}, u32[]{:S(2)}) collective-permute-start(bf16[256,2048]{1,0:T(8,128)(2,1)S(1)} %dynamic-slice_convert_fusion), channel_id=1, source_target_pairs={{0,1},{4,5},{9,10},{13,14},{18,19},{22,23},{27,24},{31,28}} | collective-permute-start | bytes 3145736 | tf_op jit(solution)/shard_map/ppermute | solution.py:232
  982.3 45.0 %collective-permute-start.16 = (bf16[128,8,256]{2,1,0:T(8,128)(2,1)S(1)}, bf16[128,8,256]{2,1,0:T(8,128)(2,1)S(1)}, u32[]{:S(2)}, u32[]{:S(2)}) collective-permute-start(bf16[128,8,256]{2,1,0:T(8,128)(2,1)S(1)} %get-tuple-element.96), channel_id=1, source_target_pairs={{0,2},{1,3},{2,0},{3,1},{4,6},{5,7},{6,4},{7,5},{8,10},{9,11},{10,... | collective-permute-start | bytes 1572872 | tf_op jit(solution)/shard_map/ppermute | solution.py:27
  1059.8 34.9 %collective-permute-start.20 = (bf16[544,640]{1,0:T(8,128)(2,1)S(1)}, bf16[544,640]{1,0:T(8,128)(2,1)S(1)}, u32[]{:S(2)}, u32[]{:S(2)}) collective-permute-start(bf16[544,640]{1,0:T(8,128)(2,1)S(1)} %get-tuple-element.88), channel_id=1, source_target_pairs={{0,3},{1,0},{2,1},{3,2},{4,7},{5,4},{6,5},{7,6},{8,11},{9,8},{10,9... | collective-permute-start | bytes 2088968 | tf_op jit(solution)/shard_map/ppermute | solution.py:27
  1063.8 57.8 %collective-permute-start.19 = (bf16[544,640]{1,0:T(8,128)(2,1)S(1)}, bf16[544,640]{1,0:T(8,128)(2,1)}, u32[]{:S(2)}, u32[]{:S(2)}) collective-permute-start(bf16[544,640]{1,0:T(8,128)(2,1)S(1)} %get-tuple-element.89), channel_id=1, source_target_pairs={{0,2},{1,3},{2,0},{3,1},{4,6},{5,7},{6,4},{7,5},{8,10},{9,11},{10,... | collective-permute-start | bytes 2088968 | tf_op jit(solution)/shard_map/ppermute | solution.py:27
  1124.2 113.9 %reduce-scatter.8.cloned.1.call-start = ((), (), s32[]{:S(2)}) async-start(), calls=%async_computation.8 | async-start | bytes 9437184 | tf_op jit(solution)/shard_map/reduce_scatter | solution.py:349
  1124.8 188.1 %reduce-scatter.6.cloned.1.call-start = ((), (), s32[]{:S(2)}) async-start(), calls=%async_computation.7 | async-start | bytes 9437184 | tf_op jit(solution)/shard_map/reduce_scatter | solution.py:310
  (49 other events, 1544.0 us)
Sparse Core Ops, SparseCore 0:
  10.5 58.5 all-gather.21
  205.7 52.4 all-gather.13
  265.6 54.2 all-gather.15
  321.6 54.2 all-gather.23
  479.4 117.5 reduce-scatter.3
  602.8 55.8 all-gather.17
  684.6 41.3 all-gather.19
  836.2 65.3 all-gather.27
  1124.3 39.0 all-gather.25
  1166.7 71.2 reduce-scatter.7
  1241.5 71.2 reduce-scatter.5
where the time goes:
time: 1340 us; the launch traced here: 1330 us
  waiting for transfers between devices  847 us (63%)
  matrix products  216 us (16%)
  local copies, waits for them, and re-layouts  96.1 us (7%)
  other arithmetic  72.6 us (5%)
  starting transfers between devices  47.2 us (4%)
  Pallas kernels  25.2 us (2%)
  between operations  15.4 us (1%)
    ppermute x24, waiting for transfers between devices, shift(): return lax.ppermute(value, 'shard', pairs)  480 us
    dot_general x12, matrix products, contract(): lax.dot_general(left, right, (((left_dim,), (right_dim,)), ((), ())), pre...  129 us
    reduce_scatter x1, waiting for transfers between devices, on_device(): lax.psum_scatter(hidden_two_grad, 'dp', scatter_dimension=0, tiled=True)  114 us
    reduce_scatter x1, waiting for transfers between devices, on_device(): lax.psum_scatter(partial_out, 'dp', scatter_dimension=0, tiled=True)  73.1 us
    reduce_scatter x1, waiting for transfers between devices, on_device(): lax.psum_scatter(hidden_one_low, 'dp', scatter_dimension=0, tiled=True)  61.7 us
    all_gather x1, waiting for transfers between devices, on_device(): lax.all_gather(attended.astype(LOW), 'dp', axis=0, tiled=True)  52.5 us
    ppermute x3, waiting for transfers between devices, on_device(): out_rows = out_rows + lax.ppermute(row_piece, ('dp', 'shard'), pairs)  49.5 us
    ppermute x24, starting transfers between devices, shift(): return lax.ppermute(value, 'shard', pairs)  38.1 us
  transfers between devices with their start and end apart: 38, of which 26 were waited for; matrix products, arithmetic and copies ran while one was open for 19% of the time, Pallas kernels for 2%

commit v1 on v0

v1 whole, which is shorter than its diff:
```python
import functools

import jax
import jax.numpy as jnp
from jax import lax
from jax.experimental import pallas as pl
from jax.experimental.pallas import tpu as pltpu
from jax.sharding import PartitionSpec as P

HEAD_DIM = 64
EPSILON = 1e-05
ROPE_BASE = 10000.0
MASKED = -1e30
LOW = jnp.bfloat16
FULL = jnp.float32
EXTRA = 32


def contract(left, right, left_dim, right_dim):
    return lax.dot_general(
        left, right, (((left_dim,), (right_dim,)), ((), ())), preferred_element_type=FULL
    )


def shift(value, amount):
    count = lax.axis_size("shard")
    pairs = [(i, (i + amount) % count) for i in range(count)]
    return lax.ppermute(value, "shard", pairs)


def swap_cores(value):
    lanes = lax.axis_size("dp")
    return lax.ppermute(value, "dp", [(d, d ^ 1) for d in range(lanes)])


def swap_chips(value, mask):
    lanes = lax.axis_size("dp")
    return lax.ppermute(value, "dp", [(d, d ^ (2 * mask)) for d in range(lanes)])


def plane_parts(value):
    count = lax.axis_size("shard")
    return [value] + [shift(value, k) for k in range(1, count)]


def assemble(parts, axis=0):
    count = lax.axis_size("shard")
    rank = lax.axis_index("shard")
    rows = parts[0].shape[axis]
    shape = list(parts[0].shape)
    shape[axis] = rows * count
    whole = jnp.zeros(shape, parts[0].dtype)
    for k, part in enumerate(parts):
        place = lax.rem(rank - k + count, count)
        whole = lax.dynamic_update_slice_in_dim(whole, part, place * rows, axis)
    return whole


def plane_send(value):
    count = lax.axis_size("shard")
    rank = lax.axis_index("shard")
    rows = value.shape[0] // count
    parts = []
    for k in range(count):
        target = lax.rem(rank + k, count)
        piece = lax.dynamic_slice_in_dim(value, target * rows, rows, 0)
        parts.append(shift(piece, k) if k else piece)
    return parts


def plane_sum(parts):
    total = parts[0].astype(FULL)
    for part in parts[1:]:
        total = total + part.astype(FULL)
    return total.astype(LOW)


def chip_stack(value):
    chips = lax.axis_size("dp") // 2
    return [value] + [swap_chips(value, k) for k in range(1, chips)]


def rope(values, cosine, sine):
    half = values.shape[-2] // 2
    front, back = values[..., :half, :], values[..., half:, :]
    return jnp.concatenate([front * cosine - back * sine, back * cosine + front * sine], axis=-2)


def norm_back(upstream, normed, row_scale, gain):
    scaled = upstream * gain
    mean = jnp.mean(scaled * normed, axis=-1, keepdims=True)
    return row_scale * (scaled - normed * mean)


class Tiles:
    def __init__(self, info_ref, planes, span, heads):
        self.info, self.planes, self.span, self.heads = info_ref, planes, span, heads
        self.seq = pl.program_id(0)

    def offset(self, part, high):
        first = self.info[self.seq, part]
        return pl.multiple_of(jnp.where(first == high, 0, 1) * self.span, self.span)

    def before(self, part):
        return self.info[self.seq, self.planes + part] == 1

    def picked(self, part, own):
        return jnp.where(self.before(part), self.offset(own, 0), self.offset(own, 1))

    def heads_of(self, ref, offset):
        offset = pl.multiple_of(offset, self.span)
        rows = [
            ref[h * HEAD_DIM : (h + 1) * HEAD_DIM, pl.ds(offset, self.span)]
            for h in range(self.heads)
        ]
        return jnp.concatenate(rows, axis=1)

    def put_heads(self, ref, offset, value):
        for h in range(self.heads):
            piece = value[:, h * self.span : (h + 1) * self.span]
            ref[h * HEAD_DIM : (h + 1) * HEAD_DIM, pl.ds(offset, self.span)] = piece.astype(
                ref.dtype
            )

    def block(self, ref, part, offset):
        return ref[part, :, pl.ds(pl.multiple_of(offset, self.span), self.span)]

    def diagonal(self):
        shape = (self.span, self.heads * self.span)
        keys = lax.broadcasted_iota(jnp.int32, shape, 0)
        queries = lax.broadcasted_iota(jnp.int32, shape, 1)
        return keys <= lax.rem(queries, self.span)


def top_of(value):
    return jnp.max(value, axis=0, keepdims=True)


def sum_of(value):
    return jnp.sum(value, axis=0, keepdims=True)


def attn_fwd_kernel(planes, span, heads, info_ref, q_ref, k_ref, v_ref, o_ref, lse_ref):
    tiles = Tiles(info_ref, planes, span, heads)
    low_at, high_at = tiles.offset(0, 0), tiles.offset(0, 1)
    q_low, q_high = tiles.heads_of(q_ref, low_at), tiles.heads_of(q_ref, high_at)
    visible = tiles.diagonal()

    def score(part, offset, query):
        return contract(tiles.block(k_ref, part, offset), query, 0, 0)

    own_low = jnp.where(visible, score(0, low_at, q_low), MASKED)
    own_high = jnp.where(visible, score(0, high_at, q_high), MASKED)
    wide = [score(p, tiles.offset(p, 0), q_high) for p in range(planes)]
    mixed = []
    for p in range(1, planes):
        query = tiles.heads_of(q_ref, tiles.picked(p, 0))
        mixed.append(score(p, tiles.picked(p, p), query))
    top_low, top_high = top_of(own_low), top_of(own_high)
    for value in wide:
        top_high = jnp.maximum(top_high, top_of(value))
    for p in range(1, planes):
        peak = top_of(mixed[p - 1])
        top_low = jnp.maximum(top_low, jnp.where(tiles.before(p), peak, MASKED))
        top_high = jnp.maximum(top_high, jnp.where(tiles.before(p), MASKED, peak))

    def add(part, offset, value, top):
        weight = jnp.exp(value - top)
        block = tiles.block(v_ref, part, offset)
        return sum_of(weight), contract(block, weight.astype(LOW), 1, 0)

    total_low, out_low = add(0, low_at, own_low, top_low)
    total_high, out_high = add(0, high_at, own_high, top_high)
    for p in range(planes):
        total, out = add(p, tiles.offset(p, 0), wide[p], top_high)
        total_high, out_high = total_high + total, out_high + out
    for p in range(1, planes):
        early = tiles.before(p)
        top = jnp.where(early, top_low, top_high)
        total, out = add(p, tiles.picked(p, p), mixed[p - 1], top)
        total_low = total_low + jnp.where(early, total, 0.0)
        total_high = total_high + jnp.where(early, 0.0, total)
        out_low = out_low + jnp.where(early, out, 0.0)
        out_high = out_high + jnp.where(early, 0.0, out)
    tiles.put_heads(o_ref, low_at, out_low / total_low)
    tiles.put_heads(o_ref, high_at, out_high / total_high)
    lse_ref[0, 0:1, :] = top_low + jnp.log(total_low)
    lse_ref[0, 1:2, :] = top_high + jnp.log(total_high)


def attn_bwd_kernel(
    planes, span, heads, info_ref, q_ref, k_ref, v_ref, o_ref, lse_ref, g_ref, dq_ref, dk_ref, dv_ref
):
    tiles = Tiles(info_ref, planes, span, heads)
    low_at, high_at = tiles.offset(0, 0), tiles.offset(0, 1)
    visible = tiles.diagonal()

    def state(offset, row):
        query, grad = tiles.heads_of(q_ref, offset), tiles.heads_of(g_ref, offset)
        out = tiles.heads_of(o_ref, offset)
        delta = sum_of(out.astype(FULL) * grad.astype(FULL))
        return query, grad, lse_ref[0, row : row + 1, :], delta

    low, high = state(low_at, 0), state(high_at, 1)

    def tile(part, offset, queries, masked=False):
        query, grad, log_total, delta = queries
        key, value = tiles.block(k_ref, part, offset), tiles.block(v_ref, part, offset)
        scores = contract(key, query, 0, 0)
        if masked:
            scores = jnp.where(visible, scores, MASKED)
        weight = jnp.exp(scores - log_total)
        change = contract(value, grad, 0, 0)
        change = (weight * (change - delta)).astype(LOW)
        dq = contract(key, change, 1, 0)
        dk = contract(query, change, 1, 1)
        dv = contract(grad, weight.astype(LOW), 1, 1)
        return dq, dk, dv

    dq_low, dk_low, dv_low = tile(0, low_at, low, True)
    dq_high, dk_high, dv_high = tile(0, high_at, high, True)

    def put(part, offset, dk, dv):
        place = pl.ds(pl.multiple_of(offset, span), span)
        dk_ref[part, :, place] = dk.astype(dk_ref.dtype)
        dv_ref[part, :, place] = dv.astype(dv_ref.dtype)

    put(0, high_at, dk_high, dv_high)
    for p in range(planes):
        dq, dk, dv = tile(p, tiles.offset(p, 0), high)
        dq_high = dq_high + dq
        if p == 0:
            put(0, low_at, dk_low + dk, dv_low + dv)
            continue
        early = tiles.before(p)
        at = tiles.picked(p, 0)
        queries = (
            tiles.heads_of(q_ref, at),
            tiles.heads_of(g_ref, at),
            jnp.where(early, low[2], high[2]),
            jnp.where(early, low[3], high[3]),
        )
        dq, dk_mixed, dv_mixed = tile(p, tiles.picked(p, p), queries)
        dq_low = dq_low + jnp.where(early, dq, 0.0)
        dq_high = dq_high + jnp.where(early, 0.0, dq)
        put(
            p,
            tiles.offset(p, 0),
            dk + jnp.where(early, dk_mixed, 0.0),
            dv + jnp.where(early, dv_mixed, 0.0),
        )
        put(
            p,
            tiles.offset(p, 1),
            jnp.where(early, 0.0, dk_mixed),
            jnp.where(early, 0.0, dv_mixed),
        )
    scale = HEAD_DIM ** (-0.5)
    tiles.put_heads(dq_ref, low_at, dq_low * scale)
    tiles.put_heads(dq_ref, high_at, dq_high * scale)


def attn_specs(planes, rows, cols, heads):
    act = pl.BlockSpec((cols, rows), lambda s, info: (0, s))
    keys = pl.BlockSpec((planes, HEAD_DIM, rows), lambda s, info: (0, 0, s))
    lse = pl.BlockSpec((1, 2, heads * rows // 2), lambda s, info: (s, 0, 0))
    return act, keys, lse


def attn_cost(seqs, planes, rows, cols, dots):
    pairs = seqs * rows * rows // 4 * (2 * planes + 1) * (cols // HEAD_DIM)
    return pl.CostEstimate(
        flops=2 * dots * pairs * HEAD_DIM,
        bytes_accessed=2 * seqs * rows * (3 * cols + 4 * planes * HEAD_DIM),
        transcendentals=pairs,
    )


def attn_forward(info, query, key, value, seqs):
    planes, cols = key.shape[0], query.shape[0]
    rows, heads = query.shape[1] // seqs, cols // HEAD_DIM
    act, keys, lse = attn_specs(planes, rows, cols, heads)
    return pl.pallas_call(
        functools.partial(attn_fwd_kernel, planes, rows // 2, heads),
        out_shape=(
            jax.ShapeDtypeStruct(query.shape, LOW),
            jax.ShapeDtypeStruct((seqs, 2, heads * rows // 2), FULL),
        ),
        grid_spec=pltpu.PrefetchScalarGridSpec(
            num_scalar_prefetch=1,
            grid=(seqs,),
            in_specs=[act, keys, keys],
            out_specs=(act, lse),
        ),
        cost_estimate=attn_cost(seqs, planes, rows, cols, 2),
    )(info, query, key, value)


def attn_backward(info, query, key, value, out, lse_value, grad, seqs):
    planes, cols = key.shape[0], query.shape[0]
    rows, heads = query.shape[1] // seqs, cols // HEAD_DIM
    act, keys, lse = attn_specs(planes, rows, cols, heads)
    return pl.pallas_call(
        functools.partial(attn_bwd_kernel, planes, rows // 2, heads),
        out_shape=(
            jax.ShapeDtypeStruct(query.shape, FULL),
            jax.ShapeDtypeStruct(key.shape, LOW),
            jax.ShapeDtypeStruct(key.shape, LOW),
        ),
        grid_spec=pltpu.PrefetchScalarGridSpec(
            num_scalar_prefetch=1,
            grid=(seqs,),
            in_specs=[act, keys, keys, act, lse, act],
            out_specs=(act, keys, keys),
        ),
        cost_estimate=attn_cost(seqs, planes, rows, cols, 5),
    )(info, query, key, value, out, lse_value, grad)


def picker(lane_ref, mine_ref, other_ref):
    lane = lane_ref[0]
    chip, core = lane // 2, lane % 2

    def pick(d, *index):
        slot = (d // 2) ^ chip
        mine = mine_ref[(slot,) + index].astype(FULL)
        other = other_ref[(slot,) + index].astype(FULL)
        return jnp.where(core == d % 2, mine, other)

    return pick


def spread_mlp_kernel(lanes, planes, unit, lane_ref, mine_ref, other_ref, gate_ref, up_ref):
    pick = picker(lane_ref, mine_ref, other_ref)
    every = slice(None)
    for which, out_ref in enumerate((gate_ref, up_ref)):
        for p in range(planes):
            for d in range(lanes):
                start = (which * planes + p) * unit
                place = (p * lanes + d) * unit
                out_ref[:, place : place + unit] = pick(d, every, slice(start, start + unit))


def spread_attn_kernel(
    lanes, head_cols, out_cols, sharing, lane_ref, mine_ref, other_ref, q_ref, k_ref, v_ref, o_ref
):
    pick = picker(lane_ref, mine_ref, other_ref)
    every = slice(None)
    middle = head_cols + HEAD_DIM
    for d in range(lanes):
        q_ref[:, d * head_cols : (d + 1) * head_cols] = pick(d, every, slice(0, head_cols))
        o_ref[:, d * out_cols : (d + 1) * out_cols] = pick(
            d, every, slice(middle, middle + out_cols)
        )
    for h in range(lanes // sharing):
        for first, out_ref in ((0, k_ref), (1, v_ref)):
            total = None
            for d in range(h * sharing + first, (h + 1) * sharing, 2):
                part = pick(d, every, slice(head_cols, middle))
                total = part if total is None else total + part
            out_ref[:, h * HEAD_DIM : (h + 1) * HEAD_DIM] = total


def spread_down_kernel(lane_ref, mine_ref, other_ref, out_ref):
    core = lane_ref[0] % 2
    mine, other = mine_ref[0].astype(FULL), other_ref[0].astype(FULL)
    out_ref[...] = jnp.where(core == pl.program_id(0) % 2, mine, other)


def spread_call(kernel, lane, mine, other, rows, block, widths):
    chips, _, cols = mine.shape
    spec = pl.BlockSpec((chips, block, cols), lambda i, lane_ref: (0, i, 0))
    return pl.pallas_call(
        kernel,
        out_shape=tuple(jax.ShapeDtypeStruct((rows, w), FULL) for w in widths),
        grid_spec=pltpu.PrefetchScalarGridSpec(
            num_scalar_prefetch=1,
            grid=(rows // block,),
            in_specs=[spec, spec],
            out_specs=tuple(pl.BlockSpec((block, w), lambda i, lane_ref: (i, 0)) for w in widths),
        ),
        cost_estimate=pl.CostEstimate(
            flops=0, bytes_accessed=chips * rows * cols * 12, transcendentals=0
        ),
    )(lane, mine, other)


def spread_down(lane, mine, other):
    chips, rows, cols = mine.shape
    spec = pl.BlockSpec(
        (1, rows, cols), lambda d, lane_ref: ((d // 2) ^ (lane_ref[0] // 2), 0, 0)
    )
    return pl.pallas_call(
        spread_down_kernel,
        out_shape=jax.ShapeDtypeStruct((2 * chips * rows, cols), FULL),
        grid_spec=pltpu.PrefetchScalarGridSpec(
            num_scalar_prefetch=1,
            grid=(2 * chips,),
            in_specs=[spec, spec],
            out_specs=pl.BlockSpec((rows, cols), lambda d, lane_ref: (d, 0)),
        ),
        cost_estimate=pl.CostEstimate(
            flops=0, bytes_accessed=chips * rows * cols * 12, transcendentals=0
        ),
    )(lane, mine, other)


def on_device(
    tokens,
    block_order,
    attn_gain,
    w_query,
    w_key,
    w_value,
    w_out,
    mlp_gain,
    w_gate,
    w_up,
    w_down,
    cotangent,
):
    planes = lax.axis_size("shard")
    plane = lax.axis_index("shard")
    lanes = lax.axis_size("dp")
    lane = lax.axis_index("dp")
    odd = lax.rem(lane, 2) == 1
    rows = tokens.shape[1]
    width = tokens.shape[2]
    span = rows // 2
    seqs = lanes
    total_rows = seqs * rows
    own_width = width // planes
    heads = w_query.shape[1] // HEAD_DIM
    kv_heads = w_key.shape[1] // HEAD_DIM
    own_heads = heads // lanes
    head_cols = own_heads * HEAD_DIM
    kv_head = (lane * own_heads * kv_heads) // heads
    out_cols = w_out.shape[1] // lanes
    ff_rows = w_down.shape[0]
    unit = ff_rows // lanes
    own_ff = unit * planes
    scale = HEAD_DIM ** (-0.5)

    inputs = lax.all_gather(tokens[0], "dp", axis=0, tiled=True)
    upstream = lax.all_gather(cotangent[0], "dp", axis=0, tiled=True)
    table = lax.all_gather(block_order[0], "dp", axis=0, tiled=False)

    def columns(weight, start, count):
        return lax.dynamic_slice_in_dim(weight, start, count, 1).astype(LOW)

    kv_at = kv_head * HEAD_DIM
    qkv_piece = jnp.concatenate(
        [
            columns(w_query, lane * head_cols, head_cols),
            jnp.where(odd, columns(w_value, kv_at, HEAD_DIM), columns(w_key, kv_at, HEAD_DIM)),
        ],
        axis=1,
    )
    qkv_cols = head_cols + HEAD_DIM
    gain_rows = jnp.stack([attn_gain, mlp_gain]).astype(LOW)
    gain_reps = -(-own_width // qkv_cols)
    gain_rows = jnp.pad(gain_rows, ((0, 0), (0, gain_reps * qkv_cols - own_width)))
    gain_rows = gain_rows.reshape(2 * gain_reps, qkv_cols)
    gain_rows = jnp.pad(gain_rows, ((0, EXTRA - 2 * gain_reps), (0, 0)))
    qkv_parts = plane_parts(jnp.concatenate([qkv_piece, gain_rows], axis=0))
    qkv_mat = assemble([part[:own_width] for part in qkv_parts])
    gains = assemble(
        [
            part[own_width : own_width + 2 * gain_reps].reshape(2, -1)[:, :own_width]
            for part in qkv_parts
        ],
        1,
    )
    gain_one, gain_two = gains[0].astype(FULL), gains[1].astype(FULL)

    mlp_piece = jnp.concatenate(
        [
            columns(weight, p * ff_rows + lane * unit, unit)
            for weight in (w_gate, w_up)
            for p in range(planes)
        ],
        axis=1,
    )
    cut = (own_ff + 127) // 128 * 128
    first_piece = jnp.concatenate(
        [columns(w_out, lane * out_cols, out_cols), mlp_piece[:, :cut]], axis=1
    )
    second_piece = mlp_piece[:, cut:]
    first_piece, second_piece = lax.optimization_barrier((first_piece, second_piece))
    first_parts = plane_parts(first_piece)
    second_parts = plane_parts(second_piece)
    out_mat = assemble([part[:, :out_cols] for part in first_parts])
    mlp_mat = jnp.zeros((width, 2 * own_ff), LOW)
    for parts, start, place in ((first_parts, out_cols, 0), (second_parts, 0, cut)):
        for k, part in enumerate(parts):
            row = lax.rem(plane - k + planes, planes) * own_width
            mlp_mat = lax.dynamic_update_slice(mlp_mat, part[:, start:], (row, place))
    down_piece = lax.dynamic_slice_in_dim(w_down, lane * unit, unit, 0).astype(LOW)
    down_parts = plane_parts(down_piece)
    down_mat = assemble(down_parts)

    first_row = lane * head_cols
    owner = first_row // own_width
    row_piece = lax.dynamic_slice_in_dim(w_out, first_row - owner * own_width, head_cols, 0).astype(
        LOW
    )
    out_rows = jnp.where(owner == plane, row_piece, jnp.zeros_like(row_piece))
    for k in range(1, planes):
        pairs = []
        for d in range(lanes):
            source = (d * head_cols) // own_width
            pairs.append((d * planes + source, d * planes + (source + k) % planes))
        out_rows = out_rows + lax.ppermute(row_piece, ("dp", "shard"), pairs)

    grouped = table.reshape(seqs, planes, 2)
    order = lax.rem(plane - jnp.arange(planes, dtype=jnp.int32) + planes, planes)
    relative = jnp.take(grouped, order, axis=1)
    smaller = jnp.min(relative, axis=2)
    info = jnp.concatenate(
        [
            (relative[:, :, 0] > relative[:, :, 1]).astype(jnp.int32),
            (smaller < smaller[:, :1]).astype(jnp.int32),
        ],
        axis=1,
    )
    places = relative[:, 0, :, None] * span + jnp.arange(span, dtype=jnp.int32)
    frequency = ROPE_BASE ** (-(jnp.arange(HEAD_DIM // 2, dtype=FULL) * 2.0) / HEAD_DIM)
    angles = frequency[:, None] * places.reshape(-1).astype(FULL)[None, :]
    cosine, sine = jnp.cos(angles), jnp.sin(angles)

    wide = inputs.astype(FULL)
    scale_one = lax.rsqrt(jnp.mean(wide * wide, axis=-1, keepdims=True) + EPSILON)
    hidden_one = (wide * scale_one * gain_one).astype(LOW)
    qkv = contract(qkv_mat, hidden_one, 0, 1)
    half = qkv[head_cols:]
    half = jnp.where(odd, half, rope(half, cosine, sine)).astype(LOW)
    half_parts = plane_parts(half)
    query = rope(qkv[:head_cols].reshape(own_heads, HEAD_DIM, total_rows), cosine, sine)
    query = (query.astype(LOW).astype(FULL) * scale).astype(LOW).reshape(head_cols, total_rows)
    half_all = jnp.stack(half_parts, axis=0)
    other_half = swap_cores(half_all)
    key_all = jnp.where(odd, other_half, half_all)
    value_all = jnp.where(odd, half_all, other_half)
    attended, log_total = attn_forward(info, query, key_all, value_all, seqs)

    attended_all = lax.all_gather(attended, "dp", axis=0, tiled=True)
    branch = contract(out_mat, attended_all, 0, 0)
    own_inputs = lax.dynamic_slice_in_dim(inputs, lane * out_cols, out_cols, 1)
    middle_part = (own_inputs.astype(FULL).T + branch).astype(LOW)
    middle = lax.all_gather(middle_part, "dp", axis=0, tiled=True)
    wide_two = middle.astype(FULL)
    scale_two = lax.rsqrt(jnp.mean(wide_two * wide_two, axis=0, keepdims=True) + EPSILON)
    hidden_two = (wide_two * scale_two * gain_two[:, None]).astype(LOW)
    both = contract(mlp_mat, hidden_two, 0, 0)
    gate_value, up_value = both[:own_ff], both[own_ff:]
    sigmoid = jax.nn.sigmoid(gate_value)
    silu = gate_value * sigmoid
    inner = (silu * up_value).astype(LOW)

    inner_grad = contract(down_mat, upstream, 1, 1)
    gate_grad = inner_grad * up_value * sigmoid * (1.0 + gate_value * (1.0 - sigmoid))
    up_grad = inner_grad * silu
    both_grad = jnp.concatenate([gate_grad.astype(LOW), up_grad.astype(LOW)], axis=0)
    hidden_two_grad = contract(both_grad, mlp_mat, 0, 1).astype(LOW)
    hidden_two_own = lax.psum_scatter(hidden_two_grad, "dp", scatter_dimension=0, tiled=True)
    mlp_grad = contract(hidden_two, both_grad, 1, 1).astype(LOW)
    down_grad = contract(inner, upstream, 1, 0).astype(LOW)
    down_sent = plane_send(down_grad)
    mlp_sent = plane_send(mlp_grad)
    partial_out = contract(inner, down_mat, 0, 0).astype(LOW)
    hidden_two_own = hidden_two_own.astype(FULL)
    middle_own = lax.dynamic_slice_in_dim(middle, lane * rows, rows, 1).astype(FULL).T
    scale_own = lax.rsqrt(jnp.mean(middle_own * middle_own, axis=-1, keepdims=True) + EPSILON)
    normed_own = middle_own * scale_own
    gain_two_grad = jnp.sum(hidden_two_own * normed_own, axis=0)
    middle_grad = cotangent[0].astype(FULL) + norm_back(
        hidden_two_own, normed_own, scale_own, gain_two
    )
    middle_grad_low = middle_grad.astype(LOW)
    branch_grad = lax.all_gather(middle_grad_low, "dp", axis=0, tiled=True)

    partial_out, branch_grad = lax.optimization_barrier((partial_out, branch_grad))
    result = lax.psum_scatter(partial_out, "dp", scatter_dimension=0, tiled=True)
    block_out = (middle_own + result.astype(FULL)).astype(LOW)[None]

    attended_grad = contract(out_rows, branch_grad, 1, 1).astype(LOW)
    query_grad, key_grad, value_grad = attn_backward(
        info, query, key_all, value_all, attended, log_total, attended_grad, seqs
    )
    other_grad = swap_cores(jnp.where(odd, key_grad, value_grad))
    half_grad = (
        jnp.where(odd, value_grad, key_grad).astype(FULL) + other_grad.astype(FULL)
    ).astype(LOW)
    half_own = half_grad[0].astype(FULL)
    for k in range(1, planes):
        part = shift(half_grad[k], planes - k)
        half_own = half_own + part.astype(FULL)
    query_lin = rope(query_grad.reshape(own_heads, HEAD_DIM, total_rows), cosine, -sine)
    query_lin = query_lin.astype(LOW).reshape(head_cols, total_rows)
    half_lin = jnp.where(odd, half_own, rope(half_own, cosine, -sine)).astype(LOW)
    qkv_lin = jnp.concatenate([query_lin, half_lin], axis=0)
    hidden_one_part = contract(qkv_lin, qkv_mat, 0, 1)
    hidden_one_low = hidden_one_part.astype(LOW)
    hidden_one_grad = lax.psum_scatter(
        hidden_one_low, "dp", scatter_dimension=0, tiled=True
    ).astype(FULL)
    gain_one_grad = jnp.sum(hidden_one_low.astype(FULL) * (wide * scale_one), axis=0)
    own_tokens = tokens[0].astype(FULL)
    own_scale = lax.rsqrt(jnp.mean(own_tokens * own_tokens, axis=-1, keepdims=True) + EPSILON)
    input_norm_grad = norm_back(hidden_one_grad, own_tokens * own_scale, own_scale, gain_one)
    tokens_grad = (middle_grad + input_norm_grad)[None]

    branch_cols = lax.dynamic_slice_in_dim(branch_grad, lane * out_cols, out_cols, 1)
    qkv_grad = contract(hidden_one, qkv_lin, 0, 1).astype(LOW)
    out_grad = contract(attended_all, branch_cols, 1, 0).astype(LOW)
    piece_cols = qkv_cols + out_cols
    out_grad = lax.optimization_barrier(out_grad)
    attn_grad = jnp.concatenate([qkv_grad, out_grad], axis=1).reshape(planes, own_width, -1)
    gain_grads = jnp.stack([gain_one_grad, gain_two_grad]).astype(LOW)
    gain_grads = jnp.transpose(gain_grads.reshape(2, planes, own_width), (1, 0, 2))
    gain_grads = jnp.pad(gain_grads, ((0, 0), (0, EXTRA - 2), (0, piece_cols - own_width)))
    attn_grad = jnp.concatenate([attn_grad, gain_grads], axis=1)
    attn_sent = plane_send(attn_grad.reshape(-1, piece_cols))

    down_sum = plane_sum(down_sent)
    down_mine = jnp.stack(chip_stack(down_sum), axis=0)
    down_other = swap_cores(down_mine)
    mlp_sum = plane_sum(mlp_sent)
    mlp_mine = jnp.stack(chip_stack(mlp_sum), axis=0)
    mlp_other = swap_cores(mlp_mine)
    attn_sum = plane_sum(attn_sent)
    attn_mine = jnp.stack(chip_stack(attn_sum), axis=0)
    attn_other = swap_cores(attn_mine)

    lane_id = lane.astype(jnp.int32).reshape(1)
    if unit % 16 == 0:
        down_out = spread_down(lane_id, down_mine, down_other)
    else:
        down_out = lax.all_gather(down_sum, "dp", axis=0, tiled=True).astype(FULL)
    gate_out, up_out = spread_call(
        functools.partial(spread_mlp_kernel, lanes, planes, unit),
        lane_id,
        mlp_mine,
        mlp_other,
        own_width,
        min(64, own_width),
        (lanes * own_ff, lanes * own_ff),
    )
    query_out, key_out, value_out, out_out = spread_call(
        functools.partial(
            spread_attn_kernel, lanes, head_cols, out_cols, lanes // kv_heads
        ),
        lane_id,
        attn_mine,
        attn_other,
        own_width,
        EXTRA,
        (lanes * head_cols, kv_heads * HEAD_DIM, kv_heads * HEAD_DIM, lanes * out_cols),
    )
    gain_at = slice(own_width, own_width + 2)
    gain_own = jnp.sum(attn_mine[:, gain_at, :own_width].astype(FULL), axis=0) + jnp.sum(
        attn_other[:, gain_at, :own_width].astype(FULL), axis=0
    )
    return (
        block_out,
        tokens_grad,
        gain_own[0],
        query_out,
        key_out,
        value_out,
        out_out,
        gain_own[1],
        gate_out,
        up_out,
        down_out,
    )


def solution(mesh):
    rows = P("shard", None)
    acts = P("dp", "shard", None)
    gain = P("shard")
    weights = (gain, rows, rows, rows, rows, gain, rows, rows, rows)

    return jax.shard_map(
        on_device,
        mesh=mesh,
        in_specs=(acts, P("dp", None)) + weights + (acts,),
        out_specs=(acts, acts) + weights,
        check_vma=False,
    )
```

time: 1340 us -> 1080 us (0.81)
  waiting for transfers between devices: 847 us -> 628 us
  matrix products: 216 us -> 130 us
  Pallas kernels: 25.2 us -> 74.5 us
  starting transfers between devices: 47.2 us -> 85.5 us
  local copies, waits for them, and re-layouts: 96.1 us -> 66.8 us
    ppermute x24 -> x27, waiting for transfers between devices: 480 us -> 360 us  [shift(): return lax.ppermute(value, 'shard', pairs)]
    ppermute x0 -> x14, waiting for transfers between devices: none -> 103 us  [the longest x9 100 us: swap_chips(): return lax.ppermute(value, 'dp', [(d, d ^ 2 * mask) for d in range(lanes)])]
    dot_general x6 -> x0, matrix products: 86.8 us -> none  [the longest x1 19.8 us: on_device(): jnp.einsum('shqd,skd->shkq', grad_heads, value_all, preferred_element_typ...]
    reduce_scatter x1, waiting for transfers between devices: 73.1 us -> 0.02 us  [on_device(): lax.psum_scatter(partial_out, 'dp', scatter_dimension=0, tiled=True)]
    all_gather x4 -> x1, waiting for transfers between devices: 66.7 us -> 0.02 us  [on_device(): attended_all = lax.all_gather(attended, 'dp', axis=0, tiled=True)]
    reduce_scatter x1, waiting for transfers between devices: 61.7 us -> 0.01 us  [on_device(): lax.psum_scatter(hidden_one_low, 'dp', scatter_dimension=0, tiled=True)]
    pallas_call x2 -> x5, Pallas kernels: 25.2 us -> 74.5 us  [the longest x2 26.5 us: spread_call(): pl.pallas_call(kernel, out_shape=tuple((jax.ShapeDtypeStruct((rows, w), F...]
    all_gather x1, waiting for transfers between devices: 0.01 us -> 32.9 us  [on_device(): branch_grad = lax.all_gather(middle_grad_low, 'dp', axis=0, tiled=True)]
  transfers between devices with their start and end apart: 38 -> 52, of which waited for: 26 -> 26; matrix products, arithmetic and copies ran while one was open for 19% -> 15% of each run, Pallas kernels for 2% -> 3%
where the time goes in v1:
time: 1080 us; the launch traced here: 1070 us
  waiting for transfers between devices  628 us (58%)
  matrix products  130 us (12%)
  starting transfers between devices  85.5 us (8%)
  Pallas kernels  74.5 us (7%)
  local copies, waits for them, and re-layouts  66.8 us (6%)
  other arithmetic  61.4 us (6%)
  between operations  15.6 us (1%)
    ppermute x27, waiting for transfers between devices, shift(): return lax.ppermute(value, 'shard', pairs)  360 us
    dot_general x12, matrix products, contract(): lax.dot_general(left, right, (((left_dim,), (right_dim,)), ((), ())), pre...  130 us
    ppermute x9, waiting for transfers between devices, swap_chips(): return lax.ppermute(value, 'dp', [(d, d ^ 2 * mask) for d in range(lanes)])  100 us
    reduce_scatter x1, waiting for transfers between devices, on_device(): lax.psum_scatter(hidden_two_grad, 'dp', scatter_dimension=0, tiled=True)  93.5 us
    ppermute x27, starting transfers between devices, shift(): return lax.ppermute(value, 'shard', pairs)  64.7 us
    all_gather x1, waiting for transfers between devices, on_device(): branch_grad = lax.all_gather(middle_grad_low, 'dp', axis=0, tiled=True)  32.9 us
    pallas_call x2, Pallas kernels, spread_call(): pl.pallas_call(kernel, out_shape=tuple((jax.ShapeDtypeStruct((rows, w), F...  26.5 us
    pallas_call x1, Pallas kernels, attn_backward(): pl.pallas_call(functools.partial(attn_bwd_kernel, planes, rows // 2, head...  25 us
  transfers between devices with their start and end apart: 52, of which 26 were waited for; matrix products, arithmetic and copies ran while one was open for 15% of the time, Pallas kernels for 3%

profile of v1, /device:TPU:0, one launch (start us, length us, event | category | flops | bytes accessed | tf_op | source)
XLA Modules:
  0.0 1070.4 jit_solution(8045999159557031508)
XLA Ops:
  32.4 12.7 %collective-permute-done.4 = bf16[544,320]{1,0:T(8,128)(2,1)} collective-permute-done((bf16[544,320]{1,0:T(8,128)(2,1)S(1)}, bf16[544,320]{1,0:T(8,128)(2,1)}, u32[]{:S(2)}, u32[]{:S(2)}) %collective-permute-start.4) | collective-permute-done | bytes 348192 | tf_op jit(solution)/shard_map/ppermute | solution.py:28
  49.9 19.2 %all-gather.15.cloned.1.call-done = bf16[1,2048,2048]{1,2,0:T(8,128)(2,1)} async-done(((bf16[1,256,2048]{1,2,0:T(8,128)(2,1)}), bf16[1,2048,2048]{1,2,0:T(8,128)(2,1)}) %all-gather.15.cloned.1.call-update) | async-done | bytes 8388624 | tf_op jit(solution)/shard_map/all_gather | solution.py:444
  91.1 16.2 %collective-permute-done.7 = bf16[64,2048]{1,0:T(8,128)(2,1)} collective-permute-done((bf16[64,2048]{1,0:T(8,128)(2,1)S(1)}, bf16[64,2048]{1,0:T(8,128)(2,1)}, u32[]{:S(2)}, u32[]{:S(2)}) %collective-permute-start.7) | collective-permute-done | bytes 262176 | tf_op jit(solution)/shard_map/ppermute | solution.py:28
  114.0 12.3 %shard_map.203 = (bf16[256,2048]{1,0:T(8,128)(2,1)}, f32[8,2,512]{2,1,0:T(2,128)}) custom-call(s32[8,8]{1,0:T(8,128)} %add_convert_fusion.7.info_ref, bf16[256,2048]{1,0:T(8,128)(2,1)} %bitcast.139, bf16[4,64,2048]{2,1,0:T(8,128)(2,1)} %get-tuple-element.111.k_ref, bf16[4,64,2048]{2,1,0:T(8,128)(2,1)} %get-tuple-element.110.v_ref), custom_call_target="tpu_custom_call" | custom-call | flops 1207959552 | bytes 7340032 | tf_op jit(solution)/shard_map/pallas_call | solution.py:283
  141.8 22.2 %collective-permute-done = bf16[512,1024]{1,0:T(8,128)(2,1)S(1)} collective-permute-done((bf16[512,1024]{1,0:T(8,128)(2,1)S(1)}, bf16[512,1024]{1,0:T(8,128)(2,1)S(1)}, u32[]{:S(2)}, u32[]{:S(2)}) %collective-permute-start) | collective-permute-done | bytes 1048608 | tf_op jit(solution)/shard_map/ppermute | solution.py:28
  164.1 44.2 %collective-permute-done.1 = bf16[512,1024]{1,0:T(8,128)(2,1)S(1)} collective-permute-done((bf16[512,1024]{1,0:T(8,128)(2,1)S(1)}, bf16[512,1024]{1,0:T(8,128)(2,1)S(1)}, u32[]{:S(2)}, u32[]{:S(2)}) %collective-permute-start.1) | collective-permute-done | bytes 1048608 | tf_op jit(solution)/shard_map/ppermute | solution.py:28
  222.2 21.5 %collective-permute-start.13 = (bf16[176,2048]{1,0:T(8,128)(2,1)S(1)}, bf16[176,2048]{1,0:T(8,128)(2,1)}, u32[]{:S(2)}, u32[]{:S(2)}) collective-permute-start(bf16[176,2048]{1,0:T(8,128)(2,1)S(1)} %get-tuple-element.77), channel_id=1, source_target_pairs={{0,1},{1,2},{2,3},{3,0},{4,5},{5,6},{6,7},{7,4},{8,9},{9,10},{10,1... | collective-permute-start | bytes 2162696 | tf_op jit(solution)/shard_map/ppermute | solution.py:28
  254.6 9.0 collective-permute-done.13
  268.9 52.5 %collective-permute-done.14 = bf16[176,2048]{1,0:T(8,128)(2,1)} collective-permute-done((bf16[176,2048]{1,0:T(8,128)(2,1)S(1)}, bf16[176,2048]{1,0:T(8,128)(2,1)}, u32[]{:S(2)}, u32[]{:S(2)}) %collective-permute-start.14) | collective-permute-done | bytes 720928 | tf_op jit(solution)/shard_map/ppermute | solution.py:28
  344.3 18.5 %fusion.24 = f32[1408,2048]{1,0:T(8,128)} fusion(bf16[2048,1408]{1,0:T(8,128)(2,1)} %constant_dynamic-update-slice_fusion.8, bf16[2048,2048]{1,0:T(8,128)(2,1)S(1)} %copy-done.1, f32[2048]{0:T(1024)S(1)} %bitcast.149, f32[2048]{0:T(1024)S(1)} %add_rsqrt_fusion), kind=kOutput, calls=%fused_computation.48 | convolution fusion | flops 11827937280 | bytes 25706496 | tf_op jit(solution)/shard_map/dot_general | solution.py:20
  362.8 15.1 %multiply_convert_fusion.1 = (bf16[704,2048]{1,0:T(8,128)(2,1)S(1)}, bf16[704,2048]{1,0:T(8,128)(2,1)S(1)}, bf16[704,2048]{1,0:T(8,128)(2,1)}) fusion(f32[1408,2048]{1,0:T(8,128)} %fusion.24, bf16[704,2048]{1,0:T(8,128)(2,1)} %constant_dynamic-update-slice_fusion, bf16[1,2048,2048]{2,1,0:T(8,128)(2,1)} %all-gather.17.cloned.1.call-done), kind=kOutput, calls=%fused_computation.24 | convolution fusion | flops 5927206912 | bytes 31457280 | tf_op jit(solution)/shard_map/dot_general | solution.py:20
  380.4 16.7 %convolution_convert_fusion.1 = bf16[2048,2048]{0,1:T(8,128)(2,1)} fusion(bf16[2048,1408]{1,0:T(8,128)(2,1)} %constant_dynamic-update-slice_fusion.8, bf16[704,2048]{1,0:T(8,128)(2,1)S(1)} %get-tuple-element.83, bf16[704,2048]{1,0:T(8,128)(2,1)S(1)} %get-tuple-element.82), kind=kOutput, calls=%fused_computation.18 | convolution fusion | flops 11826888704 | bytes 19922944 | tf_op jit(solution)/shard_map/dot_general | solution.py:20
  400.8 93.5 %reduce-scatter.4.cloned.1.call-done = bf16[256,2048]{0,1:T(8,128)(2,1)} async-done(((bf16[2048,2048]{0,1:T(8,128)(2,1)}), bf16[256,2048]{0,1:T(8,128)(2,1)}) %reduce-scatter.4.cloned.1.call-update) | async-done | bytes 1048592 | tf_op jit(solution)/shard_map/reduce_scatter | solution.py:565
  512.4 11.4 %convolution_convert_fusion.3 = bf16[2048,2048]{0,1:T(8,128)(2,1)} fusion(bf16[704,2048]{1,0:T(8,128)(2,1)} %get-tuple-element.84, bf16[704,2048]{1,0:T(8,128)(2,1)} %constant_dynamic-update-slice_fusion), kind=kOutput, calls=%fused_computation.20 | convolution fusion | flops 5909774336 | bytes 14155776 | tf_op jit(solution)/shard_map/dot_general | solution.py:20
  523.8 32.9 %all-gather.13.cloned.1.call-done = bf16[2048,2048]{0,1:T(8,128)(2,1)} async-done(((bf16[256,2048]{0,1:T(8,128)(2,1)}), bf16[2048,2048]{0,1:T(8,128)(2,1)}) %all-gather.13.cloned.1.call-update) | async-done | bytes 8388624 | tf_op jit(solution)/shard_map/all_gather | solution.py:580
  556.7 18.2 %collective-permute-done.16 = bf16[256,2048]{1,0:T(8,128)(2,1)} collective-permute-done((bf16[256,2048]{1,0:T(8,128)(2,1)S(1)}, bf16[256,2048]{1,0:T(8,128)(2,1)}, u32[]{:S(2)}, u32[]{:S(2)}) %collective-permute-start.16) | collective-permute-done | bytes 1048608 | tf_op jit(solution)/shard_map/ppermute | solution.py:513
  582.3 25.0 %shard_map.204 = (f32[256,2048]{1,0:T(8,128)}, bf16[4,64,2048]{2,1,0:T(8,128)(2,1)}, bf16[4,64,2048]{2,1,0:T(8,128)(2,1)}) custom-call(s32[8,8]{1,0:T(8,128)} %add_convert_fusion.7.info_ref, bf16[256,2048]{1,0:T(8,128)(2,1)} %bitcast.140, bf16[4,64,2048]{2,1,0:T(8,128)(2,1)} %get-tuple-element.111.k_ref, bf16[4,64,2048]{2,1,0:T(8,128)(2,1)} %get-tuple-element.110.v_ref, ...), custom_call_target="tpu_custom_call" | custom-call | flops 3019898880 | bytes 7340032 | tf_op jit(solution)/shard_map/pallas_call | solution.py:303
  623.4 10.4 collective-permute-done.21
  635.2 9.3 fusion.3
  644.6 17.8 %convolution_convert_fusion.2 = bf16[2048,1408]{1,0:T(8,128)(2,1)S(1)} fusion(bf16[704,2048]{1,0:T(8,128)(2,1)} %copy-done.46, bf16[704,2048]{1,0:T(8,128)(2,1)} %copy-done.45, bf16[2048,2048]{1,0:T(8,128)(2,1)} %all-gather.11.cloned.1.call-done, f32[2048]{0:T(1024)S(1)} %bitcast.152, f32[2048]{0:T(1024)S(1)} %add_rsqrt_fusion), kind=kOutput, calls=%fused_computation.19 | convolution fusion | flops 11842355200 | bytes 19939328 | tf_op jit(solution)/shard_map/dot_general | solution.py:20
  673.0 31.6 %collective-permute-done.32 = bf16[512,1408]{1,0:T(8,128)(2,1)} collective-permute-done((bf16[512,1408]{1,0:T(8,128)(2,1)}, bf16[512,1408]{1,0:T(8,128)(2,1)}, u32[]{:S(2)}, u32[]{:S(2)}) %collective-permute-start.32) | collective-permute-done | bytes 1441824 | tf_op jit(solution)/shard_map/ppermute | solution.py:28
  704.6 92.8 %collective-permute-done.31 = bf16[512,1408]{1,0:T(8,128)(2,1)} collective-permute-done((bf16[512,1408]{1,0:T(8,128)(2,1)S(1)}, bf16[512,1408]{1,0:T(8,128)(2,1)}, u32[]{:S(2)}, u32[]{:S(2)}) %collective-permute-start.31) | collective-permute-done | bytes 1441824 | tf_op jit(solution)/shard_map/ppermute | solution.py:28
  815.2 32.2 %collective-permute-done.35 = bf16[512,1408]{1,0:T(8,128)(2,1)S(1)} collective-permute-done((bf16[512,1408]{1,0:T(8,128)(2,1)S(1)}, bf16[512,1408]{1,0:T(8,128)(2,1)S(1)}, u32[]{:S(2)}, u32[]{:S(2)}) %collective-permute-start.35) | collective-permute-done | bytes 1441824 | tf_op jit(solution)/shard_map/ppermute | solution.py:38
  847.5 28.3 %collective-permute-done.34 = bf16[512,1408]{1,0:T(8,128)(2,1)S(1)} collective-permute-done((bf16[512,1408]{1,0:T(8,128)(2,1)S(1)}, bf16[512,1408]{1,0:T(8,128)(2,1)S(1)}, u32[]{:S(2)}, u32[]{:S(2)}) %collective-permute-start.34) | collective-permute-done | bytes 1441824 | tf_op jit(solution)/shard_map/ppermute | solution.py:38
  906.5 13.5 %collective-permute-done.25 = bf16[544,576]{1,0:T(8,128)(2,1)} collective-permute-done((bf16[544,576]{1,0:T(8,128)(2,1)}, bf16[544,576]{1,0:T(8,128)(2,1)}, u32[]{:S(2)}, u32[]{:S(2)}) %collective-permute-start.25) | collective-permute-done | bytes 626720 | tf_op jit(solution)/shard_map/ppermute | solution.py:28
  921.4 40.8 %collective-permute-done.24 = bf16[544,576]{1,0:T(8,128)(2,1)} collective-permute-done((bf16[544,576]{1,0:T(8,128)(2,1)}, bf16[544,576]{1,0:T(8,128)(2,1)}, u32[]{:S(2)}, u32[]{:S(2)}) %collective-permute-start.24) | collective-permute-done | bytes 626720 | tf_op jit(solution)/shard_map/ppermute | solution.py:28
  967.9 13.4 %collective-permute-done.40 = bf16[176,2048]{1,0:T(8,128)(2,1)} collective-permute-done((bf16[176,2048]{1,0:T(8,128)(2,1)S(1)}, bf16[176,2048]{1,0:T(8,128)(2,1)}, u32[]{:S(2)}, u32[]{:S(2)}) %collective-permute-start.40) | collective-permute-done | bytes 720928 | tf_op jit(solution)/shard_map/ppermute | solution.py:38
  983.4 13.6 %collective-permute-done.28 = bf16[544,576]{1,0:T(8,128)(2,1)S(1)} collective-permute-done((bf16[544,576]{1,0:T(8,128)(2,1)S(1)}, bf16[544,576]{1,0:T(8,128)(2,1)S(1)}, u32[]{:S(2)}, u32[]{:S(2)}) %collective-permute-start.28) | collective-permute-done | bytes 626720 | tf_op jit(solution)/shard_map/ppermute | solution.py:38
  998.8 11.2 %collective-permute-done.26 = bf16[544,576]{1,0:T(8,128)(2,1)S(1)} collective-permute-done((bf16[544,576]{1,0:T(8,128)(2,1)S(1)}, bf16[544,576]{1,0:T(8,128)(2,1)S(1)}, u32[]{:S(2)}, u32[]{:S(2)}) %collective-permute-start.26) | collective-permute-done | bytes 626720 | tf_op jit(solution)/shard_map/ppermute | solution.py:38
  1013.8 10.6 shard_map.207
  1024.5 14.4 %shard_map.206 = (f32[512,5632]{1,0:T(8,128)}, f32[512,5632]{1,0:T(8,128)}) custom-call(s32[1]{0:T(128)} %bitcast.41.lane_ref, bf16[4,512,1408]{2,1,0:T(8,128)(2,1)} %pad_maximum_fusion.1.mine_ref, bf16[4,512,1408]{2,1,0:T(8,128)(2,1)} %collective-permute-done.36.other_ref), custom_call_target="tpu_custom_call" | custom-call | bytes 34603008 | tf_op jit(solution)/shard_map/pallas_call | solution.py:373
  1040.5 12.1 %shard_map.205 = (f32[512,2048]{1,0:T(8,128)}, f32[512,256]{1,0:T(8,128)}, f32[512,256]{1,0:T(8,128)}, f32[512,2048]{1,0:T(8,128)}) custom-call(s32[1]{0:T(128)} %bitcast.41.lane_ref, bf16[4,544,576]{2,1,0:T(8,128)(2,1)} %pad_maximum_fusion.5.mine_ref, bf16[4,544,576]{2,1,0:T(8,128)(2,1)} %collective-permute-done.29.other_ref), custom_call_target="tpu_custom_call" | custom-call | bytes 14155776 | tf_op jit(solution)/shard_map/pallas_call | solution.py:373
  (314 shorter events, 261.4 us)
Async XLA Ops:
  7.2 61.9 %all-gather.15.cloned.1.call-start = ((), (), s32[]{:S(2)}) async-start(), calls=%async_computation.9 | async-start | bytes 9437184 | tf_op jit(solution)/shard_map/all_gather | solution.py:444
  9.5 200.7 %all-gather.9.cloned.1.call-start = ((), (), s32[]{:S(2)}) async-start(), calls=%async_computation.3 | async-start | bytes 9437184 | tf_op jit(solution)/shard_map/all_gather | solution.py:546
  126.4 211.9 %all-gather.11.cloned.1.call-start = ((), (), s32[]{:S(2)}) async-start(), calls=%async_computation.4 | async-start | bytes 9437184 | tf_op jit(solution)/shard_map/all_gather | solution.py:550
  136.8 71.5 %collective-permute-start.1 = (bf16[512,1024]{1,0:T(8,128)(2,1)S(1)}, bf16[512,1024]{1,0:T(8,128)(2,1)S(1)}, u32[]{:S(2)}, u32[]{:S(2)}) collective-permute-start(bf16[512,1024]{1,0:T(8,128)(2,1)S(1)} %pad_maximum_fusion.8), channel_id=1, source_target_pairs={{0,2},{1,3},{2,0},{3,1},{4,6},{5,7},{6,4},{7,5},{8,10},{9,11},{10,... | collective-permute-start | bytes 3145736 | tf_op jit(solution)/shard_map/ppermute | solution.py:28
  138.8 69.5 %collective-permute-start.2 = (bf16[512,1024]{1,0:T(8,128)(2,1)S(1)}, bf16[512,1024]{1,0:T(8,128)(2,1)S(1)}, u32[]{:S(2)}, u32[]{:S(2)}) collective-permute-start(bf16[512,1024]{1,0:T(8,128)(2,1)S(1)} %pad_maximum_fusion.8), channel_id=1, source_target_pairs={{0,3},{1,0},{2,1},{3,2},{4,7},{5,4},{6,5},{7,6},{8,11},{9,8},{10,9... | collective-permute-start | bytes 3145736 | tf_op jit(solution)/shard_map/ppermute | solution.py:28
  217.3 145.5 %all-gather.17.cloned.1.call-start = ((), (), s32[]{:S(2)}) async-start(), calls=%async_computation.10 | async-start | bytes 9437184 | tf_op jit(solution)/shard_map/all_gather | solution.py:445
  217.8 276.5 %reduce-scatter.4.cloned.1.call-start = ((), (), s32[]{:S(2)}) async-start(), calls=%async_computation.5 | async-start | bytes 9437184 | tf_op jit(solution)/shard_map/reduce_scatter | solution.py:565
  243.8 77.6 %collective-permute-start.14 = (bf16[176,2048]{1,0:T(8,128)(2,1)S(1)}, bf16[176,2048]{1,0:T(8,128)(2,1)}, u32[]{:S(2)}, u32[]{:S(2)}) collective-permute-start(bf16[176,2048]{1,0:T(8,128)(2,1)S(1)} %get-tuple-element.77), channel_id=1, source_target_pairs={{0,2},{1,3},{2,0},{3,1},{4,6},{5,7},{6,4},{7,5},{8,10},{9,11},{10,... | collective-permute-start | bytes 2162696 | tf_op jit(solution)/shard_map/ppermute | solution.py:28
  246.9 82.5 %collective-permute-start.10 = (bf16[512,640]{1,0:T(8,128)(2,1)S(1)}, bf16[512,640]{1,0:T(8,128)(2,1)}, u32[]{:S(2)}, u32[]{:S(2)}) collective-permute-start(bf16[512,640]{1,0:T(8,128)(2,1)S(1)} %pad_maximum_fusion.13), channel_id=1, source_target_pairs={{0,1},{1,2},{2,3},{3,0},{4,5},{5,6},{6,7},{7,4},{8,9},{9,10},{10,1... | collective-permute-start | bytes 1966088 | tf_op jit(solution)/shard_map/ppermute | solution.py:28
  246.9 88.5 %collective-permute-start.11 = (bf16[512,640]{1,0:T(8,128)(2,1)S(1)}, bf16[512,640]{1,0:T(8,128)(2,1)}, u32[]{:S(2)}, u32[]{:S(2)}) collective-permute-start(bf16[512,640]{1,0:T(8,128)(2,1)S(1)} %pad_maximum_fusion.13), channel_id=1, source_target_pairs={{0,2},{1,3},{2,0},{3,1},{4,6},{5,7},{6,4},{7,5},{8,10},{9,11},{10,... | collective-permute-start | bytes 1966088 | tf_op jit(solution)/shard_map/ppermute | solution.py:28
  247.0 76.7 %collective-permute-start.15 = (bf16[176,2048]{1,0:T(8,128)(2,1)S(1)}, bf16[176,2048]{1,0:T(8,128)(2,1)}, u32[]{:S(2)}, u32[]{:S(2)}) collective-permute-start(bf16[176,2048]{1,0:T(8,128)(2,1)S(1)} %get-tuple-element.77), channel_id=1, source_target_pairs={{0,3},{1,0},{2,1},{3,2},{4,7},{5,4},{6,5},{7,6},{8,11},{9,8},{10,9... | collective-permute-start | bytes 2162696 | tf_op jit(solution)/shard_map/ppermute | solution.py:28
  263.6 73.8 %collective-permute-start.12 = (bf16[512,640]{1,0:T(8,128)(2,1)S(1)}, bf16[512,640]{1,0:T(8,128)(2,1)S(1)}, u32[]{:S(2)}, u32[]{:S(2)}) collective-permute-start(bf16[512,640]{1,0:T(8,128)(2,1)S(1)} %pad_maximum_fusion.13), channel_id=1, source_target_pairs={{0,3},{1,0},{2,1},{3,2},{4,7},{5,4},{6,5},{7,6},{8,11},{9,8},{10,9... | collective-permute-start | bytes 1966088 | tf_op jit(solution)/shard_map/ppermute | solution.py:28
  397.2 159.6 %all-gather.13.cloned.1.call-start = ((), (), s32[]{:S(2)}) async-start(), calls=%async_computation.6 | async-start | bytes 9437184 | tf_op jit(solution)/shard_map/all_gather | solution.py:580
  500.7 552.5 %reduce-scatter.8.cloned.1.call-start = ((), (), s32[]{:S(2)}) async-start(), calls=%async_computation.8 | async-start | bytes 9437184 | tf_op jit(solution)/shard_map/reduce_scatter | solution.py:604
  502.5 54.2 %collective-permute-start.18 = (bf16[256,2048]{1,0:T(8,128)(2,1)S(1)}, bf16[256,2048]{1,0:T(8,128)(2,1)S(1)}, u32[]{:S(2)}, u32[]{:S(2)}) collective-permute-start(bf16[256,2048]{1,0:T(8,128)(2,1)S(1)} %dynamic-slice_convert_fusion), channel_id=1, source_target_pairs={{0,3},{4,7},{9,8},{13,12},{18,17},{22,21},{27,26},{31,30}} | collective-permute-start | bytes 3145736 | tf_op jit(solution)/shard_map/ppermute | solution.py:513
  507.8 48.9 %collective-permute-start.17 = (bf16[256,2048]{1,0:T(8,128)(2,1)S(1)}, bf16[256,2048]{1,0:T(8,128)(2,1)}, u32[]{:S(2)}, u32[]{:S(2)}) collective-permute-start(bf16[256,2048]{1,0:T(8,128)(2,1)S(1)} %dynamic-slice_convert_fusion), channel_id=1, source_target_pairs={{0,2},{4,6},{9,11},{13,15},{18,16},{22,20},{27,25},{31,29}} | collective-permute-start | bytes 3145736 | tf_op jit(solution)/shard_map/ppermute | solution.py:513
  510.1 64.8 %collective-permute-start.16 = (bf16[256,2048]{1,0:T(8,128)(2,1)S(1)}, bf16[256,2048]{1,0:T(8,128)(2,1)}, u32[]{:S(2)}, u32[]{:S(2)}) collective-permute-start(bf16[256,2048]{1,0:T(8,128)(2,1)S(1)} %dynamic-slice_convert_fusion), channel_id=1, source_target_pairs={{0,1},{4,5},{9,10},{13,14},{18,19},{22,23},{27,24},{31,28}} | collective-permute-start | bytes 3145736 | tf_op jit(solution)/shard_map/ppermute | solution.py:513
  644.6 410.4 %reduce-scatter.6.cloned.1.call-start = ((), (), s32[]{:S(2)}) async-start(), calls=%async_computation.7 | async-start | bytes 9437184 | tf_op jit(solution)/shard_map/reduce_scatter | solution.py:583
  672.2 125.2 %collective-permute-start.31 = (bf16[512,1408]{1,0:T(8,128)(2,1)S(1)}, bf16[512,1408]{1,0:T(8,128)(2,1)}, u32[]{:S(2)}, u32[]{:S(2)}) collective-permute-start(bf16[512,1408]{1,0:T(8,128)(2,1)S(1)} %get-tuple-element.97), channel_id=1, source_target_pairs={{0,2},{1,3},{2,0},{3,1},{4,6},{5,7},{6,4},{7,5},{8,10},{9,11},{10,... | collective-permute-start | bytes 4325384 | tf_op jit(solution)/shard_map/ppermute | solution.py:28
  672.9 124.5 %collective-permute-start.30 = (bf16[512,1408]{1,0:T(8,128)(2,1)S(1)}, bf16[512,1408]{1,0:T(8,128)(2,1)}, u32[]{:S(2)}, u32[]{:S(2)}) collective-permute-start(bf16[512,1408]{1,0:T(8,128)(2,1)S(1)} %get-tuple-element.95), channel_id=1, source_target_pairs={{0,1},{1,2},{2,3},{3,0},{4,5},{5,6},{6,7},{7,4},{8,9},{9,10},{10,1... | collective-permute-start | bytes 4325384 | tf_op jit(solution)/shard_map/ppermute | solution.py:28
  800.8 46.7 %collective-permute-start.35 = (bf16[512,1408]{1,0:T(8,128)(2,1)S(1)}, bf16[512,1408]{1,0:T(8,128)(2,1)S(1)}, u32[]{:S(2)}, u32[]{:S(2)}) collective-permute-start(bf16[512,1408]{1,0:T(8,128)(2,1)S(1)} %add_convert_fusion), channel_id=1, source_target_pairs={{0,24},{4,28},{8,16},{12,20},{16,8},{20,12},{24,0},{28,4},{1,25},{... | collective-permute-start | bytes 4325384 | tf_op jit(solution)/shard_map/ppermute | solution.py:38
  801.9 73.8 %collective-permute-start.34 = (bf16[512,1408]{1,0:T(8,128)(2,1)S(1)}, bf16[512,1408]{1,0:T(8,128)(2,1)S(1)}, u32[]{:S(2)}, u32[]{:S(2)}) collective-permute-start(bf16[512,1408]{1,0:T(8,128)(2,1)S(1)} %add_convert_fusion), channel_id=1, source_target_pairs={{0,16},{4,20},{8,24},{12,28},{16,0},{20,4},{24,8},{28,12},{1,17},{... | collective-permute-start | bytes 4325384 | tf_op jit(solution)/shard_map/ppermute | solution.py:38
  801.9 73.8 %collective-permute-start.33 = (bf16[512,1408]{1,0:T(8,128)(2,1)S(1)}, bf16[512,1408]{1,0:T(8,128)(2,1)S(1)}, u32[]{:S(2)}, u32[]{:S(2)}) collective-permute-start(bf16[512,1408]{1,0:T(8,128)(2,1)S(1)} %add_convert_fusion), channel_id=1, source_target_pairs={{0,8},{4,12},{8,0},{12,4},{16,24},{20,28},{24,16},{28,20},{1,9},{5... | collective-permute-start | bytes 4325384 | tf_op jit(solution)/shard_map/ppermute | solution.py:38
  814.5 85.9 %collective-permute-start.39 = (bf16[176,2048]{1,0:T(8,128)(2,1)}, bf16[176,2048]{1,0:T(8,128)(2,1)}, u32[]{:S(2)}, u32[]{:S(2)}) collective-permute-start(bf16[176,2048]{1,0:T(8,128)(2,1)} %get-tuple-element.99), channel_id=1, source_target_pairs={{0,3},{1,0},{2,1},{3,2},{4,7},{5,4},{6,5},{7,6},{8,11},{9,8},{10,9... | collective-permute-start | bytes 2162696 | tf_op jit(solution)/shard_map/ppermute | solution.py:28
  814.5 86.3 %collective-permute-start.38 = (bf16[176,2048]{1,0:T(8,128)(2,1)}, bf16[176,2048]{1,0:T(8,128)(2,1)}, u32[]{:S(2)}, u32[]{:S(2)}) collective-permute-start(bf16[176,2048]{1,0:T(8,128)(2,1)} %get-tuple-element.100), channel_id=1, source_target_pairs={{0,2},{1,3},{2,0},{3,1},{4,6},{5,7},{6,4},{7,5},{8,10},{9,11},{10,... | collective-permute-start | bytes 2162696 | tf_op jit(solution)/shard_map/ppermute | solution.py:28
  847.5 55.4 %collective-permute-start.37 = (bf16[176,2048]{1,0:T(8,128)(2,1)}, bf16[176,2048]{1,0:T(8,128)(2,1)}, u32[]{:S(2)}, u32[]{:S(2)}) collective-permute-start(bf16[176,2048]{1,0:T(8,128)(2,1)} %get-tuple-element.98), channel_id=1, source_target_pairs={{0,1},{1,2},{2,3},{3,0},{4,5},{5,6},{6,7},{7,4},{8,9},{9,10},{10,1... | collective-permute-start | bytes 2162696 | tf_op jit(solution)/shard_map/ppermute | solution.py:28
  879.2 145.3 %collective-permute-start.36 = (bf16[4,512,1408]{2,1,0:T(8,128)(2,1)}, bf16[4,512,1408]{2,1,0:T(8,128)(2,1)}, u32[]{:S(2)}, u32[]{:S(2)}) collective-permute-start(bf16[4,512,1408]{2,1,0:T(8,128)(2,1)} %pad_maximum_fusion.1.mine_ref), channel_id=1, source_target_pairs={{0,4},{4,0},{8,12},{12,8},{16,20},{20,16},{24,28},{28,24},{1,5},{5... | collective-permute-start | bytes 17301512 | tf_op jit(solution)/shard_map/ppermute | solution.py:33
  900.4 61.8 %collective-permute-start.24 = (bf16[544,576]{1,0:T(8,128)(2,1)}, bf16[544,576]{1,0:T(8,128)(2,1)}, u32[]{:S(2)}, u32[]{:S(2)}) collective-permute-start(bf16[544,576]{1,0:T(8,128)(2,1)} %get-tuple-element.103), channel_id=1, source_target_pairs={{0,2},{1,3},{2,0},{3,1},{4,6},{5,7},{6,4},{7,5},{8,10},{9,11},{10,... | collective-permute-start | bytes 1880072 | tf_op jit(solution)/shard_map/ppermute | solution.py:28
  900.9 61.6 %collective-permute-start.23 = (bf16[544,576]{1,0:T(8,128)(2,1)}, bf16[544,576]{1,0:T(8,128)(2,1)}, u32[]{:S(2)}, u32[]{:S(2)}) collective-permute-start(bf16[544,576]{1,0:T(8,128)(2,1)} %get-tuple-element.101), channel_id=1, source_target_pairs={{0,1},{1,2},{2,3},{3,0},{4,5},{5,6},{6,7},{7,4},{8,9},{9,10},{10,1... | collective-permute-start | bytes 1880072 | tf_op jit(solution)/shard_map/ppermute | solution.py:28
  905.2 61.9 %collective-permute-start.42 = (bf16[176,2048]{1,0:T(8,128)(2,1)S(1)}, bf16[176,2048]{1,0:T(8,128)(2,1)}, u32[]{:S(2)}, u32[]{:S(2)}) collective-permute-start(bf16[176,2048]{1,0:T(8,128)(2,1)S(1)} %add_convert_fusion.2), channel_id=1, source_target_pairs={{0,24},{4,28},{8,16},{12,20},{16,8},{20,12},{24,0},{28,4},{1,25},{... | collective-permute-start | bytes 2162696 | tf_op jit(solution)/shard_map/ppermute | solution.py:38
  920.0 47.6 %collective-permute-start.41 = (bf16[176,2048]{1,0:T(8,128)(2,1)S(1)}, bf16[176,2048]{1,0:T(8,128)(2,1)}, u32[]{:S(2)}, u32[]{:S(2)}) collective-permute-start(bf16[176,2048]{1,0:T(8,128)(2,1)S(1)} %add_convert_fusion.2), channel_id=1, source_target_pairs={{0,16},{4,20},{8,24},{12,28},{16,0},{20,4},{24,8},{28,12},{1,17},{... | collective-permute-start | bytes 2162696 | tf_op jit(solution)/shard_map/ppermute | solution.py:38
  967.6 42.4 %collective-permute-start.26 = (bf16[544,576]{1,0:T(8,128)(2,1)S(1)}, bf16[544,576]{1,0:T(8,128)(2,1)S(1)}, u32[]{:S(2)}, u32[]{:S(2)}) collective-permute-start(bf16[544,576]{1,0:T(8,128)(2,1)S(1)} %add_convert_fusion.3), channel_id=1, source_target_pairs={{0,8},{4,12},{8,0},{12,4},{16,24},{20,28},{24,16},{28,20},{1,9},{5... | collective-permute-start | bytes 1880072 | tf_op jit(solution)/shard_map/ppermute | solution.py:38
  (67 other events, 1538.5 us)
Sparse Core Ops, SparseCore 0:
  10.5 58.5 all-gather.14
  126.5 53.6 all-gather.8
  217.4 75.0 all-gather.10
  294.2 54.2 all-gather.16
  397.3 97.0 reduce-scatter.3
  500.8 55.8 all-gather.12
  644.7 74.3 reduce-scatter.7
  722.5 135.9 reduce-scatter.5

commit v2 on v1

--- a/solution.py
+++ b/solution.py
@@ -8,6 +8,7 @@
 from jax.sharding import PartitionSpec as P
 
 HEAD_DIM = 64
+DP, SHARD = "dp", "shard"
 EPSILON = 1e-05
 ROPE_BASE = 10000.0
 MASKED = -1e30
@@ -23,29 +24,29 @@
 
 
 def shift(value, amount):
-    count = lax.axis_size("shard")
+    count = lax.axis_size(SHARD)
     pairs = [(i, (i + amount) % count) for i in range(count)]
-    return lax.ppermute(value, "shard", pairs)
+    return lax.ppermute(value, SHARD, pairs)
 
 
 def swap_cores(value):
-    lanes = lax.axis_size("dp")
-    return lax.ppermute(value, "dp", [(d, d ^ 1) for d in range(lanes)])
+    lanes = lax.axis_size(DP)
+    return lax.ppermute(value, DP, [(d, d ^ 1) for d in range(lanes)])
 
 
 def swap_chips(value, mask):
-    lanes = lax.axis_size("dp")
-    return lax.ppermute(value, "dp", [(d, d ^ (2 * mask)) for d in range(lanes)])
+    lanes = lax.axis_size(DP)
+    return lax.ppermute(value, DP, [(d, d ^ (2 * mask)) for d in range(lanes)])
 
 
 def plane_parts(value):
-    count = lax.axis_size("shard")
+    count = lax.axis_size(SHARD)
     return [value] + [shift(value, k) for k in range(1, count)]
 
 
 def assemble(parts, axis=0):
-    count = lax.axis_size("shard")
-    rank = lax.axis_index("shard")
+    count = lax.axis_size(SHARD)
+    rank = lax.axis_index(SHARD)
     rows = parts[0].shape[axis]
     shape = list(parts[0].shape)
     shape[axis] = rows * count
@@ -57,8 +58,8 @@
 
 
 def plane_send(value):
-    count = lax.axis_size("shard")
-    rank = lax.axis_index("shard")
+    count = lax.axis_size(SHARD)
+    rank = lax.axis_index(SHARD)
     rows = value.shape[0] // count
     parts = []
     for k in range(count):
@@ -76,7 +77,7 @@
 
 
 def chip_stack(value):
-    chips = lax.axis_size("dp") // 2
+    chips = lax.axis_size(DP) // 2
     return [value] + [swap_chips(value, k) for k in range(1, chips)]
 
 
@@ -419,10 +420,10 @@
     w_down,
     cotangent,
 ):
-    planes = lax.axis_size("shard")
-    plane = lax.axis_index("shard")
-    lanes = lax.axis_size("dp")
-    lane = lax.axis_index("dp")
+    planes = lax.axis_size(SHARD)
+    plane = lax.axis_index(SHARD)
+    lanes = lax.axis_size(DP)
+    lane = lax.axis_index(DP)
     odd = lax.rem(lane, 2) == 1
     rows = tokens.shape[1]
     width = tokens.shape[2]
@@ -441,9 +442,9 @@
     own_ff = unit * planes
     scale = HEAD_DIM ** (-0.5)
 
-    inputs = lax.all_gather(tokens[0], "dp", axis=0, tiled=True)
-    upstream = lax.all_gather(cotangent[0], "dp", axis=0, tiled=True)
-    table = lax.all_gather(block_order[0], "dp", axis=0, tiled=False)
+    inputs = lax.all_gather(tokens[0], DP, axis=0, tiled=True)
+    upstream = lax.all_gather(cotangent[0], DP, axis=0, tiled=True)
+    table = lax.all_gather(block_order[0], DP, axis=0, tiled=False)
 
     def columns(weight, start, count):
         return lax.dynamic_slice_in_dim(weight, start, count, 1).astype(LOW)
@@ -481,7 +482,7 @@
         ],
         axis=1,
     )
-    cut = (own_ff + 127) // 128 * 128
+    cut = 128
     first_piece = jnp.concatenate(
         [columns(w_out, lane * out_cols, out_cols), mlp_piece[:, :cut]], axis=1
     )
@@ -498,19 +499,6 @@
     down_piece = lax.dynamic_slice_in_dim(w_down, lane * unit, unit, 0).astype(LOW)
     down_parts = plane_parts(down_piece)
     down_mat = assemble(down_parts)
-
-    first_row = lane * head_cols
-    owner = first_row // own_width
-    row_piece = lax.dynamic_slice_in_dim(w_out, first_row - owner * own_width, head_cols, 0).astype(
-        LOW
-    )
-    out_rows = jnp.where(owner == plane, row_piece, jnp.zeros_like(row_piece))
-    for k in range(1, planes):
-        pairs = []
-        for d in range(lanes):
-            source = (d * head_cols) // own_width
-            pairs.append((d * planes + source, d * planes + (source + k) % planes))
-        out_rows = out_rows + lax.ppermute(row_piece, ("dp", "shard"), pairs)
 
     grouped = table.reshape(seqs, planes, 2)
     order = lax.rem(plane - jnp.arange(planes, dtype=jnp.int32) + planes, planes)
@@ -543,11 +531,18 @@
     value_all = jnp.where(odd, half_all, other_half)
     attended, log_total = attn_forward(info, query, key_all, value_all, seqs)
 
-    attended_all = lax.all_gather(attended, "dp", axis=0, tiled=True)
+    attended_all = lax.all_gather(attended, DP, axis=0, tiled=True)
     branch = contract(out_mat, attended_all, 0, 0)
     own_inputs = lax.dynamic_slice_in_dim(inputs, lane * out_cols, out_cols, 1)
+    out_rows = jnp.zeros((head_cols, lanes * out_cols), LOW)
+    for m in range(lanes):
+        peer = lane ^ m
+        block = lax.dynamic_slice_in_dim(out_mat, peer * head_cols, head_cols, 0)
+        if m:
+            block = lax.ppermute(block, DP, [(d, d ^ m) for d in range(lanes)])
+        out_rows = lax.dynamic_update_slice_in_dim(out_rows, block, peer * out_cols, 1)
     middle_part = (own_inputs.astype(FULL).T + branch).astype(LOW)
-    middle = lax.all_gather(middle_part, "dp", axis=0, tiled=True)
+    middle = lax.all_gather(middle_part, DP, axis=0, tiled=True)
     wide_two = middle.astype(FULL)
     scale_two = lax.rsqrt(jnp.mean(wide_two * wide_two, axis=0, keepdims=True) + EPSILON)
     hidden_two = (wide_two * scale_two * gain_two[:, None]).astype(LOW)
@@ -562,11 +557,14 @@
     up_grad = inner_grad * silu
     both_grad = jnp.concatenate([gate_grad.astype(LOW), up_grad.astype(LOW)], axis=0)
     hidden_two_grad = contract(both_grad, mlp_mat, 0, 1).astype(LOW)
-    hidden_two_own = lax.psum_scatter(hidden_two_grad, "dp", scatter_dimension=0, tiled=True)
+    hidden_two_own = lax.psum_scatter(hidden_two_grad, DP, scatter_dimension=0, tiled=True)
     mlp_grad = contract(hidden_two, both_grad, 1, 1).astype(LOW)
     down_grad = contract(inner, upstream, 1, 0).astype(LOW)
     down_sent = plane_send(down_grad)
-    mlp_sent = plane_send(mlp_grad)
+    tail = own_width * 3 // 16
+    mlp_grad = mlp_grad.reshape(planes, own_width, 2 * own_ff)
+    mlp_sent = plane_send(mlp_grad[:, :-tail].reshape(-1, 2 * own_ff))
+    mlp_tail_sent = plane_send(mlp_grad[:, -tail:].reshape(-1, 2 * own_ff))
     partial_out = contract(inner, down_mat, 0, 0).astype(LOW)
     hidden_two_own = hidden_two_own.astype(FULL)
     middle_own = lax.dynamic_slice_in_dim(middle, lane * rows, rows, 1).astype(FULL).T
@@ -577,10 +575,10 @@
         hidden_two_own, normed_own, scale_own, gain_two
     )
     middle_grad_low = middle_grad.astype(LOW)
-    branch_grad = lax.all_gather(middle_grad_low, "dp", axis=0, tiled=True)
+    branch_grad = lax.all_gather(middle_grad_low, DP, axis=0, tiled=True)
 
     partial_out, branch_grad = lax.optimization_barrier((partial_out, branch_grad))
-    result = lax.psum_scatter(partial_out, "dp", scatter_dimension=0, tiled=True)
+    result = lax.psum_scatter(partial_out, DP, scatter_dimension=0, tiled=True)
     block_out = (middle_own + result.astype(FULL)).astype(LOW)[None]
 
     attended_grad = contract(out_rows, branch_grad, 1, 1).astype(LOW)
@@ -602,7 +600,7 @@
     hidden_one_part = contract(qkv_lin, qkv_mat, 0, 1)
     hidden_one_low = hidden_one_part.astype(LOW)
     hidden_one_grad = lax.psum_scatter(
-        hidden_one_low, "dp", scatter_dimension=0, tiled=True
+        hidden_one_low, DP, scatter_dimension=0, tiled=True
     ).astype(FULL)
     gain_one_grad = jnp.sum(hidden_one_low.astype(FULL) * (wide * scale_one), axis=0)
     own_tokens = tokens[0].astype(FULL)
@@ -625,7 +623,7 @@
     down_sum = plane_sum(down_sent)
     down_mine = jnp.stack(chip_stack(down_sum), axis=0)
     down_other = swap_cores(down_mine)
-    mlp_sum = plane_sum(mlp_sent)
+    mlp_sum = jnp.concatenate([plane_sum(mlp_sent), plane_sum(mlp_tail_sent)], axis=0)
     mlp_mine = jnp.stack(chip_stack(mlp_sum), axis=0)
     mlp_other = swap_cores(mlp_mine)
     attn_sum = plane_sum(attn_sent)
@@ -636,7 +634,7 @@
     if unit % 16 == 0:
         down_out = spread_down(lane_id, down_mine, down_other)
     else:
-        down_out = lax.all_gather(down_sum, "dp", axis=0, tiled=True).astype(FULL)
+        down_out = lax.all_gather(down_sum, DP, axis=0, tiled=True).astype(FULL)
     gate_out, up_out = spread_call(
         functools.partial(spread_mlp_kernel, lanes, planes, unit),
         lane_id,
@@ -677,15 +675,15 @@
 
 
 def solution(mesh):
-    rows = P("shard", None)
-    acts = P("dp", "shard", None)
-    gain = P("shard")
+    rows = P(SHARD, None)
+    acts = P(DP, SHARD, None)
+    gain = P(SHARD)
     weights = (gain, rows, rows, rows, rows, gain, rows, rows, rows)
 
     return jax.shard_map(
         on_device,
         mesh=mesh,
-        in_specs=(acts, P("dp", None)) + weights + (acts,),
+        in_specs=(acts, P(DP, None)) + weights + (acts,),
         out_specs=(acts, acts) + weights,
         check_vma=False,
     )

time: 1080 us -> 1090 us (level)
    reduce_scatter x3, waiting for transfers between devices: 93.6 us -> 68.2 us  [the longest x1 68.2 us: on_device(): lax.psum_scatter(hidden_two_grad, DP, scatter_dimension=0, tiled=True)]
    ppermute x44 -> x51, waiting for transfers between devices: 481 us -> 505 us  [the longest x30 412 us: shift(): return lax.ppermute(value, SHARD, pairs)]
    ppermute x44 -> x51, starting transfers between devices: 84.9 us -> 89.8 us  [the longest x30 71.1 us: shift(): return lax.ppermute(value, SHARD, pairs)]
  transfers between devices with their start and end apart: 52 -> 59, of which waited for: 26 -> 30; matrix products, arithmetic and copies ran while one was open for 15% -> 14% of each run, Pallas kernels for 3% -> 3%
where the time goes in v2:
time: 1090 us; the launch traced here: 1080 us
  waiting for transfers between devices  620 us (57%)
  matrix products  140 us (13%)
  starting transfers between devices  90.1 us (8%)
  Pallas kernels  74.5 us (7%)
  local copies, waits for them, and re-layouts  67.2 us (6%)
  other arithmetic  59.1 us (5%)
  between operations  15.4 us (1%)
    ppermute x30, waiting for transfers between devices, shift(): return lax.ppermute(value, SHARD, pairs)  412 us
    dot_general x12, matrix products, contract(): lax.dot_general(left, right, (((left_dim,), (right_dim,)), ((), ())), pre...  140 us
    ppermute x9, waiting for transfers between devices, swap_chips(): return lax.ppermute(value, DP, [(d, d ^ 2 * mask) for d in range(lanes)])  74.4 us
    ppermute x30, starting transfers between devices, shift(): return lax.ppermute(value, SHARD, pairs)  71.1 us
    reduce_scatter x1, waiting for transfers between devices, on_device(): lax.psum_scatter(hidden_two_grad, DP, scatter_dimension=0, tiled=True)  68.2 us
    all_gather x1, waiting for transfers between devices, on_device(): branch_grad = lax.all_gather(middle_grad_low, DP, axis=0, tiled=True)  28.2 us
    pallas_call x2, Pallas kernels, spread_call(): pl.pallas_call(kernel, out_shape=tuple((jax.ShapeDtypeStruct((rows, w), F...  26.5 us
    pallas_call x1, Pallas kernels, attn_backward(): pl.pallas_call(functools.partial(attn_bwd_kernel, planes, rows // 2, head...  25 us
  transfers between devices with their start and end apart: 59, of which 30 were waited for; matrix products, arithmetic and copies ran while one was open for 14% of the time, Pallas kernels for 3%

profile of v2, /device:TPU:0, one launch (start us, length us, event | category | flops | bytes accessed | tf_op | source)
XLA Modules:
  0.0 1075.2 jit_solution(11758533502273584481)
XLA Ops:
  30.2 22.8 %collective-permute-done.4 = bf16[544,320]{1,0:T(8,128)(2,1)} collective-permute-done((bf16[544,320]{1,0:T(8,128)(2,1)S(1)}, bf16[544,320]{1,0:T(8,128)(2,1)}, u32[]{:S(2)}, u32[]{:S(2)}) %collective-permute-start.4) | collective-permute-done | bytes 348192 | tf_op jit(solution)/shard_map/ppermute | solution.py:29
  56.9 12.2 %all-gather.15.cloned.1.call-done = bf16[1,2048,2048]{1,2,0:T(8,128)(2,1)} async-done(((bf16[1,256,2048]{1,2,0:T(8,128)(2,1)}), bf16[1,2048,2048]{1,2,0:T(8,128)(2,1)}) %all-gather.15.cloned.1.call-update) | async-done | bytes 8388624 | tf_op jit(solution)/shard_map/all_gather | solution.py:445
  91.0 16.2 %collective-permute-done.7 = bf16[64,2048]{1,0:T(8,128)(2,1)} collective-permute-done((bf16[64,2048]{1,0:T(8,128)(2,1)S(1)}, bf16[64,2048]{1,0:T(8,128)(2,1)}, u32[]{:S(2)}, u32[]{:S(2)}) %collective-permute-start.7) | collective-permute-done | bytes 262176 | tf_op jit(solution)/shard_map/ppermute | solution.py:29
  113.8 12.3 %shard_map.203 = (bf16[256,2048]{1,0:T(8,128)(2,1)}, f32[8,2,512]{2,1,0:T(2,128)}) custom-call(s32[8,8]{1,0:T(8,128)} %add_convert_fusion.8.info_ref, bf16[256,2048]{1,0:T(8,128)(2,1)} %bitcast.149, bf16[4,64,2048]{2,1,0:T(8,128)(2,1)} %get-tuple-element.111.k_ref, bf16[4,64,2048]{2,1,0:T(8,128)(2,1)} %get-tuple-element.110.v_ref), custom_call_target="tpu_custom_call" | custom-call | flops 1207959552 | bytes 7340032 | tf_op jit(solution)/shard_map/pallas_call | solution.py:284
  148.9 24.5 %collective-permute-done.1 = bf16[512,384]{1,0:T(8,128)(2,1)S(1)} collective-permute-done((bf16[512,384]{1,0:T(8,128)(2,1)S(1)}, bf16[512,384]{1,0:T(8,128)(2,1)S(1)}, u32[]{:S(2)}, u32[]{:S(2)}) %collective-permute-start.1) | collective-permute-done | bytes 393248 | tf_op jit(solution)/shard_map/ppermute | solution.py:29
  207.5 100.2 %collective-permute-done.13 = bf16[176,2048]{1,0:T(8,128)(2,1)} collective-permute-done((bf16[176,2048]{1,0:T(8,128)(2,1)}, bf16[176,2048]{1,0:T(8,128)(2,1)}, u32[]{:S(2)}, u32[]{:S(2)}) %collective-permute-start.13) | collective-permute-done | bytes 720928 | tf_op jit(solution)/shard_map/ppermute | solution.py:29
  310.8 39.3 %collective-permute-done.14 = bf16[176,2048]{1,0:T(8,128)(2,1)} collective-permute-done((bf16[176,2048]{1,0:T(8,128)(2,1)}, bf16[176,2048]{1,0:T(8,128)(2,1)}, u32[]{:S(2)}, u32[]{:S(2)}) %collective-permute-start.14) | collective-permute-done | bytes 720928 | tf_op jit(solution)/shard_map/ppermute | solution.py:29
  352.2 30.1 %collective-permute-done.15 = bf16[176,2048]{1,0:T(8,128)(2,1)S(1)} collective-permute-done((bf16[176,2048]{1,0:T(8,128)(2,1)}, bf16[176,2048]{1,0:T(8,128)(2,1)S(1)}, u32[]{:S(2)}, u32[]{:S(2)}) %collective-permute-start.15) | collective-permute-done | bytes 720928 | tf_op jit(solution)/shard_map/ppermute | solution.py:29
  396.4 18.2 %fusion.24 = f32[1408,2048]{1,0:T(8,128)} fusion(bf16[2048,1408]{1,0:T(8,128)(2,1)} %constant_dynamic-update-slice_fusion.15, bf16[2048,2048]{1,0:T(8,128)(2,1)S(1)} %copy-done.1, f32[2048]{0:T(1024)S(1)} %bitcast.159, f32[2048]{0:T(1024)S(1)} %add_rsqrt_fusion), kind=kOutput, calls=%fused_computation.47 | convolution fusion | flops 11827937280 | bytes 25706496 | tf_op jit(solution)/shard_map/dot_general | solution.py:21
  414.6 15.1 %multiply_convert_fusion.1 = (bf16[704,2048]{1,0:T(8,128)(2,1)S(1)}, bf16[704,2048]{1,0:T(8,128)(2,1)S(1)}, bf16[704,2048]{1,0:T(8,128)(2,1)}) fusion(f32[1408,2048]{1,0:T(8,128)} %fusion.24, bf16[704,2048]{1,0:T(8,128)(2,1)} %constant_dynamic-update-slice_fusion.7, bf16[1,2048,2048]{2,1,0:T(8,128)(2,1)} %all-gather.17.cloned.1.call-done), kind=kOutput, calls=%fused_computation.24 | convolution fusion | flops 5927206912 | bytes 31457280 | tf_op jit(solution)/shard_map/dot_general | solution.py:21
  432.2 28.9 %convolution_convert_fusion.1 = bf16[2048,2048]{0,1:T(8,128)(2,1)} fusion(bf16[2048,1408]{1,0:T(8,128)(2,1)} %constant_dynamic-update-slice_fusion.15, bf16[704,2048]{1,0:T(8,128)(2,1)S(1)} %get-tuple-element.83, bf16[704,2048]{1,0:T(8,128)(2,1)S(1)} %get-tuple-element.82), kind=kOutput, calls=%fused_computation.18 | convolution fusion | flops 11826888704 | bytes 19922944 | tf_op jit(solution)/shard_map/dot_general | solution.py:21
  464.8 68.2 %reduce-scatter.4.cloned.1.call-done = bf16[256,2048]{0,1:T(8,128)(2,1)} async-done(((bf16[2048,2048]{0,1:T(8,128)(2,1)}), bf16[256,2048]{0,1:T(8,128)(2,1)}) %reduce-scatter.4.cloned.1.call-update) | async-done | bytes 1048592 | tf_op jit(solution)/shard_map/reduce_scatter | solution.py:560
  547.0 11.2 %collective-permute-done.18 = bf16[256,256]{1,0:T(8,128)(2,1)S(1)} collective-permute-done((bf16[256,256]{1,0:T(8,128)(2,1)S(1)}, bf16[256,256]{1,0:T(8,128)(2,1)S(1)}, u32[]{:S(2)}, u32[]{:S(2)}) %collective-permute-start.18) | collective-permute-done | bytes 131104 | tf_op jit(solution)/shard_map/ppermute | solution.py:542
  562.8 10.9 %convolution_convert_fusion.3 = bf16[2048,2048]{0,1:T(8,128)(2,1)} fusion(bf16[704,2048]{1,0:T(8,128)(2,1)S(1)} %copy-done.29, bf16[704,2048]{1,0:T(8,128)(2,1)} %constant_dynamic-update-slice_fusion.7), kind=kOutput, calls=%fused_computation.20 | convolution fusion | flops 5909774336 | bytes 14155776 | tf_op jit(solution)/shard_map/dot_general | solution.py:21
  573.7 28.2 %all-gather.13.cloned.1.call-done = bf16[2048,2048]{0,1:T(8,128)(2,1)} async-done(((bf16[256,2048]{0,1:T(8,128)(2,1)}), bf16[2048,2048]{0,1:T(8,128)(2,1)}) %all-gather.13.cloned.1.call-update) | async-done | bytes 8388624 | tf_op jit(solution)/shard_map/all_gather | solution.py:578
  608.6 25.0 %shard_map.204 = (f32[256,2048]{1,0:T(8,128)}, bf16[4,64,2048]{2,1,0:T(8,128)(2,1)}, bf16[4,64,2048]{2,1,0:T(8,128)(2,1)}) custom-call(s32[8,8]{1,0:T(8,128)} %add_convert_fusion.8.info_ref, bf16[256,2048]{1,0:T(8,128)(2,1)} %bitcast.150, bf16[4,64,2048]{2,1,0:T(8,128)(2,1)} %get-tuple-element.111.k_ref, bf16[4,64,2048]{2,1,0:T(8,128)(2,1)} %get-tuple-element.110.v_ref, ...), custom_call_target="tpu_custom_call" | custom-call | flops 3019898880 | bytes 7340032 | tf_op jit(solution)/shard_map/pallas_call | solution.py:304
  655.3 9.5 collective-permute-done.25
  666.2 9.3 fusion.3
  677.3 16.9 %convolution_convert_fusion.2 = bf16[2048,1408]{1,0:T(8,128)(2,1)S(1)} fusion(bf16[704,2048]{1,0:T(8,128)(2,1)} %copy-done.33, bf16[704,2048]{1,0:T(8,128)(2,1)S(1)} %copy-done.32, bf16[2048,2048]{1,0:T(8,128)(2,1)} %all-gather.11.cloned.1.call-done, f32[2048]{0:T(1024)S(1)} %bitcast.162, f32[2048]{0:T(1024)S(1)} %add_rsqrt_fusion), kind=kOutput, calls=%fused_computation.19 | convolution fusion | flops 11842355200 | bytes 19939328 | tf_op jit(solution)/shard_map/dot_general | solution.py:21
  706.2 78.2 %collective-permute-done.37 = bf16[96,1408]{1,0:T(8,128)(2,1)} collective-permute-done((bf16[96,1408]{1,0:T(8,128)(2,1)}, bf16[96,1408]{1,0:T(8,128)(2,1)}, u32[]{:S(2)}, u32[]{:S(2)}) %collective-permute-start.37) | collective-permute-done | bytes 270368 | tf_op jit(solution)/shard_map/ppermute | solution.py:29
  784.4 27.8 %collective-permute-start.38 = (bf16[96,1408]{1,0:T(8,128)(2,1)}, bf16[96,1408]{1,0:T(8,128)(2,1)}, u32[]{:S(2)}, u32[]{:S(2)}) collective-permute-start(bf16[96,1408]{1,0:T(8,128)(2,1)} %get-tuple-element.116), channel_id=1, source_target_pairs={{0,2},{1,3},{2,0},{3,1},{4,6},{5,7},{6,4},{7,5},{8,10},{9,11},{10,... | collective-permute-start | bytes 811016 | tf_op jit(solution)/shard_map/ppermute | solution.py:29
  812.2 12.2 %collective-permute-done.38 = bf16[96,1408]{1,0:T(8,128)(2,1)} collective-permute-done((bf16[96,1408]{1,0:T(8,128)(2,1)}, bf16[96,1408]{1,0:T(8,128)(2,1)}, u32[]{:S(2)}, u32[]{:S(2)}) %collective-permute-start.38) | collective-permute-done | bytes 270368 | tf_op jit(solution)/shard_map/ppermute | solution.py:29
  846.1 16.0 %collective-permute-done.41 = bf16[512,1408]{1,0:T(8,128)(2,1)S(1)} collective-permute-done((bf16[512,1408]{1,0:T(8,128)(2,1)S(1)}, bf16[512,1408]{1,0:T(8,128)(2,1)S(1)}, u32[]{:S(2)}, u32[]{:S(2)}) %collective-permute-start.41) | collective-permute-done | bytes 1441824 | tf_op jit(solution)/shard_map/ppermute | solution.py:39
  863.6 29.7 %collective-permute-done.42 = bf16[512,1408]{1,0:T(8,128)(2,1)S(1)} collective-permute-done((bf16[512,1408]{1,0:T(8,128)(2,1)S(1)}, bf16[512,1408]{1,0:T(8,128)(2,1)S(1)}, u32[]{:S(2)}, u32[]{:S(2)}) %collective-permute-start.42) | collective-permute-done | bytes 1441824 | tf_op jit(solution)/shard_map/ppermute | solution.py:39
  925.7 13.0 %collective-permute-done.27 = bf16[544,576]{1,0:T(8,128)(2,1)} collective-permute-done((bf16[544,576]{1,0:T(8,128)(2,1)}, bf16[544,576]{1,0:T(8,128)(2,1)}, u32[]{:S(2)}, u32[]{:S(2)}) %collective-permute-start.27) | collective-permute-done | bytes 626720 | tf_op jit(solution)/shard_map/ppermute | solution.py:29
  939.2 14.6 %collective-permute-done.29 = bf16[544,576]{1,0:T(8,128)(2,1)} collective-permute-done((bf16[544,576]{1,0:T(8,128)(2,1)}, bf16[544,576]{1,0:T(8,128)(2,1)}, u32[]{:S(2)}, u32[]{:S(2)}) %collective-permute-start.29) | collective-permute-done | bytes 626720 | tf_op jit(solution)/shard_map/ppermute | solution.py:29
  955.3 25.1 %collective-permute-done.28 = bf16[544,576]{1,0:T(8,128)(2,1)} collective-permute-done((bf16[544,576]{1,0:T(8,128)(2,1)}, bf16[544,576]{1,0:T(8,128)(2,1)}, u32[]{:S(2)}, u32[]{:S(2)}) %collective-permute-start.28) | collective-permute-done | bytes 626720 | tf_op jit(solution)/shard_map/ppermute | solution.py:29
  987.9 13.9 %collective-permute-done.32 = bf16[544,576]{1,0:T(8,128)(2,1)S(1)} collective-permute-done((bf16[544,576]{1,0:T(8,128)(2,1)S(1)}, bf16[544,576]{1,0:T(8,128)(2,1)S(1)}, u32[]{:S(2)}, u32[]{:S(2)}) %collective-permute-start.32) | collective-permute-done | bytes 626720 | tf_op jit(solution)/shard_map/ppermute | solution.py:39
  1001.8 13.3 %collective-permute-done.31 = bf16[544,576]{1,0:T(8,128)(2,1)S(1)} collective-permute-done((bf16[544,576]{1,0:T(8,128)(2,1)S(1)}, bf16[544,576]{1,0:T(8,128)(2,1)S(1)}, u32[]{:S(2)}, u32[]{:S(2)}) %collective-permute-start.31) | collective-permute-done | bytes 626720 | tf_op jit(solution)/shard_map/ppermute | solution.py:39
  1018.8 10.6 shard_map.207
  1029.5 14.4 %shard_map.206 = (f32[512,5632]{1,0:T(8,128)}, f32[512,5632]{1,0:T(8,128)}) custom-call(s32[1]{0:T(128)} %bitcast.41.lane_ref, bf16[4,512,1408]{2,1,0:T(8,128)(2,1)} %pad_maximum_fusion.1.mine_ref, bf16[4,512,1408]{2,1,0:T(8,128)(2,1)} %collective-permute-done.43.other_ref), custom_call_target="tpu_custom_call" | custom-call | bytes 34603008 | tf_op jit(solution)/shard_map/pallas_call | solution.py:374
  1045.5 12.1 %shard_map.205 = (f32[512,2048]{1,0:T(8,128)}, f32[512,256]{1,0:T(8,128)}, f32[512,256]{1,0:T(8,128)}, f32[512,2048]{1,0:T(8,128)}) custom-call(s32[1]{0:T(128)} %bitcast.41.lane_ref, bf16[4,544,576]{2,1,0:T(8,128)(2,1)} %pad_maximum_fusion.5.mine_ref, bf16[4,544,576]{2,1,0:T(8,128)(2,1)} %collective-permute-done.33.other_ref), custom_call_target="tpu_custom_call" | custom-call | bytes 14155776 | tf_op jit(solution)/shard_map/pallas_call | solution.py:374
  (315 shorter events, 279.7 us)
Async XLA Ops:
  7.2 61.9 %all-gather.15.cloned.1.call-start = ((), (), s32[]{:S(2)}) async-start(), calls=%async_computation.9 | async-start | bytes 9437184 | tf_op jit(solution)/shard_map/all_gather | solution.py:445
  9.5 170.4 %all-gather.9.cloned.1.call-start = ((), (), s32[]{:S(2)}) async-start(), calls=%async_computation.3 | async-start | bytes 9437184 | tf_op jit(solution)/shard_map/all_gather | solution.py:534
  17.3 35.8 %collective-permute-start.4 = (bf16[544,320]{1,0:T(8,128)(2,1)S(1)}, bf16[544,320]{1,0:T(8,128)(2,1)}, u32[]{:S(2)}, u32[]{:S(2)}) collective-permute-start(bf16[544,320]{1,0:T(8,128)(2,1)S(1)} %fusion.49), channel_id=1, source_target_pairs={{0,2},{1,3},{2,0},{3,1},{4,6},{5,7},{6,4},{7,5},{8,10},{9,11},{10,... | collective-permute-start | bytes 1044488 | tf_op jit(solution)/shard_map/ppermute | solution.py:29
  17.3 36.5 %collective-permute-start.3 = (bf16[544,320]{1,0:T(8,128)(2,1)S(1)}, bf16[544,320]{1,0:T(8,128)(2,1)}, u32[]{:S(2)}, u32[]{:S(2)}) collective-permute-start(bf16[544,320]{1,0:T(8,128)(2,1)S(1)} %fusion.49), channel_id=1, source_target_pairs={{0,1},{1,2},{2,3},{3,0},{4,5},{5,6},{6,7},{7,4},{8,9},{9,10},{10,1... | collective-permute-start | bytes 1044488 | tf_op jit(solution)/shard_map/ppermute | solution.py:29
  126.2 264.5 %all-gather.11.cloned.1.call-start = ((), (), s32[]{:S(2)}) async-start(), calls=%async_computation.4 | async-start | bytes 9437184 | tf_op jit(solution)/shard_map/all_gather | solution.py:545
  135.7 37.7 %collective-permute-start.2 = (bf16[512,384]{1,0:T(8,128)(2,1)S(1)}, bf16[512,384]{1,0:T(8,128)(2,1)S(1)}, u32[]{:S(2)}, u32[]{:S(2)}) collective-permute-start(bf16[512,384]{1,0:T(8,128)(2,1)S(1)} %pad_maximum_fusion.13), channel_id=1, source_target_pairs={{0,3},{1,0},{2,1},{3,2},{4,7},{5,4},{6,5},{7,6},{8,11},{9,8},{10,9... | collective-permute-start | bytes 1179656 | tf_op jit(solution)/shard_map/ppermute | solution.py:29
  186.9 227.7 %all-gather.17.cloned.1.call-start = ((), (), s32[]{:S(2)}) async-start(), calls=%async_computation.10 | async-start | bytes 9437184 | tf_op jit(solution)/shard_map/all_gather | solution.py:446
  187.5 345.4 %reduce-scatter.4.cloned.1.call-start = ((), (), s32[]{:S(2)}) async-start(), calls=%async_computation.5 | async-start | bytes 9437184 | tf_op jit(solution)/shard_map/reduce_scatter | solution.py:560
  187.5 200.6 %collective-permute-start.12 = (bf16[512,1280]{1,0:T(8,128)(2,1)S(1)}, bf16[512,1280]{1,0:T(8,128)(2,1)}, u32[]{:S(2)}, u32[]{:S(2)}) collective-permute-start(bf16[512,1280]{1,0:T(8,128)(2,1)S(1)} %slice.195), channel_id=1, source_target_pairs={{0,3},{1,0},{2,1},{3,2},{4,7},{5,4},{6,5},{7,6},{8,11},{9,8},{10,9... | collective-permute-start | bytes 3932168 | tf_op jit(solution)/shard_map/ppermute | solution.py:29
  190.9 194.8 %collective-permute-start.11 = (bf16[512,1280]{1,0:T(8,128)(2,1)S(1)}, bf16[512,1280]{1,0:T(8,128)(2,1)}, u32[]{:S(2)}, u32[]{:S(2)}) collective-permute-start(bf16[512,1280]{1,0:T(8,128)(2,1)S(1)} %slice.195), channel_id=1, source_target_pairs={{0,2},{1,3},{2,0},{3,1},{4,6},{5,7},{6,4},{7,5},{8,10},{9,11},{10,... | collective-permute-start | bytes 3932168 | tf_op jit(solution)/shard_map/ppermute | solution.py:29
  190.9 192.3 %collective-permute-start.10 = (bf16[512,1280]{1,0:T(8,128)(2,1)S(1)}, bf16[512,1280]{1,0:T(8,128)(2,1)}, u32[]{:S(2)}, u32[]{:S(2)}) collective-permute-start(bf16[512,1280]{1,0:T(8,128)(2,1)S(1)} %slice.195), channel_id=1, source_target_pairs={{0,1},{1,2},{2,3},{3,0},{4,5},{5,6},{6,7},{7,4},{8,9},{9,10},{10,1... | collective-permute-start | bytes 3932168 | tf_op jit(solution)/shard_map/ppermute | solution.py:29
  196.8 153.4 %collective-permute-start.14 = (bf16[176,2048]{1,0:T(8,128)(2,1)}, bf16[176,2048]{1,0:T(8,128)(2,1)}, u32[]{:S(2)}, u32[]{:S(2)}) collective-permute-start(bf16[176,2048]{1,0:T(8,128)(2,1)} %get-tuple-element.77), channel_id=1, source_target_pairs={{0,2},{1,3},{2,0},{3,1},{4,6},{5,7},{6,4},{7,5},{8,10},{9,11},{10,... | collective-permute-start | bytes 2162696 | tf_op jit(solution)/shard_map/ppermute | solution.py:29
  198.6 109.1 %collective-permute-start.13 = (bf16[176,2048]{1,0:T(8,128)(2,1)}, bf16[176,2048]{1,0:T(8,128)(2,1)}, u32[]{:S(2)}, u32[]{:S(2)}) collective-permute-start(bf16[176,2048]{1,0:T(8,128)(2,1)} %get-tuple-element.77), channel_id=1, source_target_pairs={{0,1},{1,2},{2,3},{3,0},{4,5},{5,6},{6,7},{7,4},{8,9},{9,10},{10,1... | collective-permute-start | bytes 2162696 | tf_op jit(solution)/shard_map/ppermute | solution.py:29
  307.7 74.7 %collective-permute-start.15 = (bf16[176,2048]{1,0:T(8,128)(2,1)}, bf16[176,2048]{1,0:T(8,128)(2,1)S(1)}, u32[]{:S(2)}, u32[]{:S(2)}) collective-permute-start(bf16[176,2048]{1,0:T(8,128)(2,1)} %get-tuple-element.77), channel_id=1, source_target_pairs={{0,3},{1,0},{2,1},{3,2},{4,7},{5,4},{6,5},{7,6},{8,11},{9,8},{10,9... | collective-permute-start | bytes 2162696 | tf_op jit(solution)/shard_map/ppermute | solution.py:29
  461.1 140.8 %all-gather.13.cloned.1.call-start = ((), (), s32[]{:S(2)}) async-start(), calls=%async_computation.6 | async-start | bytes 9437184 | tf_op jit(solution)/shard_map/all_gather | solution.py:578
  538.7 519.5 %reduce-scatter.8.cloned.1.call-start = ((), (), s32[]{:S(2)}) async-start(), calls=%async_computation.8 | async-start | bytes 9437184 | tf_op jit(solution)/shard_map/reduce_scatter | solution.py:602
  675.5 384.4 %reduce-scatter.6.cloned.1.call-start = ((), (), s32[]{:S(2)}) async-start(), calls=%async_computation.7 | async-start | bytes 9437184 | tf_op jit(solution)/shard_map/reduce_scatter | solution.py:581
  697.6 128.1 %collective-permute-start.34 = (bf16[416,1408]{1,0:T(8,128)(2,1)}, bf16[416,1408]{1,0:T(8,128)(2,1)S(1)}, u32[]{:S(2)}, u32[]{:S(2)}) collective-permute-start(bf16[416,1408]{1,0:T(8,128)(2,1)} %get-tuple-element.95), channel_id=1, source_target_pairs={{0,1},{1,2},{2,3},{3,0},{4,5},{5,6},{6,7},{7,4},{8,9},{9,10},{10,1... | collective-permute-start | bytes 3514376 | tf_op jit(solution)/shard_map/ppermute | solution.py:29
  697.6 128.1 %collective-permute-start.36 = (bf16[416,1408]{1,0:T(8,128)(2,1)}, bf16[416,1408]{1,0:T(8,128)(2,1)}, u32[]{:S(2)}, u32[]{:S(2)}) collective-permute-start(bf16[416,1408]{1,0:T(8,128)(2,1)} %get-tuple-element.96), channel_id=1, source_target_pairs={{0,3},{1,0},{2,1},{3,2},{4,7},{5,4},{6,5},{7,6},{8,11},{9,8},{10,9... | collective-permute-start | bytes 3514376 | tf_op jit(solution)/shard_map/ppermute | solution.py:29
  701.4 124.3 %collective-permute-start.35 = (bf16[416,1408]{1,0:T(8,128)(2,1)S(1)}, bf16[416,1408]{1,0:T(8,128)(2,1)}, u32[]{:S(2)}, u32[]{:S(2)}) collective-permute-start(bf16[416,1408]{1,0:T(8,128)(2,1)S(1)} %get-tuple-element.97), channel_id=1, source_target_pairs={{0,2},{1,3},{2,0},{3,1},{4,6},{5,7},{6,4},{7,5},{8,10},{9,11},{10,... | collective-permute-start | bytes 3514376 | tf_op jit(solution)/shard_map/ppermute | solution.py:29
  702.3 82.1 %collective-permute-start.37 = (bf16[96,1408]{1,0:T(8,128)(2,1)}, bf16[96,1408]{1,0:T(8,128)(2,1)}, u32[]{:S(2)}, u32[]{:S(2)}) collective-permute-start(bf16[96,1408]{1,0:T(8,128)(2,1)} %get-tuple-element.114), channel_id=1, source_target_pairs={{0,1},{1,2},{2,3},{3,0},{4,5},{5,6},{6,7},{7,4},{8,9},{9,10},{10,1... | collective-permute-start | bytes 811016 | tf_op jit(solution)/shard_map/ppermute | solution.py:29
  703.7 108.4 %collective-permute-start.39 = (bf16[96,1408]{1,0:T(8,128)(2,1)}, bf16[96,1408]{1,0:T(8,128)(2,1)}, u32[]{:S(2)}, u32[]{:S(2)}) collective-permute-start(bf16[96,1408]{1,0:T(8,128)(2,1)} %get-tuple-element.115), channel_id=1, source_target_pairs={{0,3},{1,0},{2,1},{3,2},{4,7},{5,4},{6,5},{7,6},{8,11},{9,8},{10,9... | collective-permute-start | bytes 811016 | tf_op jit(solution)/shard_map/ppermute | solution.py:29
  784.4 40.0 %collective-permute-start.38 = (bf16[96,1408]{1,0:T(8,128)(2,1)}, bf16[96,1408]{1,0:T(8,128)(2,1)}, u32[]{:S(2)}, u32[]{:S(2)}) collective-permute-start(bf16[96,1408]{1,0:T(8,128)(2,1)} %get-tuple-element.116), channel_id=1, source_target_pairs={{0,2},{1,3},{2,0},{3,1},{4,6},{5,7},{6,4},{7,5},{8,10},{9,11},{10,... | collective-permute-start | bytes 811016 | tf_op jit(solution)/shard_map/ppermute | solution.py:29
  830.6 62.7 %collective-permute-start.42 = (bf16[512,1408]{1,0:T(8,128)(2,1)S(1)}, bf16[512,1408]{1,0:T(8,128)(2,1)S(1)}, u32[]{:S(2)}, u32[]{:S(2)}) collective-permute-start(bf16[512,1408]{1,0:T(8,128)(2,1)S(1)} %get-tuple-element.113), channel_id=1, source_target_pairs={{0,24},{4,28},{8,16},{12,20},{16,8},{20,12},{24,0},{28,4},{1,25},{... | collective-permute-start | bytes 4325384 | tf_op jit(solution)/shard_map/ppermute | solution.py:39
  842.2 75.8 %collective-permute-start.44 = (bf16[176,2048]{1,0:T(8,128)(2,1)}, bf16[176,2048]{1,0:T(8,128)(2,1)}, u32[]{:S(2)}, u32[]{:S(2)}) collective-permute-start(bf16[176,2048]{1,0:T(8,128)(2,1)} %get-tuple-element.98), channel_id=1, source_target_pairs={{0,1},{1,2},{2,3},{3,0},{4,5},{5,6},{6,7},{7,4},{8,9},{9,10},{10,1... | collective-permute-start | bytes 2162696 | tf_op jit(solution)/shard_map/ppermute | solution.py:29
  842.2 79.6 %collective-permute-start.46 = (bf16[176,2048]{1,0:T(8,128)(2,1)}, bf16[176,2048]{1,0:T(8,128)(2,1)}, u32[]{:S(2)}, u32[]{:S(2)}) collective-permute-start(bf16[176,2048]{1,0:T(8,128)(2,1)} %get-tuple-element.99), channel_id=1, source_target_pairs={{0,3},{1,0},{2,1},{3,2},{4,7},{5,4},{6,5},{7,6},{8,11},{9,8},{10,9... | collective-permute-start | bytes 2162696 | tf_op jit(solution)/shard_map/ppermute | solution.py:29
  862.1 59.8 %collective-permute-start.45 = (bf16[176,2048]{1,0:T(8,128)(2,1)}, bf16[176,2048]{1,0:T(8,128)(2,1)}, u32[]{:S(2)}, u32[]{:S(2)}) collective-permute-start(bf16[176,2048]{1,0:T(8,128)(2,1)} %get-tuple-element.100), channel_id=1, source_target_pairs={{0,2},{1,3},{2,0},{3,1},{4,6},{5,7},{6,4},{7,5},{8,10},{9,11},{10,... | collective-permute-start | bytes 2162696 | tf_op jit(solution)/shard_map/ppermute | solution.py:29
  896.8 132.6 %collective-permute-start.43 = (bf16[4,512,1408]{2,1,0:T(8,128)(2,1)}, bf16[4,512,1408]{2,1,0:T(8,128)(2,1)}, u32[]{:S(2)}, u32[]{:S(2)}) collective-permute-start(bf16[4,512,1408]{2,1,0:T(8,128)(2,1)} %pad_maximum_fusion.1.mine_ref), channel_id=1, source_target_pairs={{0,4},{4,0},{8,12},{12,8},{16,20},{20,16},{24,28},{28,24},{1,5},{5... | collective-permute-start | bytes 17301512 | tf_op jit(solution)/shard_map/ppermute | solution.py:34
  918.0 35.8 %collective-permute-start.29 = (bf16[544,576]{1,0:T(8,128)(2,1)}, bf16[544,576]{1,0:T(8,128)(2,1)}, u32[]{:S(2)}, u32[]{:S(2)}) collective-permute-start(bf16[544,576]{1,0:T(8,128)(2,1)} %get-tuple-element.102), channel_id=1, source_target_pairs={{0,3},{1,0},{2,1},{3,2},{4,7},{5,4},{6,5},{7,6},{8,11},{9,8},{10,9... | collective-permute-start | bytes 1880072 | tf_op jit(solution)/shard_map/ppermute | solution.py:29
  921.8 58.6 %collective-permute-start.28 = (bf16[544,576]{1,0:T(8,128)(2,1)}, bf16[544,576]{1,0:T(8,128)(2,1)}, u32[]{:S(2)}, u32[]{:S(2)}) collective-permute-start(bf16[544,576]{1,0:T(8,128)(2,1)} %get-tuple-element.103), channel_id=1, source_target_pairs={{0,2},{1,3},{2,0},{3,1},{4,6},{5,7},{6,4},{7,5},{8,10},{9,11},{10,... | collective-permute-start | bytes 1880072 | tf_op jit(solution)/shard_map/ppermute | solution.py:29
  924.1 59.8 %collective-permute-start.49 = (bf16[176,2048]{1,0:T(8,128)(2,1)S(1)}, bf16[176,2048]{1,0:T(8,128)(2,1)}, u32[]{:S(2)}, u32[]{:S(2)}) collective-permute-start(bf16[176,2048]{1,0:T(8,128)(2,1)S(1)} %add_convert_fusion.2), channel_id=1, source_target_pairs={{0,24},{4,28},{8,16},{12,20},{16,8},{20,12},{24,0},{28,4},{1,25},{... | collective-permute-start | bytes 2162696 | tf_op jit(solution)/shard_map/ppermute | solution.py:39
  938.7 46.7 %collective-permute-start.48 = (bf16[176,2048]{1,0:T(8,128)(2,1)S(1)}, bf16[176,2048]{1,0:T(8,128)(2,1)}, u32[]{:S(2)}, u32[]{:S(2)}) collective-permute-start(bf16[176,2048]{1,0:T(8,128)(2,1)S(1)} %add_convert_fusion.2), channel_id=1, source_target_pairs={{0,16},{4,20},{8,24},{12,28},{16,0},{20,4},{24,8},{28,12},{1,17},{... | collective-permute-start | bytes 2162696 | tf_op jit(solution)/shard_map/ppermute | solution.py:39
  (61 other events, 995.3 us)
Sparse Core Ops, SparseCore 0:
  10.5 58.5 all-gather.14
  126.3 53.6 all-gather.8
  187.0 54.2 all-gather.10
  243.1 54.2 all-gather.16
  461.2 71.6 reduce-scatter.3
  538.8 63.0 all-gather.12
  675.6 70.5 reduce-scatter.7
  749.7 71.2 reduce-scatter.5

commit v3 on v2

--- a/solution.py
+++ b/solution.py
@@ -36,7 +36,8 @@
 
 def swap_chips(value, mask):
     lanes = lax.axis_size(DP)
-    return lax.ppermute(value, DP, [(d, d ^ (2 * mask)) for d in range(lanes)])
+    pairs = [(d, d ^ (2 * mask)) for d in range(lanes)]
+    return lax.ppermute(value, DP, pairs)
 
 
 def plane_parts(value):
@@ -44,15 +45,39 @@
     return [value] + [shift(value, k) for k in range(1, count)]
 
 
-def assemble(parts, axis=0):
+def placed(parts):
     count = lax.axis_size(SHARD)
     rank = lax.axis_index(SHARD)
-    rows = parts[0].shape[axis]
-    shape = list(parts[0].shape)
+    return [(part, lax.rem(rank - k + count, count)) for k, part in enumerate(parts)]
+
+
+def forwarded(value):
+    count = lax.axis_size(SHARD)
+    rank = lax.axis_index(SHARD)
+    if count != 4:
+        return placed(plane_parts(value))
+    across = shift(value, 2)
+    up = lax.ppermute(value, SHARD, [(0, 1), (1, 2), (2, 3)])
+    down = lax.ppermute(value, SHARD, [(1, 0), (2, 1), (3, 2)])
+    far = lax.ppermute(across, SHARD, [(2, 3), (1, 0)])
+    edge = (rank == 0) | (rank == 3)
+    far_place = jnp.where(edge, 3 - rank, rank)
+    return [
+        (value, rank),
+        (up, lax.rem(rank + 3, 4)),
+        (down, lax.rem(rank + 1, 4)),
+        (across, lax.rem(rank + 2, 4)),
+        (jnp.where(edge, far, value), far_place),
+    ]
+
+
+def assemble(pieces, axis=0):
+    count = lax.axis_size(SHARD)
+    rows = pieces[0][0].shape[axis]
+    shape = list(pieces[0][0].shape)
     shape[axis] = rows * count
-    whole = jnp.zeros(shape, parts[0].dtype)
-    for k, part in enumerate(parts):
-        place = lax.rem(rank - k + count, count)
+    whole = jnp.zeros(shape, pieces[0][0].dtype)
+    for part, place in pieces:
         whole = lax.dynamic_update_slice_in_dim(whole, part, place * rows, axis)
     return whole
 
@@ -464,14 +489,12 @@
     gain_rows = gain_rows.reshape(2 * gain_reps, qkv_cols)
     gain_rows = jnp.pad(gain_rows, ((0, EXTRA - 2 * gain_reps), (0, 0)))
     qkv_parts = plane_parts(jnp.concatenate([qkv_piece, gain_rows], axis=0))
-    qkv_mat = assemble([part[:own_width] for part in qkv_parts])
-    gains = assemble(
-        [
-            part[own_width : own_width + 2 * gain_reps].reshape(2, -1)[:, :own_width]
-            for part in qkv_parts
-        ],
-        1,
-    )
+    qkv_mat = assemble(placed([part[:own_width] for part in qkv_parts]))
+    gain_parts = [
+        part[own_width : own_width + 2 * gain_reps].reshape(2, -1)[:, :own_width]
+        for part in qkv_parts
+    ]
+    gains = assemble(placed(gain_parts), 1)
     gain_one, gain_two = gains[0].astype(FULL), gains[1].astype(FULL)
 
     mlp_piece = jnp.concatenate(
@@ -489,16 +512,17 @@
     second_piece = mlp_piece[:, cut:]
     first_piece, second_piece = lax.optimization_barrier((first_piece, second_piece))
     first_parts = plane_parts(first_piece)
-    second_parts = plane_parts(second_piece)
-    out_mat = assemble([part[:, :out_cols] for part in first_parts])
+    second_pieces = forwarded(second_piece)
+    out_mat = assemble(placed([part[:, :out_cols] for part in first_parts]))
     mlp_mat = jnp.zeros((width, 2 * own_ff), LOW)
-    for parts, start, place in ((first_parts, out_cols, 0), (second_parts, 0, cut)):
-        for k, part in enumerate(parts):
-            row = lax.rem(plane - k + planes, planes) * own_width
-            mlp_mat = lax.dynamic_update_slice(mlp_mat, part[:, start:], (row, place))
+    for part, place in placed([part[:, out_cols:] for part in first_parts]):
+        mlp_mat = lax.dynamic_update_slice(mlp_mat, part, (place * own_width, 0))
+    for part, place in second_pieces[:-1]:
+        mlp_mat = lax.dynamic_update_slice(mlp_mat, part, (place * own_width, cut))
+    part, place = second_pieces[-1]
+    mlp_mat = lax.dynamic_update_slice(mlp_mat, part, (place * own_width, cut))
     down_piece = lax.dynamic_slice_in_dim(w_down, lane * unit, unit, 0).astype(LOW)
-    down_parts = plane_parts(down_piece)
-    down_mat = assemble(down_parts)
+    down_mat = assemble(forwarded(down_piece))
 
     grouped = table.reshape(seqs, planes, 2)
     order = lax.rem(plane - jnp.arange(planes, dtype=jnp.int32) + planes, planes)
@@ -611,14 +635,17 @@
     branch_cols = lax.dynamic_slice_in_dim(branch_grad, lane * out_cols, out_cols, 1)
     qkv_grad = contract(hidden_one, qkv_lin, 0, 1).astype(LOW)
     out_grad = contract(attended_all, branch_cols, 1, 0).astype(LOW)
-    piece_cols = qkv_cols + out_cols
     out_grad = lax.optimization_barrier(out_grad)
     attn_grad = jnp.concatenate([qkv_grad, out_grad], axis=1).reshape(planes, own_width, -1)
-    gain_grads = jnp.stack([gain_one_grad, gain_two_grad]).astype(LOW)
+    attn_grad = jnp.pad(attn_grad, ((0, 0), (0, 16), (0, 0)))
+    attn_sent = plane_send(attn_grad.reshape(planes * (own_width + 16), -1))
+    gain_grads = jnp.stack([gain_one_grad, gain_two_grad])
     gain_grads = jnp.transpose(gain_grads.reshape(2, planes, own_width), (1, 0, 2))
-    gain_grads = jnp.pad(gain_grads, ((0, 0), (0, EXTRA - 2), (0, piece_cols - own_width)))
-    attn_grad = jnp.concatenate([attn_grad, gain_grads], axis=1)
-    attn_sent = plane_send(attn_grad.reshape(-1, piece_cols))
+    gain_sent = plane_send(gain_grads.reshape(2 * planes, own_width))
+    gain_own = sum(gain_sent[1:], gain_sent[0])
+    gain_stack = chip_stack(gain_own)
+    gain_own = sum(gain_stack[1:], gain_stack[0])
+    gain_own = gain_own + swap_cores(gain_own)
 
     down_sum = plane_sum(down_sent)
     down_mine = jnp.stack(chip_stack(down_sum), axis=0)
@@ -655,10 +682,6 @@
         EXTRA,
         (lanes * head_cols, kv_heads * HEAD_DIM, kv_heads * HEAD_DIM, lanes * out_cols),
     )
-    gain_at = slice(own_width, own_width + 2)
-    gain_own = jnp.sum(attn_mine[:, gain_at, :own_width].astype(FULL), axis=0) + jnp.sum(
-        attn_other[:, gain_at, :own_width].astype(FULL), axis=0
-    )
     return (
         block_out,
         tokens_grad,

time: 1090 us -> 1070 us (0.982)
  waiting for transfers between devices: 620 us -> 593 us
  matrix products: 140 us -> 121 us
  starting transfers between devices: 90.1 us -> 109 us
    ppermute x30 -> x29, waiting for transfers between devices: 412 us -> 287 us  [shift(): return lax.ppermute(value, SHARD, pairs)]
    ppermute x9 -> x18, waiting for transfers between devices: 74.4 us -> 172 us  [the longest x12 75.2 us: swap_chips(): return lax.ppermute(value, DP, pairs)]
    ppermute x9 -> x18, starting transfers between devices: 10.7 us -> 31.1 us  [the longest x12 17.2 us: swap_chips(): return lax.ppermute(value, DP, pairs)]
    dot_general x12, matrix products: 140 us -> 121 us  [contract(): lax.dot_general(left, right, (((left_dim,), (right_dim,)), ((), ())), pre...]
    ppermute x30 -> x29, starting transfers between devices: 71.1 us -> 69.8 us  [shift(): return lax.ppermute(value, SHARD, pairs)]
  transfers between devices with their start and end apart: 59 -> 68, of which waited for: 30 -> 36; matrix products, arithmetic and copies ran while one was open for 14% -> 15% of each run, Pallas kernels for 3% -> 4%
where the time goes in v3:
time: 1070 us; the launch traced here: 1060 us
  waiting for transfers between devices  593 us (55%)
  matrix products  121 us (11%)
  starting transfers between devices  109 us (10%)
  local copies, waits for them, and re-layouts  76.1 us (7%)
  Pallas kernels  74.8 us (7%)
  other arithmetic  58.1 us (5%)
  between operations  15.8 us (1%)
    ppermute x29, waiting for transfers between devices, shift(): return lax.ppermute(value, SHARD, pairs)  287 us
    dot_general x12, matrix products, contract(): lax.dot_general(left, right, (((left_dim,), (right_dim,)), ((), ())), pre...  121 us
    ppermute x12, waiting for transfers between devices, swap_chips(): return lax.ppermute(value, DP, pairs)  75.2 us
    ppermute x29, starting transfers between devices, shift(): return lax.ppermute(value, SHARD, pairs)  69.8 us
    reduce_scatter x1, waiting for transfers between devices, on_device(): lax.psum_scatter(hidden_two_grad, DP, scatter_dimension=0, tiled=True)  67.9 us
    ppermute x2, waiting for transfers between devices, forwarded(): far = lax.ppermute(across, SHARD, [(2, 3), (1, 0)])  61.8 us
    all_gather x1, waiting for transfers between devices, on_device(): branch_grad = lax.all_gather(middle_grad_low, DP, axis=0, tiled=True)  28.1 us
    pallas_call x2, Pallas kernels, spread_call(): pl.pallas_call(kernel, out_shape=tuple((jax.ShapeDtypeStruct((rows, w), F...  26.5 us
  transfers between devices with their start and end apart: 68, of which 36 were waited for; matrix products, arithmetic and copies ran while one was open for 15% of the time, Pallas kernels for 4%

profile of v3, /device:TPU:0, one launch (start us, length us, event | category | flops | bytes accessed | tf_op | source)
XLA Modules:
  0.0 1057.2 jit_solution(1665561287747743631)
XLA Ops:
  30.2 22.8 %collective-permute-done.4 = bf16[544,320]{1,0:T(8,128)(2,1)} collective-permute-done((bf16[544,320]{1,0:T(8,128)(2,1)S(1)}, bf16[544,320]{1,0:T(8,128)(2,1)}, u32[]{:S(2)}, u32[]{:S(2)}) %collective-permute-start.4) | collective-permute-done | bytes 348192 | tf_op jit(solution)/shard_map/ppermute | solution.py:29
  56.9 12.2 %all-gather.15.cloned.1.call-done = bf16[1,2048,2048]{1,2,0:T(8,128)(2,1)} async-done(((bf16[1,256,2048]{1,2,0:T(8,128)(2,1)}), bf16[1,2048,2048]{1,2,0:T(8,128)(2,1)}) %all-gather.15.cloned.1.call-update) | async-done | bytes 8388624 | tf_op jit(solution)/shard_map/all_gather | solution.py:470
  91.0 16.2 %collective-permute-done.7 = bf16[64,2048]{1,0:T(8,128)(2,1)} collective-permute-done((bf16[64,2048]{1,0:T(8,128)(2,1)S(1)}, bf16[64,2048]{1,0:T(8,128)(2,1)}, u32[]{:S(2)}, u32[]{:S(2)}) %collective-permute-start.7) | collective-permute-done | bytes 262176 | tf_op jit(solution)/shard_map/ppermute | solution.py:29
  113.8 12.4 %shard_map.203 = (bf16[256,2048]{1,0:T(8,128)(2,1)}, f32[8,2,512]{2,1,0:T(2,128)}) custom-call(s32[8,8]{1,0:T(8,128)} %add_convert_fusion.8.info_ref, bf16[256,2048]{1,0:T(8,128)(2,1)} %bitcast.155, bf16[4,64,2048]{2,1,0:T(8,128)(2,1)} %get-tuple-element.111.k_ref, bf16[4,64,2048]{2,1,0:T(8,128)(2,1)} %get-tuple-element.110.v_ref), custom_call_target="tpu_custom_call" | custom-call | flops 1207959552 | bytes 7340032 | tf_op jit(solution)/shard_map/pallas_call | solution.py:309
  149.1 24.5 %collective-permute-done.1 = bf16[512,384]{1,0:T(8,128)(2,1)S(1)} collective-permute-done((bf16[512,384]{1,0:T(8,128)(2,1)S(1)}, bf16[512,384]{1,0:T(8,128)(2,1)S(1)}, u32[]{:S(2)}, u32[]{:S(2)}) %collective-permute-start.1) | collective-permute-done | bytes 393248 | tf_op jit(solution)/shard_map/ppermute | solution.py:29
  212.5 42.9 %collective-permute-done.16 = bf16[176,2048]{1,0:T(8,128)(2,1)} collective-permute-done((bf16[176,2048]{1,0:T(8,128)(2,1)S(1)}, bf16[176,2048]{1,0:T(8,128)(2,1)}, u32[]{:S(2)}, u32[]{:S(2)}) %collective-permute-start.16) | collective-permute-done | bytes 720928 | tf_op jit(solution)/shard_map/ppermute | solution.py:29
  259.4 22.3 %collective-permute-done.14 = bf16[176,2048]{1,0:T(8,128)(2,1)} collective-permute-done((bf16[176,2048]{1,0:T(8,128)(2,1)S(1)}, bf16[176,2048]{1,0:T(8,128)(2,1)}, u32[]{:S(2)}, u32[]{:S(2)}) %collective-permute-start.14) | collective-permute-done | bytes 720928 | tf_op jit(solution)/shard_map/ppermute | solution.py:60
  285.1 13.0 %collective-permute-done.15 = bf16[176,2048]{1,0:T(8,128)(2,1)S(1)} collective-permute-done((bf16[176,2048]{1,0:T(8,128)(2,1)S(1)}, bf16[176,2048]{1,0:T(8,128)(2,1)S(1)}, u32[]{:S(2)}, u32[]{:S(2)}) %collective-permute-start.15) | collective-permute-done | bytes 720928 | tf_op jit(solution)/shard_map/ppermute | solution.py:61
  309.8 35.4 %collective-permute-done.17 = bf16[176,2048]{1,0:T(8,128)(2,1)S(1)} collective-permute-done((bf16[176,2048]{1,0:T(8,128)(2,1)}, bf16[176,2048]{1,0:T(8,128)(2,1)S(1)}, u32[]{:S(2)}, u32[]{:S(2)}) %collective-permute-start.17) | collective-permute-done | bytes 720928 | tf_op jit(solution)/shard_map/ppermute | solution.py:62
  346.3 26.3 %collective-permute-done.13 = bf16[512,1280]{1,0:T(8,128)(2,1)S(1)} collective-permute-done((bf16[512,1280]{1,0:T(8,128)(2,1)}, bf16[512,1280]{1,0:T(8,128)(2,1)S(1)}, u32[]{:S(2)}, u32[]{:S(2)}) %collective-permute-start.13) | collective-permute-done | bytes 1310752 | tf_op jit(solution)/shard_map/ppermute | solution.py:62
  379.8 18.4 %fusion.22 = f32[1408,2048]{1,0:T(8,128)} fusion(bf16[2048,1408]{1,0:T(8,128)(2,1)} %select_dynamic-update-slice_fusion, bf16[2048,2048]{1,0:T(8,128)(2,1)S(1)} %copy-done.1, f32[2048]{0:T(1024)S(1)} %bitcast.165, f32[2048]{0:T(1024)S(1)} %add_rsqrt_fusion), kind=kOutput, calls=%fused_computation.44 | convolution fusion | flops 11827937280 | bytes 25706496 | tf_op jit(solution)/shard_map/dot_general | solution.py:21
  398.3 15.1 %multiply_convert_fusion.1 = (bf16[704,2048]{1,0:T(8,128)(2,1)S(1)}, bf16[704,2048]{1,0:T(8,128)(2,1)S(1)}, bf16[704,2048]{1,0:T(8,128)(2,1)}) fusion(f32[1408,2048]{1,0:T(8,128)} %fusion.22, bf16[704,2048]{1,0:T(8,128)(2,1)} %select_dynamic-update-slice_fusion.1, bf16[1,2048,2048]{2,1,0:T(8,128)(2,1)} %all-gather.17.cloned.1.call-done), kind=kOutput, calls=%fused_computation.24 | convolution fusion | flops 5927206912 | bytes 31457280 | tf_op jit(solution)/shard_map/dot_general | solution.py:21
  415.9 17.1 %convolution_convert_fusion.1 = bf16[2048,2048]{0,1:T(8,128)(2,1)} fusion(bf16[2048,1408]{1,0:T(8,128)(2,1)} %select_dynamic-update-slice_fusion, bf16[704,2048]{1,0:T(8,128)(2,1)S(1)} %get-tuple-element.83, bf16[704,2048]{1,0:T(8,128)(2,1)S(1)} %get-tuple-element.82), kind=kOutput, calls=%fused_computation.18 | convolution fusion | flops 11826888704 | bytes 19922944 | tf_op jit(solution)/shard_map/dot_general | solution.py:21
  436.7 67.9 %reduce-scatter.4.cloned.1.call-done = bf16[256,2048]{0,1:T(8,128)(2,1)} async-done(((bf16[2048,2048]{0,1:T(8,128)(2,1)}), bf16[256,2048]{0,1:T(8,128)(2,1)}) %reduce-scatter.4.cloned.1.call-update) | async-done | bytes 1048592 | tf_op jit(solution)/shard_map/reduce_scatter | solution.py:584
  518.7 11.3 %collective-permute-done.20 = bf16[256,256]{1,0:T(8,128)(2,1)S(1)} collective-permute-done((bf16[256,256]{1,0:T(8,128)(2,1)S(1)}, bf16[256,256]{1,0:T(8,128)(2,1)S(1)}, u32[]{:S(2)}, u32[]{:S(2)}) %collective-permute-start.20) | collective-permute-done | bytes 131104 | tf_op jit(solution)/shard_map/ppermute | solution.py:566
  534.5 11.0 %convolution_convert_fusion.3 = bf16[2048,2048]{0,1:T(8,128)(2,1)} fusion(bf16[704,2048]{1,0:T(8,128)(2,1)S(1)} %copy-done.29, bf16[704,2048]{1,0:T(8,128)(2,1)} %select_dynamic-update-slice_fusion.1), kind=kOutput, calls=%fused_computation.20 | convolution fusion | flops 5909774336 | bytes 14155776 | tf_op jit(solution)/shard_map/dot_general | solution.py:21
  545.5 28.1 %all-gather.13.cloned.1.call-done = bf16[2048,2048]{0,1:T(8,128)(2,1)} async-done(((bf16[256,2048]{0,1:T(8,128)(2,1)}), bf16[2048,2048]{0,1:T(8,128)(2,1)}) %all-gather.13.cloned.1.call-update) | async-done | bytes 8388624 | tf_op jit(solution)/shard_map/all_gather | solution.py:602
  580.3 25.0 %shard_map.204 = (f32[256,2048]{1,0:T(8,128)}, bf16[4,64,2048]{2,1,0:T(8,128)(2,1)}, bf16[4,64,2048]{2,1,0:T(8,128)(2,1)}) custom-call(s32[8,8]{1,0:T(8,128)} %add_convert_fusion.8.info_ref, bf16[256,2048]{1,0:T(8,128)(2,1)} %bitcast.156, bf16[4,64,2048]{2,1,0:T(8,128)(2,1)} %get-tuple-element.111.k_ref, bf16[4,64,2048]{2,1,0:T(8,128)(2,1)} %get-tuple-element.110.v_ref, ...), custom_call_target="tpu_custom_call" | custom-call | flops 3019898880 | bytes 7340032 | tf_op jit(solution)/shard_map/pallas_call | solution.py:329
  648.9 16.9 %convolution_convert_fusion.2 = bf16[2048,1408]{1,0:T(8,128)(2,1)S(1)} fusion(bf16[704,2048]{1,0:T(8,128)(2,1)} %copy-done.33, bf16[704,2048]{1,0:T(8,128)(2,1)S(1)} %copy-done.32, bf16[2048,2048]{1,0:T(8,128)(2,1)} %all-gather.11.cloned.1.call-done, f32[2048]{0:T(1024)S(1)} %bitcast.168, f32[2048]{0:T(1024)S(1)} %add_rsqrt_fusion), kind=kOutput, calls=%fused_computation.19 | convolution fusion | flops 11842355200 | bytes 19939328 | tf_op jit(solution)/shard_map/dot_general | solution.py:21
  684.8 78.3 %collective-permute-done.46 = bf16[96,1408]{1,0:T(8,128)(2,1)} collective-permute-done((bf16[96,1408]{1,0:T(8,128)(2,1)S(1)}, bf16[96,1408]{1,0:T(8,128)(2,1)}, u32[]{:S(2)}, u32[]{:S(2)}) %collective-permute-start.46) | collective-permute-done | bytes 270368 | tf_op jit(solution)/shard_map/ppermute | solution.py:29
  763.1 27.6 %collective-permute-start.47 = (bf16[96,1408]{1,0:T(8,128)(2,1)}, bf16[96,1408]{1,0:T(8,128)(2,1)}, u32[]{:S(2)}, u32[]{:S(2)}) collective-permute-start(bf16[96,1408]{1,0:T(8,128)(2,1)} %get-tuple-element.116), channel_id=1, source_target_pairs={{0,2},{1,3},{2,0},{3,1},{4,6},{5,7},{6,4},{7,5},{8,10},{9,11},{10,... | collective-permute-start | bytes 811016 | tf_op jit(solution)/shard_map/ppermute | solution.py:29
  790.6 11.6 %collective-permute-done.47 = bf16[96,1408]{1,0:T(8,128)(2,1)} collective-permute-done((bf16[96,1408]{1,0:T(8,128)(2,1)}, bf16[96,1408]{1,0:T(8,128)(2,1)}, u32[]{:S(2)}, u32[]{:S(2)}) %collective-permute-start.47) | collective-permute-done | bytes 270368 | tf_op jit(solution)/shard_map/ppermute | solution.py:29
  824.3 16.2 %collective-permute-done.50 = bf16[512,1408]{1,0:T(8,128)(2,1)S(1)} collective-permute-done((bf16[512,1408]{1,0:T(8,128)(2,1)S(1)}, bf16[512,1408]{1,0:T(8,128)(2,1)S(1)}, u32[]{:S(2)}, u32[]{:S(2)}) %collective-permute-start.50) | collective-permute-done | bytes 1441824 | tf_op jit(solution)/shard_map/ppermute | solution.py:40
  842.2 29.0 %collective-permute-done.51 = bf16[512,1408]{1,0:T(8,128)(2,1)S(1)} collective-permute-done((bf16[512,1408]{1,0:T(8,128)(2,1)S(1)}, bf16[512,1408]{1,0:T(8,128)(2,1)S(1)}, u32[]{:S(2)}, u32[]{:S(2)}) %collective-permute-start.51) | collective-permute-done | bytes 1441824 | tf_op jit(solution)/shard_map/ppermute | solution.py:40
  896.1 11.8 %collective-permute-done.36 = bf16[528,576]{1,0:T(8,128)(2,1)} collective-permute-done((bf16[528,576]{1,0:T(8,128)(2,1)}, bf16[528,576]{1,0:T(8,128)(2,1)}, u32[]{:S(2)}, u32[]{:S(2)}) %collective-permute-start.36) | collective-permute-done | bytes 608288 | tf_op jit(solution)/shard_map/ppermute | solution.py:29
  909.2 13.2 %collective-permute-done.38 = bf16[528,576]{1,0:T(8,128)(2,1)} collective-permute-done((bf16[528,576]{1,0:T(8,128)(2,1)}, bf16[528,576]{1,0:T(8,128)(2,1)}, u32[]{:S(2)}, u32[]{:S(2)}) %collective-permute-start.38) | collective-permute-done | bytes 608288 | tf_op jit(solution)/shard_map/ppermute | solution.py:29
  924.1 24.1 %collective-permute-done.37 = bf16[528,576]{1,0:T(8,128)(2,1)} collective-permute-done((bf16[528,576]{1,0:T(8,128)(2,1)}, bf16[528,576]{1,0:T(8,128)(2,1)}, u32[]{:S(2)}, u32[]{:S(2)}) %collective-permute-start.37) | collective-permute-done | bytes 608288 | tf_op jit(solution)/shard_map/ppermute | solution.py:29
  956.5 12.5 %collective-permute-done.41 = bf16[528,576]{1,0:T(8,128)(2,1)S(1)} collective-permute-done((bf16[528,576]{1,0:T(8,128)(2,1)S(1)}, bf16[528,576]{1,0:T(8,128)(2,1)S(1)}, u32[]{:S(2)}, u32[]{:S(2)}) %collective-permute-start.41) | collective-permute-done | bytes 608288 | tf_op jit(solution)/shard_map/ppermute | solution.py:40
  969.0 12.7 %collective-permute-done.40 = bf16[528,576]{1,0:T(8,128)(2,1)S(1)} collective-permute-done((bf16[528,576]{1,0:T(8,128)(2,1)S(1)}, bf16[528,576]{1,0:T(8,128)(2,1)S(1)}, u32[]{:S(2)}, u32[]{:S(2)}) %collective-permute-start.40) | collective-permute-done | bytes 608288 | tf_op jit(solution)/shard_map/ppermute | solution.py:40
  1001.7 11.0 %shard_map.207 = f32[1408,2048]{1,0:T(8,128)} custom-call(s32[1]{0:T(128)} %bitcast.37.lane_ref, bf16[4,176,2048]{2,1,0:T(8,128)(2,1)} %pad_maximum_fusion.4.mine_ref, bf16[4,176,2048]{2,1,0:T(8,128)(2,1)} %collective-permute-done.59.other_ref), custom_call_target="tpu_custom_call" | custom-call | bytes 17301504 | tf_op jit(solution)/shard_map/pallas_call | solution.py:419
  1012.7 14.4 %shard_map.206 = (f32[512,5632]{1,0:T(8,128)}, f32[512,5632]{1,0:T(8,128)}) custom-call(s32[1]{0:T(128)} %bitcast.37.lane_ref, bf16[4,512,1408]{2,1,0:T(8,128)(2,1)} %pad_maximum_fusion.1.mine_ref, bf16[4,512,1408]{2,1,0:T(8,128)(2,1)} %collective-permute-done.52.other_ref), custom_call_target="tpu_custom_call" | custom-call | bytes 34603008 | tf_op jit(solution)/shard_map/pallas_call | solution.py:399
  1027.7 12.1 %shard_map.205 = (f32[512,2048]{1,0:T(8,128)}, f32[512,256]{1,0:T(8,128)}, f32[512,256]{1,0:T(8,128)}, f32[512,2048]{1,0:T(8,128)}) custom-call(s32[1]{0:T(128)} %bitcast.37.lane_ref, bf16[4,528,576]{2,1,0:T(8,128)(2,1)} %pad_maximum_fusion.5.mine_ref, bf16[4,528,576]{2,1,0:T(8,128)(2,1)} %collective-permute-done.42.other_ref), custom_call_target="tpu_custom_call" | custom-call | bytes 14155776 | tf_op jit(solution)/shard_map/pallas_call | solution.py:399
  (344 shorter events, 328.1 us)
Async XLA Ops:
  7.2 61.9 %all-gather.15.cloned.1.call-start = ((), (), s32[]{:S(2)}) async-start(), calls=%async_computation.9 | async-start | bytes 9437184 | tf_op jit(solution)/shard_map/all_gather | solution.py:470
  9.5 170.4 %all-gather.9.cloned.1.call-start = ((), (), s32[]{:S(2)}) async-start(), calls=%async_computation.3 | async-start | bytes 9437184 | tf_op jit(solution)/shard_map/all_gather | solution.py:558
  126.2 247.9 %all-gather.11.cloned.1.call-start = ((), (), s32[]{:S(2)}) async-start(), calls=%async_computation.4 | async-start | bytes 9437184 | tf_op jit(solution)/shard_map/all_gather | solution.py:569
  186.9 211.4 %all-gather.17.cloned.1.call-start = ((), (), s32[]{:S(2)}) async-start(), calls=%async_computation.10 | async-start | bytes 9437184 | tf_op jit(solution)/shard_map/all_gather | solution.py:471
  187.5 317.2 %reduce-scatter.4.cloned.1.call-start = ((), (), s32[]{:S(2)}) async-start(), calls=%async_computation.5 | async-start | bytes 9437184 | tf_op jit(solution)/shard_map/reduce_scatter | solution.py:584
  191.9 63.6 %collective-permute-start.16 = (bf16[176,2048]{1,0:T(8,128)(2,1)S(1)}, bf16[176,2048]{1,0:T(8,128)(2,1)}, u32[]{:S(2)}, u32[]{:S(2)}) collective-permute-start(bf16[176,2048]{1,0:T(8,128)(2,1)S(1)} %get-tuple-element.77), channel_id=1, source_target_pairs={{0,2},{1,3},{2,0},{3,1},{4,6},{5,7},{6,4},{7,5},{8,10},{9,11},{10,... | collective-permute-start | bytes 2162696 | tf_op jit(solution)/shard_map/ppermute | solution.py:29
  194.3 106.8 %collective-permute-start.12 = (bf16[512,1280]{1,0:T(8,128)(2,1)S(1)}, bf16[512,1280]{1,0:T(8,128)(2,1)}, u32[]{:S(2)}, u32[]{:S(2)}) collective-permute-start(bf16[512,1280]{1,0:T(8,128)(2,1)S(1)} %slice.187), channel_id=1, source_target_pairs={{0,2},{1,3},{2,0},{3,1},{4,6},{5,7},{6,4},{7,5},{8,10},{9,11},{10,... | collective-permute-start | bytes 3932168 | tf_op jit(solution)/shard_map/ppermute | solution.py:29
  194.8 110.1 %collective-permute-start.11 = (bf16[512,1280]{1,0:T(8,128)(2,1)S(1)}, bf16[512,1280]{1,0:T(8,128)(2,1)}, u32[]{:S(2)}, u32[]{:S(2)}) collective-permute-start(bf16[512,1280]{1,0:T(8,128)(2,1)S(1)} %slice.187), channel_id=1, source_target_pairs={{1,0},{2,1},{3,2},{5,4},{6,5},{7,6},{9,8},{10,9},{11,10},{13,12},{... | collective-permute-start | bytes 3932168 | tf_op jit(solution)/shard_map/ppermute | solution.py:61
  196.1 106.3 %collective-permute-start.10 = (bf16[512,1280]{1,0:T(8,128)(2,1)S(1)}, bf16[512,1280]{1,0:T(8,128)(2,1)}, u32[]{:S(2)}, u32[]{:S(2)}) collective-permute-start(bf16[512,1280]{1,0:T(8,128)(2,1)S(1)} %slice.187), channel_id=1, source_target_pairs={{0,1},{1,2},{2,3},{4,5},{5,6},{6,7},{8,9},{9,10},{10,11},{12,13},{... | collective-permute-start | bytes 3932168 | tf_op jit(solution)/shard_map/ppermute | solution.py:60
  201.7 80.0 %collective-permute-start.14 = (bf16[176,2048]{1,0:T(8,128)(2,1)S(1)}, bf16[176,2048]{1,0:T(8,128)(2,1)}, u32[]{:S(2)}, u32[]{:S(2)}) collective-permute-start(bf16[176,2048]{1,0:T(8,128)(2,1)S(1)} %get-tuple-element.77), channel_id=1, source_target_pairs={{0,1},{1,2},{2,3},{4,5},{5,6},{6,7},{8,9},{9,10},{10,11},{12,13},{... | collective-permute-start | bytes 2162696 | tf_op jit(solution)/shard_map/ppermute | solution.py:60
  255.4 42.7 %collective-permute-start.15 = (bf16[176,2048]{1,0:T(8,128)(2,1)S(1)}, bf16[176,2048]{1,0:T(8,128)(2,1)S(1)}, u32[]{:S(2)}, u32[]{:S(2)}) collective-permute-start(bf16[176,2048]{1,0:T(8,128)(2,1)S(1)} %get-tuple-element.77), channel_id=1, source_target_pairs={{1,0},{2,1},{3,2},{5,4},{6,5},{7,6},{9,8},{10,9},{11,10},{13,12},{... | collective-permute-start | bytes 2162696 | tf_op jit(solution)/shard_map/ppermute | solution.py:61
  281.7 63.5 %collective-permute-start.17 = (bf16[176,2048]{1,0:T(8,128)(2,1)}, bf16[176,2048]{1,0:T(8,128)(2,1)S(1)}, u32[]{:S(2)}, u32[]{:S(2)}) collective-permute-start(bf16[176,2048]{1,0:T(8,128)(2,1)} %collective-permute-done.16), channel_id=1, source_target_pairs={{2,3},{1,0},{6,7},{5,4},{10,11},{9,8},{14,15},{13,12},{18,19},{17,... | collective-permute-start | bytes 2162696 | tf_op jit(solution)/shard_map/ppermute | solution.py:62
  301.1 71.6 %collective-permute-start.13 = (bf16[512,1280]{1,0:T(8,128)(2,1)}, bf16[512,1280]{1,0:T(8,128)(2,1)S(1)}, u32[]{:S(2)}, u32[]{:S(2)}) collective-permute-start(bf16[512,1280]{1,0:T(8,128)(2,1)} %collective-permute-done.12), channel_id=1, source_target_pairs={{2,3},{1,0},{6,7},{5,4},{10,11},{9,8},{14,15},{13,12},{18,19},{17,... | collective-permute-start | bytes 3932168 | tf_op jit(solution)/shard_map/ppermute | solution.py:62
  433.1 140.6 %all-gather.13.cloned.1.call-start = ((), (), s32[]{:S(2)}) async-start(), calls=%async_computation.6 | async-start | bytes 9437184 | tf_op jit(solution)/shard_map/all_gather | solution.py:602
  510.4 529.5 %reduce-scatter.8.cloned.1.call-start = ((), (), s32[]{:S(2)}) async-start(), calls=%async_computation.8 | async-start | bytes 9437184 | tf_op jit(solution)/shard_map/reduce_scatter | solution.py:626
  647.2 394.4 %reduce-scatter.6.cloned.1.call-start = ((), (), s32[]{:S(2)}) async-start(), calls=%async_computation.7 | async-start | bytes 9437184 | tf_op jit(solution)/shard_map/reduce_scatter | solution.py:605
  676.2 127.3 %collective-permute-start.43 = (bf16[416,1408]{1,0:T(8,128)(2,1)}, bf16[416,1408]{1,0:T(8,128)(2,1)}, u32[]{:S(2)}, u32[]{:S(2)}) collective-permute-start(bf16[416,1408]{1,0:T(8,128)(2,1)} %get-tuple-element.95), channel_id=1, source_target_pairs={{0,1},{1,2},{2,3},{3,0},{4,5},{5,6},{6,7},{7,4},{8,9},{9,10},{10,1... | collective-permute-start | bytes 3514376 | tf_op jit(solution)/shard_map/ppermute | solution.py:29
  676.2 127.2 %collective-permute-start.45 = (bf16[416,1408]{1,0:T(8,128)(2,1)S(1)}, bf16[416,1408]{1,0:T(8,128)(2,1)}, u32[]{:S(2)}, u32[]{:S(2)}) collective-permute-start(bf16[416,1408]{1,0:T(8,128)(2,1)S(1)} %get-tuple-element.96), channel_id=1, source_target_pairs={{0,3},{1,0},{2,1},{3,2},{4,7},{5,4},{6,5},{7,6},{8,11},{9,8},{10,9... | collective-permute-start | bytes 3514376 | tf_op jit(solution)/shard_map/ppermute | solution.py:29
  680.1 123.4 %collective-permute-start.44 = (bf16[416,1408]{1,0:T(8,128)(2,1)S(1)}, bf16[416,1408]{1,0:T(8,128)(2,1)}, u32[]{:S(2)}, u32[]{:S(2)}) collective-permute-start(bf16[416,1408]{1,0:T(8,128)(2,1)S(1)} %get-tuple-element.97), channel_id=1, source_target_pairs={{0,2},{1,3},{2,0},{3,1},{4,6},{5,7},{6,4},{7,5},{8,10},{9,11},{10,... | collective-permute-start | bytes 3514376 | tf_op jit(solution)/shard_map/ppermute | solution.py:29
  680.9 82.1 %collective-permute-start.46 = (bf16[96,1408]{1,0:T(8,128)(2,1)S(1)}, bf16[96,1408]{1,0:T(8,128)(2,1)}, u32[]{:S(2)}, u32[]{:S(2)}) collective-permute-start(bf16[96,1408]{1,0:T(8,128)(2,1)S(1)} %get-tuple-element.114), channel_id=1, source_target_pairs={{0,1},{1,2},{2,3},{3,0},{4,5},{5,6},{6,7},{7,4},{8,9},{9,10},{10,1... | collective-permute-start | bytes 811016 | tf_op jit(solution)/shard_map/ppermute | solution.py:29
  681.8 108.8 %collective-permute-start.48 = (bf16[96,1408]{1,0:T(8,128)(2,1)}, bf16[96,1408]{1,0:T(8,128)(2,1)}, u32[]{:S(2)}, u32[]{:S(2)}) collective-permute-start(bf16[96,1408]{1,0:T(8,128)(2,1)} %get-tuple-element.115), channel_id=1, source_target_pairs={{0,3},{1,0},{2,1},{3,2},{4,7},{5,4},{6,5},{7,6},{8,11},{9,8},{10,9... | collective-permute-start | bytes 811016 | tf_op jit(solution)/shard_map/ppermute | solution.py:29
  763.1 39.2 %collective-permute-start.47 = (bf16[96,1408]{1,0:T(8,128)(2,1)}, bf16[96,1408]{1,0:T(8,128)(2,1)}, u32[]{:S(2)}, u32[]{:S(2)}) collective-permute-start(bf16[96,1408]{1,0:T(8,128)(2,1)} %get-tuple-element.116), channel_id=1, source_target_pairs={{0,2},{1,3},{2,0},{3,1},{4,6},{5,7},{6,4},{7,5},{8,10},{9,11},{10,... | collective-permute-start | bytes 811016 | tf_op jit(solution)/shard_map/ppermute | solution.py:29
  809.2 62.0 %collective-permute-start.51 = (bf16[512,1408]{1,0:T(8,128)(2,1)S(1)}, bf16[512,1408]{1,0:T(8,128)(2,1)S(1)}, u32[]{:S(2)}, u32[]{:S(2)}) collective-permute-start(bf16[512,1408]{1,0:T(8,128)(2,1)S(1)} %get-tuple-element.113), channel_id=1, source_target_pairs={{0,24},{4,28},{8,16},{12,20},{16,8},{20,12},{24,0},{28,4},{1,25},{... | collective-permute-start | bytes 4325384 | tf_op jit(solution)/shard_map/ppermute | solution.py:40
  820.4 67.2 %collective-permute-start.53 = (bf16[176,2048]{1,0:T(8,128)(2,1)}, bf16[176,2048]{1,0:T(8,128)(2,1)}, u32[]{:S(2)}, u32[]{:S(2)}) collective-permute-start(bf16[176,2048]{1,0:T(8,128)(2,1)} %get-tuple-element.98), channel_id=1, source_target_pairs={{0,1},{1,2},{2,3},{3,0},{4,5},{5,6},{6,7},{7,4},{8,9},{9,10},{10,1... | collective-permute-start | bytes 2162696 | tf_op jit(solution)/shard_map/ppermute | solution.py:29
  820.4 71.1 %collective-permute-start.55 = (bf16[176,2048]{1,0:T(8,128)(2,1)}, bf16[176,2048]{1,0:T(8,128)(2,1)}, u32[]{:S(2)}, u32[]{:S(2)}) collective-permute-start(bf16[176,2048]{1,0:T(8,128)(2,1)} %get-tuple-element.99), channel_id=1, source_target_pairs={{0,3},{1,0},{2,1},{3,2},{4,7},{5,4},{6,5},{7,6},{8,11},{9,8},{10,9... | collective-permute-start | bytes 2162696 | tf_op jit(solution)/shard_map/ppermute | solution.py:29
  840.4 51.1 %collective-permute-start.54 = (bf16[176,2048]{1,0:T(8,128)(2,1)S(1)}, bf16[176,2048]{1,0:T(8,128)(2,1)}, u32[]{:S(2)}, u32[]{:S(2)}) collective-permute-start(bf16[176,2048]{1,0:T(8,128)(2,1)S(1)} %get-tuple-element.100), channel_id=1, source_target_pairs={{0,2},{1,3},{2,0},{3,1},{4,6},{5,7},{6,4},{7,5},{8,10},{9,11},{10,... | collective-permute-start | bytes 2162696 | tf_op jit(solution)/shard_map/ppermute | solution.py:29
  874.7 138.0 %collective-permute-start.52 = (bf16[4,512,1408]{2,1,0:T(8,128)(2,1)}, bf16[4,512,1408]{2,1,0:T(8,128)(2,1)}, u32[]{:S(2)}, u32[]{:S(2)}) collective-permute-start(bf16[4,512,1408]{2,1,0:T(8,128)(2,1)} %pad_maximum_fusion.1.mine_ref), channel_id=1, source_target_pairs={{0,4},{4,0},{8,12},{12,8},{16,20},{20,16},{24,28},{28,24},{1,5},{5... | collective-permute-start | bytes 17301512 | tf_op jit(solution)/shard_map/ppermute | solution.py:34
  891.5 56.6 %collective-permute-start.37 = (bf16[528,576]{1,0:T(8,128)(2,1)}, bf16[528,576]{1,0:T(8,128)(2,1)}, u32[]{:S(2)}, u32[]{:S(2)}) collective-permute-start(bf16[528,576]{1,0:T(8,128)(2,1)} %get-tuple-element.103), channel_id=1, source_target_pairs={{0,2},{1,3},{2,0},{3,1},{4,6},{5,7},{6,4},{7,5},{8,10},{9,11},{10,... | collective-permute-start | bytes 1824776 | tf_op jit(solution)/shard_map/ppermute | solution.py:29
  893.8 58.5 %collective-permute-start.58 = (bf16[176,2048]{1,0:T(8,128)(2,1)S(1)}, bf16[176,2048]{1,0:T(8,128)(2,1)}, u32[]{:S(2)}, u32[]{:S(2)}) collective-permute-start(bf16[176,2048]{1,0:T(8,128)(2,1)S(1)} %add_convert_fusion.2), channel_id=1, source_target_pairs={{0,24},{4,28},{8,16},{12,20},{16,8},{20,12},{24,0},{28,4},{1,25},{... | collective-permute-start | bytes 2162696 | tf_op jit(solution)/shard_map/ppermute | solution.py:40
  907.9 45.3 %collective-permute-start.57 = (bf16[176,2048]{1,0:T(8,128)(2,1)S(1)}, bf16[176,2048]{1,0:T(8,128)(2,1)}, u32[]{:S(2)}, u32[]{:S(2)}) collective-permute-start(bf16[176,2048]{1,0:T(8,128)(2,1)S(1)} %add_convert_fusion.2), channel_id=1, source_target_pairs={{0,16},{4,20},{8,24},{12,28},{16,0},{20,4},{24,8},{28,12},{1,17},{... | collective-permute-start | bytes 2162696 | tf_op jit(solution)/shard_map/ppermute | solution.py:40
  956.5 45.2 %collective-permute-start.59 = (bf16[4,176,2048]{2,1,0:T(8,128)(2,1)}, bf16[4,176,2048]{2,1,0:T(8,128)(2,1)}, u32[]{:S(2)}, u32[]{:S(2)}) collective-permute-start(bf16[4,176,2048]{2,1,0:T(8,128)(2,1)} %pad_maximum_fusion.4.mine_ref), channel_id=1, source_target_pairs={{0,4},{4,0},{8,12},{12,8},{16,20},{20,16},{24,28},{28,24},{1,5},{5... | collective-permute-start | bytes 8650760 | tf_op jit(solution)/shard_map/ppermute | solution.py:34
  983.5 44.2 %collective-permute-start.42 = (bf16[4,528,576]{2,1,0:T(8,128)(2,1)}, bf16[4,528,576]{2,1,0:T(8,128)(2,1)}, u32[]{:S(2)}, u32[]{:S(2)}) collective-permute-start(bf16[4,528,576]{2,1,0:T(8,128)(2,1)} %pad_maximum_fusion.5.mine_ref), channel_id=1, source_target_pairs={{0,4},{4,0},{8,12},{12,8},{16,20},{20,16},{24,28},{28,24},{1,5},{5... | collective-permute-start | bytes 7299080 | tf_op jit(solution)/shard_map/ppermute | solution.py:34
  (74 other events, 1317.1 us)
Sparse Core Ops, SparseCore 0:
  10.5 58.5 all-gather.14
  126.3 53.6 all-gather.8
  187.0 54.2 all-gather.10
  243.1 54.2 all-gather.16
  433.2 71.4 reduce-scatter.3
  510.5 63.0 all-gather.12
  647.3 70.5 reduce-scatter.7
  721.4 71.2 reduce-scatter.5

commit v4 on v3

--- a/solution.py
+++ b/solution.py
@@ -645,14 +645,20 @@
     gain_own = sum(gain_sent[1:], gain_sent[0])
     gain_stack = chip_stack(gain_own)
     gain_own = sum(gain_stack[1:], gain_stack[0])
-    gain_own = gain_own + swap_cores(gain_own)
+    gain_other = swap_cores(gain_own)
+    gain_own = gain_own + gain_other
+    gain_one_out, gain_two_out = gain_own[0], gain_own[1]
 
     down_sum = plane_sum(down_sent)
     down_mine = jnp.stack(chip_stack(down_sum), axis=0)
     down_other = swap_cores(down_mine)
-    mlp_sum = jnp.concatenate([plane_sum(mlp_sent), plane_sum(mlp_tail_sent)], axis=0)
+    mlp_sum = plane_sum(mlp_sent)
     mlp_mine = jnp.stack(chip_stack(mlp_sum), axis=0)
     mlp_other = swap_cores(mlp_mine)
+    mlp_tail_mine = jnp.stack(chip_stack(plane_sum(mlp_tail_sent)), axis=0)
+    mlp_tail_other = swap_cores(mlp_tail_mine)
+    mlp_mine = jnp.concatenate([mlp_mine, mlp_tail_mine], axis=1)
+    mlp_other = jnp.concatenate([mlp_other, mlp_tail_other], axis=1)
     attn_sum = plane_sum(attn_sent)
     attn_mine = jnp.stack(chip_stack(attn_sum), axis=0)
     attn_other = swap_cores(attn_mine)
@@ -685,12 +691,12 @@
     return (
         block_out,
         tokens_grad,
-        gain_own[0],
+        gain_one_out,
         query_out,
         key_out,
         value_out,
         out_out,
-        gain_own[1],
+        gain_two_out,
         gate_out,
         up_out,
         down_out,

time: 1070 us -> 1140 us (1.065)
  starting transfers between devices: 109 us -> 167 us
  other arithmetic: 58.1 us -> 80.9 us
  waiting for transfers between devices: 593 us -> 581 us
    ppermute x29, starting transfers between devices: 69.8 us -> 129 us  [shift(): return lax.ppermute(value, SHARD, pairs)]
    ppermute x2, waiting for transfers between devices: 61.8 us -> 36.5 us  [forwarded(): far = lax.ppermute(across, SHARD, [(2, 3), (1, 0)])]
    ppermute x2, waiting for transfers between devices: 22.3 us -> 0.14 us  [forwarded(): up = lax.ppermute(value, SHARD, [(0, 1), (1, 2), (2, 3)])]
    ppermute x12 -> x15, waiting for transfers between devices: 75.2 us -> 91.7 us  [swap_chips(): return lax.ppermute(value, DP, pairs)]
    ppermute x29, waiting for transfers between devices: 287 us -> 301 us  [shift(): return lax.ppermute(value, SHARD, pairs)]
    ppermute x2, waiting for transfers between devices: 13 us -> 0.01 us  [forwarded(): down = lax.ppermute(value, SHARD, [(1, 0), (2, 1), (3, 2)])]
    concatenate x0 -> x2, other arithmetic: none -> 12.9 us  [the longest x1 7.35 us: on_device(): mlp_mine = jnp.concatenate([mlp_mine, mlp_tail_mine], axis=1)]
  transfers between devices with their start and end apart: 68 -> 72, of which waited for: 36 -> 30; matrix products, arithmetic and copies ran while one was open for 15% -> 16% of each run, Pallas kernels for 4% -> 3%
where the time goes in v4:
time: 1140 us; the launch traced here: 1130 us
  waiting for transfers between devices  581 us (51%)
  starting transfers between devices  167 us (15%)
  matrix products  125 us (11%)
  other arithmetic  80.9 us (7%)
  local copies, waits for them, and re-layouts  77.4 us (7%)
  Pallas kernels  74.5 us (7%)
  between operations  15.8 us (1%)
    ppermute x29, waiting for transfers between devices, shift(): return lax.ppermute(value, SHARD, pairs)  301 us
    ppermute x29, starting transfers between devices, shift(): return lax.ppermute(value, SHARD, pairs)  129 us
    dot_general x12, matrix products, contract(): lax.dot_general(left, right, (((left_dim,), (right_dim,)), ((), ())), pre...  125 us
    ppermute x15, waiting for transfers between devices, swap_chips(): return lax.ppermute(value, DP, pairs)  91.7 us
    reduce_scatter x1, waiting for transfers between devices, on_device(): lax.psum_scatter(hidden_two_grad, DP, scatter_dimension=0, tiled=True)  70.1 us
    ppermute x2, waiting for transfers between devices, forwarded(): far = lax.ppermute(across, SHARD, [(2, 3), (1, 0)])  36.5 us
    all_gather x1, waiting for transfers between devices, on_device(): branch_grad = lax.all_gather(middle_grad_low, DP, axis=0, tiled=True)  30.7 us
    pallas_call x2, Pallas kernels, spread_call(): pl.pallas_call(kernel, out_shape=tuple((jax.ShapeDtypeStruct((rows, w), F...  26.5 us
  transfers between devices with their start and end apart: 72, of which 30 were waited for; matrix products, arithmetic and copies ran while one was open for 16% of the time, Pallas kernels for 3%

profile of v4, /device:TPU:0, one launch (start us, length us, event | category | flops | bytes accessed | tf_op | source)
XLA Modules:
  0.0 1129.8 jit_solution(4511108999938691803)
XLA Ops:
  31.1 13.9 %collective-permute-done.4 = bf16[544,320]{1,0:T(8,128)(2,1)} collective-permute-done((bf16[544,320]{1,0:T(8,128)(2,1)S(1)}, bf16[544,320]{1,0:T(8,128)(2,1)}, u32[]{:S(2)}, u32[]{:S(2)}) %collective-permute-start.4) | collective-permute-done | bytes 348192 | tf_op jit(solution)/shard_map/ppermute | solution.py:29
  48.9 20.2 %all-gather.15.cloned.1.call-done = bf16[1,2048,2048]{1,2,0:T(8,128)(2,1)} async-done(((bf16[1,256,2048]{1,2,0:T(8,128)(2,1)}), bf16[1,2048,2048]{1,2,0:T(8,128)(2,1)}) %all-gather.15.cloned.1.call-update) | async-done | bytes 8388624 | tf_op jit(solution)/shard_map/all_gather | solution.py:470
  91.0 16.2 %collective-permute-done.7 = bf16[64,2048]{1,0:T(8,128)(2,1)} collective-permute-done((bf16[64,2048]{1,0:T(8,128)(2,1)S(1)}, bf16[64,2048]{1,0:T(8,128)(2,1)}, u32[]{:S(2)}, u32[]{:S(2)}) %collective-permute-start.7) | collective-permute-done | bytes 262176 | tf_op jit(solution)/shard_map/ppermute | solution.py:29
  113.8 12.4 %shard_map.203 = (bf16[256,2048]{1,0:T(8,128)(2,1)}, f32[8,2,512]{2,1,0:T(2,128)}) custom-call(s32[8,8]{1,0:T(8,128)} %add_convert_fusion.8.info_ref, bf16[256,2048]{1,0:T(8,128)(2,1)} %bitcast.159, bf16[4,64,2048]{2,1,0:T(8,128)(2,1)} %get-tuple-element.111.k_ref, bf16[4,64,2048]{2,1,0:T(8,128)(2,1)} %get-tuple-element.110.v_ref), custom_call_target="tpu_custom_call" | custom-call | flops 1207959552 | bytes 7340032 | tf_op jit(solution)/shard_map/pallas_call | solution.py:309
  149.2 16.1 %collective-permute-done.1 = bf16[512,384]{1,0:T(8,128)(2,1)S(1)} collective-permute-done((bf16[512,384]{1,0:T(8,128)(2,1)S(1)}, bf16[512,384]{1,0:T(8,128)(2,1)S(1)}, u32[]{:S(2)}, u32[]{:S(2)}) %collective-permute-start.1) | collective-permute-done | bytes 393248 | tf_op jit(solution)/shard_map/ppermute | solution.py:29
  166.1 13.9 %all-gather.9.cloned.1.call-done = bf16[2048,2048]{1,0:T(8,128)(2,1)} async-done(((bf16[256,2048]{1,0:T(8,128)(2,1)}), bf16[2048,2048]{1,0:T(8,128)(2,1)}) %all-gather.9.cloned.1.call-update) | async-done | bytes 8388624 | tf_op jit(solution)/shard_map/all_gather | solution.py:558
  215.8 104.5 %collective-permute-done.16 = bf16[176,2048]{1,0:T(8,128)(2,1)} collective-permute-done((bf16[176,2048]{1,0:T(8,128)(2,1)S(1)}, bf16[176,2048]{1,0:T(8,128)(2,1)}, u32[]{:S(2)}, u32[]{:S(2)}) %collective-permute-start.16) | collective-permute-done | bytes 720928 | tf_op jit(solution)/shard_map/ppermute | solution.py:29
  335.3 10.9 collective-permute-done.17
  347.3 25.7 %collective-permute-done.13 = bf16[512,1280]{1,0:T(8,128)(2,1)S(1)} collective-permute-done((bf16[512,1280]{1,0:T(8,128)(2,1)}, bf16[512,1280]{1,0:T(8,128)(2,1)S(1)}, u32[]{:S(2)}, u32[]{:S(2)}) %collective-permute-start.13) | collective-permute-done | bytes 1310752 | tf_op jit(solution)/shard_map/ppermute | solution.py:62
  380.1 18.4 %fusion.22 = f32[1408,2048]{1,0:T(8,128)} fusion(bf16[2048,1408]{1,0:T(8,128)(2,1)} %select_dynamic-update-slice_fusion, bf16[2048,2048]{1,0:T(8,128)(2,1)S(1)} %copy-done.1, f32[2048]{0:T(1024)S(1)} %bitcast.170, f32[2048]{0:T(1024)S(1)} %add_rsqrt_fusion), kind=kOutput, calls=%fused_computation.46 | convolution fusion | flops 11827937280 | bytes 25706496 | tf_op jit(solution)/shard_map/dot_general | solution.py:21
  398.5 15.1 %multiply_convert_fusion.1 = (bf16[704,2048]{1,0:T(8,128)(2,1)S(1)}, bf16[704,2048]{1,0:T(8,128)(2,1)S(1)}, bf16[704,2048]{1,0:T(8,128)(2,1)}) fusion(f32[1408,2048]{1,0:T(8,128)} %fusion.22, bf16[704,2048]{1,0:T(8,128)(2,1)} %select_dynamic-update-slice_fusion.1, bf16[1,2048,2048]{2,1,0:T(8,128)(2,1)} %all-gather.17.cloned.1.call-done), kind=kOutput, calls=%fused_computation.25 | convolution fusion | flops 5927206912 | bytes 31457280 | tf_op jit(solution)/shard_map/dot_general | solution.py:21
  416.2 17.1 %convolution_convert_fusion.1 = bf16[2048,2048]{0,1:T(8,128)(2,1)} fusion(bf16[2048,1408]{1,0:T(8,128)(2,1)} %select_dynamic-update-slice_fusion, bf16[704,2048]{1,0:T(8,128)(2,1)S(1)} %get-tuple-element.83, bf16[704,2048]{1,0:T(8,128)(2,1)S(1)} %get-tuple-element.82), kind=kOutput, calls=%fused_computation.18 | convolution fusion | flops 11826888704 | bytes 19922944 | tf_op jit(solution)/shard_map/dot_general | solution.py:21
  436.6 70.1 %reduce-scatter.4.cloned.1.call-done = bf16[256,2048]{0,1:T(8,128)(2,1)} async-done(((bf16[2048,2048]{0,1:T(8,128)(2,1)}), bf16[256,2048]{0,1:T(8,128)(2,1)}) %reduce-scatter.4.cloned.1.call-update) | async-done | bytes 1048592 | tf_op jit(solution)/shard_map/reduce_scatter | solution.py:584
  532.6 11.0 convolution_convert_fusion.3
  543.7 30.7 %all-gather.13.cloned.1.call-done = bf16[2048,2048]{0,1:T(8,128)(2,1)} async-done(((bf16[256,2048]{0,1:T(8,128)(2,1)}), bf16[2048,2048]{0,1:T(8,128)(2,1)}) %all-gather.13.cloned.1.call-update) | async-done | bytes 8388624 | tf_op jit(solution)/shard_map/all_gather | solution.py:602
  581.1 25.0 %shard_map.204 = (f32[256,2048]{1,0:T(8,128)}, bf16[4,64,2048]{2,1,0:T(8,128)(2,1)}, bf16[4,64,2048]{2,1,0:T(8,128)(2,1)}) custom-call(s32[8,8]{1,0:T(8,128)} %add_convert_fusion.8.info_ref, bf16[256,2048]{1,0:T(8,128)(2,1)} %bitcast.160, bf16[4,64,2048]{2,1,0:T(8,128)(2,1)} %get-tuple-element.111.k_ref, bf16[4,64,2048]{2,1,0:T(8,128)(2,1)} %get-tuple-element.110.v_ref, ...), custom_call_target="tpu_custom_call" | custom-call | flops 3019898880 | bytes 7340032 | tf_op jit(solution)/shard_map/pallas_call | solution.py:329
  622.1 10.5 collective-permute-done.27
  634.1 10.0 fusion.3
  644.2 9.6 fusion.13
  663.7 17.8 %convolution_convert_fusion.2 = bf16[2048,1408]{1,0:T(8,128)(2,1)S(1)} fusion(bf16[704,2048]{1,0:T(8,128)(2,1)} %copy-done.46, bf16[704,2048]{1,0:T(8,128)(2,1)} %copy-done.45, bf16[2048,2048]{1,0:T(8,128)(2,1)} %all-gather.11.cloned.1.call-done, f32[2048]{0:T(1024)S(1)} %bitcast.173, f32[2048]{0:T(1024)S(1)} %add_rsqrt_fusion), kind=kOutput, calls=%fused_computation.19 | convolution fusion | flops 11842355200 | bytes 19939328 | tf_op jit(solution)/shard_map/dot_general | solution.py:21
  693.7 39.9 %collective-permute-done.58 = bf16[176,2048]{1,0:T(8,128)(2,1)} collective-permute-done((bf16[176,2048]{1,0:T(8,128)(2,1)}, bf16[176,2048]{1,0:T(8,128)(2,1)}, u32[]{:S(2)}, u32[]{:S(2)}) %collective-permute-start.58) | collective-permute-done | bytes 720928 | tf_op jit(solution)/shard_map/ppermute | solution.py:29
  733.6 51.9 %collective-permute-start.50 = (bf16[96,1408]{1,0:T(8,128)(2,1)S(1)}, bf16[96,1408]{1,0:T(8,128)(2,1)S(1)}, u32[]{:S(2)}, u32[]{:S(2)}) collective-permute-start(bf16[96,1408]{1,0:T(8,128)(2,1)S(1)} %get-tuple-element.114), channel_id=1, source_target_pairs={{0,2},{1,3},{2,0},{3,1},{4,6},{5,7},{6,4},{7,5},{8,10},{9,11},{10,... | collective-permute-start | bytes 811016 | tf_op jit(solution)/shard_map/ppermute | solution.py:29
  787.8 33.3 %collective-permute-start.49 = (bf16[96,1408]{1,0:T(8,128)(2,1)S(1)}, bf16[96,1408]{1,0:T(8,128)(2,1)S(1)}, u32[]{:S(2)}, u32[]{:S(2)}) collective-permute-start(bf16[96,1408]{1,0:T(8,128)(2,1)S(1)} %get-tuple-element.112), channel_id=1, source_target_pairs={{0,1},{1,2},{2,3},{3,0},{4,5},{5,6},{6,7},{7,4},{8,9},{9,10},{10,1... | collective-permute-start | bytes 811016 | tf_op jit(solution)/shard_map/ppermute | solution.py:29
  821.1 24.5 %collective-permute-done.44 = bf16[416,1408]{1,0:T(8,128)(2,1)} collective-permute-done((bf16[416,1408]{1,0:T(8,128)(2,1)}, bf16[416,1408]{1,0:T(8,128)(2,1)}, u32[]{:S(2)}, u32[]{:S(2)}) %collective-permute-start.44) | collective-permute-done | bytes 1171488 | tf_op jit(solution)/shard_map/ppermute | solution.py:29
  869.3 60.9 %collective-permute-done.61 = bf16[176,2048]{1,0:T(8,128)(2,1)} collective-permute-done((bf16[176,2048]{1,0:T(8,128)(2,1)S(1)}, bf16[176,2048]{1,0:T(8,128)(2,1)}, u32[]{:S(2)}, u32[]{:S(2)}) %collective-permute-start.61) | collective-permute-done | bytes 720928 | tf_op jit(solution)/shard_map/ppermute | solution.py:40
  966.9 12.2 %collective-permute-done.38 = bf16[528,576]{1,0:T(8,128)(2,1)} collective-permute-done((bf16[528,576]{1,0:T(8,128)(2,1)}, bf16[528,576]{1,0:T(8,128)(2,1)}, u32[]{:S(2)}, u32[]{:S(2)}) %collective-permute-start.38) | collective-permute-done | bytes 608288 | tf_op jit(solution)/shard_map/ppermute | solution.py:29
  980.7 38.5 %collective-permute-done.37 = bf16[528,576]{1,0:T(8,128)(2,1)} collective-permute-done((bf16[528,576]{1,0:T(8,128)(2,1)}, bf16[528,576]{1,0:T(8,128)(2,1)}, u32[]{:S(2)}, u32[]{:S(2)}) %collective-permute-start.37) | collective-permute-done | bytes 608288 | tf_op jit(solution)/shard_map/ppermute | solution.py:29
  1030.6 11.3 %collective-permute-done.41 = bf16[528,576]{1,0:T(8,128)(2,1)S(1)} collective-permute-done((bf16[528,576]{1,0:T(8,128)(2,1)S(1)}, bf16[528,576]{1,0:T(8,128)(2,1)S(1)}, u32[]{:S(2)}, u32[]{:S(2)}) %collective-permute-start.41) | collective-permute-done | bytes 608288 | tf_op jit(solution)/shard_map/ppermute | solution.py:40
  1041.9 13.1 %collective-permute-done.40 = bf16[528,576]{1,0:T(8,128)(2,1)S(1)} collective-permute-done((bf16[528,576]{1,0:T(8,128)(2,1)S(1)}, bf16[528,576]{1,0:T(8,128)(2,1)S(1)}, u32[]{:S(2)}, u32[]{:S(2)}) %collective-permute-start.40) | collective-permute-done | bytes 608288 | tf_op jit(solution)/shard_map/ppermute | solution.py:40
  1068.0 10.7 shard_map.207
  1085.5 14.4 %shard_map.206 = (f32[512,5632]{1,0:T(8,128)}, f32[512,5632]{1,0:T(8,128)}) custom-call(s32[1]{0:T(128)} %bitcast.37.lane_ref, bf16[4,512,1408]{2,1,0:T(8,128)(2,1)} %maximum_maximum_fusion.mine_ref, bf16[4,512,1408]{2,1,0:T(8,128)(2,1)} %pad_maximum_fusion.1.other_ref), custom_call_target="tpu_custom_call" | custom-call | bytes 34603008 | tf_op jit(solution)/shard_map/pallas_call | solution.py:399
  1100.5 12.1 %shard_map.205 = (f32[512,2048]{1,0:T(8,128)}, f32[512,256]{1,0:T(8,128)}, f32[512,256]{1,0:T(8,128)}, f32[512,2048]{1,0:T(8,128)}) custom-call(s32[1]{0:T(128)} %bitcast.37.lane_ref, bf16[4,528,576]{2,1,0:T(8,128)(2,1)} %pad_maximum_fusion.6.mine_ref, bf16[4,528,576]{2,1,0:T(8,128)(2,1)} %collective-permute-done.42.other_ref), custom_call_target="tpu_custom_call" | custom-call | bytes 14155776 | tf_op jit(solution)/shard_map/pallas_call | solution.py:399
  (380 shorter events, 321.9 us)
Async XLA Ops:
  7.2 61.9 %all-gather.15.cloned.1.call-start = ((), (), s32[]{:S(2)}) async-start(), calls=%async_computation.9 | async-start | bytes 9437184 | tf_op jit(solution)/shard_map/all_gather | solution.py:470
  9.5 170.4 %all-gather.9.cloned.1.call-start = ((), (), s32[]{:S(2)}) async-start(), calls=%async_computation.3 | async-start | bytes 9437184 | tf_op jit(solution)/shard_map/all_gather | solution.py:558
  126.2 248.2 %all-gather.11.cloned.1.call-start = ((), (), s32[]{:S(2)}) async-start(), calls=%async_computation.4 | async-start | bytes 9437184 | tf_op jit(solution)/shard_map/all_gather | solution.py:569
  186.9 211.6 %all-gather.17.cloned.1.call-start = ((), (), s32[]{:S(2)}) async-start(), calls=%async_computation.10 | async-start | bytes 9437184 | tf_op jit(solution)/shard_map/all_gather | solution.py:471
  187.5 319.2 %reduce-scatter.4.cloned.1.call-start = ((), (), s32[]{:S(2)}) async-start(), calls=%async_computation.5 | async-start | bytes 9437184 | tf_op jit(solution)/shard_map/reduce_scatter | solution.py:584
  196.1 131.8 %collective-permute-start.10 = (bf16[512,1280]{1,0:T(8,128)(2,1)S(1)}, bf16[512,1280]{1,0:T(8,128)(2,1)}, u32[]{:S(2)}, u32[]{:S(2)}) collective-permute-start(bf16[512,1280]{1,0:T(8,128)(2,1)S(1)} %slice.187), channel_id=1, source_target_pairs={{0,1},{1,2},{2,3},{4,5},{5,6},{6,7},{8,9},{9,10},{10,11},{12,13},{... | collective-permute-start | bytes 3932168 | tf_op jit(solution)/shard_map/ppermute | solution.py:60
  199.7 130.7 %collective-permute-start.11 = (bf16[512,1280]{1,0:T(8,128)(2,1)S(1)}, bf16[512,1280]{1,0:T(8,128)(2,1)}, u32[]{:S(2)}, u32[]{:S(2)}) collective-permute-start(bf16[512,1280]{1,0:T(8,128)(2,1)S(1)} %slice.187), channel_id=1, source_target_pairs={{1,0},{2,1},{3,2},{5,4},{6,5},{7,6},{9,8},{10,9},{11,10},{13,12},{... | collective-permute-start | bytes 3932168 | tf_op jit(solution)/shard_map/ppermute | solution.py:61
  201.0 125.6 %collective-permute-start.12 = (bf16[512,1280]{1,0:T(8,128)(2,1)S(1)}, bf16[512,1280]{1,0:T(8,128)(2,1)}, u32[]{:S(2)}, u32[]{:S(2)}) collective-permute-start(bf16[512,1280]{1,0:T(8,128)(2,1)S(1)} %slice.187), channel_id=1, source_target_pairs={{0,2},{1,3},{2,0},{3,1},{4,6},{5,7},{6,4},{7,5},{8,10},{9,11},{10,... | collective-permute-start | bytes 3932168 | tf_op jit(solution)/shard_map/ppermute | solution.py:29
  203.6 116.7 %collective-permute-start.16 = (bf16[176,2048]{1,0:T(8,128)(2,1)S(1)}, bf16[176,2048]{1,0:T(8,128)(2,1)}, u32[]{:S(2)}, u32[]{:S(2)}) collective-permute-start(bf16[176,2048]{1,0:T(8,128)(2,1)S(1)} %get-tuple-element.77), channel_id=1, source_target_pairs={{0,2},{1,3},{2,0},{3,1},{4,6},{5,7},{6,4},{7,5},{8,10},{9,11},{10,... | collective-permute-start | bytes 2162696 | tf_op jit(solution)/shard_map/ppermute | solution.py:29
  211.8 111.9 %collective-permute-start.15 = (bf16[176,2048]{1,0:T(8,128)(2,1)S(1)}, bf16[176,2048]{1,0:T(8,128)(2,1)S(1)}, u32[]{:S(2)}, u32[]{:S(2)}) collective-permute-start(bf16[176,2048]{1,0:T(8,128)(2,1)S(1)} %get-tuple-element.77), channel_id=1, source_target_pairs={{1,0},{2,1},{3,2},{5,4},{6,5},{7,6},{9,8},{10,9},{11,10},{13,12},{... | collective-permute-start | bytes 2162696 | tf_op jit(solution)/shard_map/ppermute | solution.py:61
  326.6 46.3 %collective-permute-start.13 = (bf16[512,1280]{1,0:T(8,128)(2,1)}, bf16[512,1280]{1,0:T(8,128)(2,1)S(1)}, u32[]{:S(2)}, u32[]{:S(2)}) collective-permute-start(bf16[512,1280]{1,0:T(8,128)(2,1)} %collective-permute-done.12), channel_id=1, source_target_pairs={{2,3},{1,0},{6,7},{5,4},{10,11},{9,8},{14,15},{13,12},{18,19},{17,... | collective-permute-start | bytes 3932168 | tf_op jit(solution)/shard_map/ppermute | solution.py:62
  433.3 141.1 %all-gather.13.cloned.1.call-start = ((), (), s32[]{:S(2)}) async-start(), calls=%async_computation.6 | async-start | bytes 9437184 | tf_op jit(solution)/shard_map/all_gather | solution.py:602
  513.0 599.5 %reduce-scatter.8.cloned.1.call-start = ((), (), s32[]{:S(2)}) async-start(), calls=%async_computation.8 | async-start | bytes 9437184 | tf_op jit(solution)/shard_map/reduce_scatter | solution.py:626
  644.1 470.2 %reduce-scatter.6.cloned.1.call-start = ((), (), s32[]{:S(2)}) async-start(), calls=%async_computation.7 | async-start | bytes 9437184 | tf_op jit(solution)/shard_map/reduce_scatter | solution.py:605
  684.0 49.6 %collective-permute-start.58 = (bf16[176,2048]{1,0:T(8,128)(2,1)}, bf16[176,2048]{1,0:T(8,128)(2,1)}, u32[]{:S(2)}, u32[]{:S(2)}) collective-permute-start(bf16[176,2048]{1,0:T(8,128)(2,1)} %get-tuple-element.100), channel_id=1, source_target_pairs={{0,2},{1,3},{2,0},{3,1},{4,6},{5,7},{6,4},{7,5},{8,10},{9,11},{10,... | collective-permute-start | bytes 2162696 | tf_op jit(solution)/shard_map/ppermute | solution.py:29
  685.1 48.5 %collective-permute-start.57 = (bf16[176,2048]{1,0:T(8,128)(2,1)S(1)}, bf16[176,2048]{1,0:T(8,128)(2,1)}, u32[]{:S(2)}, u32[]{:S(2)}) collective-permute-start(bf16[176,2048]{1,0:T(8,128)(2,1)S(1)} %get-tuple-element.98), channel_id=1, source_target_pairs={{0,1},{1,2},{2,3},{3,0},{4,5},{5,6},{6,7},{7,4},{8,9},{9,10},{10,1... | collective-permute-start | bytes 2162696 | tf_op jit(solution)/shard_map/ppermute | solution.py:29
  687.4 100.4 %collective-permute-start.45 = (bf16[416,1408]{1,0:T(8,128)(2,1)}, bf16[416,1408]{1,0:T(8,128)(2,1)}, u32[]{:S(2)}, u32[]{:S(2)}) collective-permute-start(bf16[416,1408]{1,0:T(8,128)(2,1)} %get-tuple-element.96), channel_id=1, source_target_pairs={{0,3},{1,0},{2,1},{3,2},{4,7},{5,4},{6,5},{7,6},{8,11},{9,8},{10,9... | collective-permute-start | bytes 3514376 | tf_op jit(solution)/shard_map/ppermute | solution.py:29
  690.7 154.9 %collective-permute-start.44 = (bf16[416,1408]{1,0:T(8,128)(2,1)}, bf16[416,1408]{1,0:T(8,128)(2,1)}, u32[]{:S(2)}, u32[]{:S(2)}) collective-permute-start(bf16[416,1408]{1,0:T(8,128)(2,1)} %get-tuple-element.97), channel_id=1, source_target_pairs={{0,2},{1,3},{2,0},{3,1},{4,6},{5,7},{6,4},{7,5},{8,10},{9,11},{10,... | collective-permute-start | bytes 3514376 | tf_op jit(solution)/shard_map/ppermute | solution.py:29
  690.8 156.6 %collective-permute-start.43 = (bf16[416,1408]{1,0:T(8,128)(2,1)S(1)}, bf16[416,1408]{1,0:T(8,128)(2,1)}, u32[]{:S(2)}, u32[]{:S(2)}) collective-permute-start(bf16[416,1408]{1,0:T(8,128)(2,1)S(1)} %get-tuple-element.95), channel_id=1, source_target_pairs={{0,1},{1,2},{2,3},{3,0},{4,5},{5,6},{6,7},{7,4},{8,9},{9,10},{10,1... | collective-permute-start | bytes 3514376 | tf_op jit(solution)/shard_map/ppermute | solution.py:29
  733.6 117.9 %collective-permute-start.51 = (bf16[96,1408]{1,0:T(8,128)(2,1)S(1)}, bf16[96,1408]{1,0:T(8,128)(2,1)S(1)}, u32[]{:S(2)}, u32[]{:S(2)}) collective-permute-start(bf16[96,1408]{1,0:T(8,128)(2,1)S(1)} %get-tuple-element.113), channel_id=1, source_target_pairs={{0,3},{1,0},{2,1},{3,2},{4,7},{5,4},{6,5},{7,6},{8,11},{9,8},{10,9... | collective-permute-start | bytes 811016 | tf_op jit(solution)/shard_map/ppermute | solution.py:29
  733.6 123.4 %collective-permute-start.50 = (bf16[96,1408]{1,0:T(8,128)(2,1)S(1)}, bf16[96,1408]{1,0:T(8,128)(2,1)S(1)}, u32[]{:S(2)}, u32[]{:S(2)}) collective-permute-start(bf16[96,1408]{1,0:T(8,128)(2,1)S(1)} %get-tuple-element.114), channel_id=1, source_target_pairs={{0,2},{1,3},{2,0},{3,1},{4,6},{5,7},{6,4},{7,5},{8,10},{9,11},{10,... | collective-permute-start | bytes 811016 | tf_op jit(solution)/shard_map/ppermute | solution.py:29
  787.8 70.7 %collective-permute-start.49 = (bf16[96,1408]{1,0:T(8,128)(2,1)S(1)}, bf16[96,1408]{1,0:T(8,128)(2,1)S(1)}, u32[]{:S(2)}, u32[]{:S(2)}) collective-permute-start(bf16[96,1408]{1,0:T(8,128)(2,1)S(1)} %get-tuple-element.112), channel_id=1, source_target_pairs={{0,1},{1,2},{2,3},{3,0},{4,5},{5,6},{6,7},{7,4},{8,9},{9,10},{10,1... | collective-permute-start | bytes 811016 | tf_op jit(solution)/shard_map/ppermute | solution.py:29
  850.3 86.2 %collective-permute-start.48 = (bf16[416,1408]{1,0:T(8,128)(2,1)S(1)}, bf16[416,1408]{1,0:T(8,128)(2,1)}, u32[]{:S(2)}, u32[]{:S(2)}) collective-permute-start(bf16[416,1408]{1,0:T(8,128)(2,1)S(1)} %add_convert_fusion), channel_id=1, source_target_pairs={{0,24},{4,28},{8,16},{12,20},{16,8},{20,12},{24,0},{28,4},{1,25},{... | collective-permute-start | bytes 3514376 | tf_op jit(solution)/shard_map/ppermute | solution.py:40
  851.5 85.6 %collective-permute-start.47 = (bf16[416,1408]{1,0:T(8,128)(2,1)S(1)}, bf16[416,1408]{1,0:T(8,128)(2,1)}, u32[]{:S(2)}, u32[]{:S(2)}) collective-permute-start(bf16[416,1408]{1,0:T(8,128)(2,1)S(1)} %add_convert_fusion), channel_id=1, source_target_pairs={{0,16},{4,20},{8,24},{12,28},{16,0},{20,4},{24,8},{28,12},{1,17},{... | collective-permute-start | bytes 3514376 | tf_op jit(solution)/shard_map/ppermute | solution.py:40
  857.0 80.1 %collective-permute-start.46 = (bf16[416,1408]{1,0:T(8,128)(2,1)S(1)}, bf16[416,1408]{1,0:T(8,128)(2,1)}, u32[]{:S(2)}, u32[]{:S(2)}) collective-permute-start(bf16[416,1408]{1,0:T(8,128)(2,1)S(1)} %add_convert_fusion), channel_id=1, source_target_pairs={{0,8},{4,12},{8,0},{12,4},{16,24},{20,28},{24,16},{28,20},{1,9},{5... | collective-permute-start | bytes 3514376 | tf_op jit(solution)/shard_map/ppermute | solution.py:40
  858.5 71.8 %collective-permute-start.61 = (bf16[176,2048]{1,0:T(8,128)(2,1)S(1)}, bf16[176,2048]{1,0:T(8,128)(2,1)}, u32[]{:S(2)}, u32[]{:S(2)}) collective-permute-start(bf16[176,2048]{1,0:T(8,128)(2,1)S(1)} %add_convert_fusion.2), channel_id=1, source_target_pairs={{0,16},{4,20},{8,24},{12,28},{16,0},{20,4},{24,8},{28,12},{1,17},{... | collective-permute-start | bytes 2162696 | tf_op jit(solution)/shard_map/ppermute | solution.py:40
  866.5 65.5 %collective-permute-start.60 = (bf16[176,2048]{1,0:T(8,128)(2,1)S(1)}, bf16[176,2048]{1,0:T(8,128)(2,1)}, u32[]{:S(2)}, u32[]{:S(2)}) collective-permute-start(bf16[176,2048]{1,0:T(8,128)(2,1)S(1)} %add_convert_fusion.2), channel_id=1, source_target_pairs={{0,8},{4,12},{8,0},{12,4},{16,24},{20,28},{24,16},{28,20},{1,9},{5... | collective-permute-start | bytes 2162696 | tf_op jit(solution)/shard_map/ppermute | solution.py:40
  937.1 122.5 %collective-permute-start.63 = (bf16[4,176,2048]{2,1,0:T(8,128)(2,1)}, bf16[4,176,2048]{2,1,0:T(8,128)(2,1)}, u32[]{:S(2)}, u32[]{:S(2)}) collective-permute-start(bf16[4,176,2048]{2,1,0:T(8,128)(2,1)} %pad_maximum_fusion.5.mine_ref), channel_id=1, source_target_pairs={{0,4},{4,0},{8,12},{12,8},{16,20},{20,16},{24,28},{28,24},{1,5},{5... | collective-permute-start | bytes 8650760 | tf_op jit(solution)/shard_map/ppermute | solution.py:34
  941.4 138.5 %collective-permute-start.55 = (bf16[4,416,1408]{2,1,0:T(8,128)(2,1)}, bf16[4,416,1408]{2,1,0:T(8,128)(2,1)}, u32[]{:S(2)}, u32[]{:S(2)}) collective-permute-start(bf16[4,416,1408]{2,1,0:T(8,128)(2,1)} %pad_maximum_fusion.2), channel_id=1, source_target_pairs={{0,4},{4,0},{8,12},{12,8},{16,20},{20,16},{24,28},{28,24},{1,5},{5... | collective-permute-start | bytes 14057480 | tf_op jit(solution)/shard_map/ppermute | solution.py:34
  960.4 58.8 %collective-permute-start.37 = (bf16[528,576]{1,0:T(8,128)(2,1)}, bf16[528,576]{1,0:T(8,128)(2,1)}, u32[]{:S(2)}, u32[]{:S(2)}) collective-permute-start(bf16[528,576]{1,0:T(8,128)(2,1)} %get-tuple-element.103), channel_id=1, source_target_pairs={{0,2},{1,3},{2,0},{3,1},{4,6},{5,7},{6,4},{7,5},{8,10},{9,11},{10,... | collective-permute-start | bytes 1824776 | tf_op jit(solution)/shard_map/ppermute | solution.py:29
  960.5 58.7 %collective-permute-start.36 = (bf16[528,576]{1,0:T(8,128)(2,1)}, bf16[528,576]{1,0:T(8,128)(2,1)}, u32[]{:S(2)}, u32[]{:S(2)}) collective-permute-start(bf16[528,576]{1,0:T(8,128)(2,1)} %get-tuple-element.101), channel_id=1, source_target_pairs={{0,1},{1,2},{2,3},{3,0},{4,5},{5,6},{6,7},{7,4},{8,9},{9,10},{10,1... | collective-permute-start | bytes 1824776 | tf_op jit(solution)/shard_map/ppermute | solution.py:29
  979.1 43.8 %collective-permute-start.31 = (f32[2,512]{1,0:T(2,128)S(1)}, f32[2,512]{1,0:T(2,128)S(1)}, u32[]{:S(2)}, u32[]{:S(2)}) collective-permute-start(f32[2,512]{1,0:T(2,128)S(1)} %get-tuple-element.129), channel_id=1, source_target_pairs={{0,3},{1,0},{2,1},{3,2},{4,7},{5,4},{6,5},{7,6},{8,11},{9,8},{10,9... | collective-permute-start | bytes 12296 | tf_op jit(solution)/shard_map/ppermute | solution.py:29
  (91 other events, 1950.3 us)
Sparse Core Ops, SparseCore 0:
  10.5 58.5 all-gather.14
  126.3 53.6 all-gather.8
  187.0 54.2 all-gather.10
  243.1 54.2 all-gather.16
  433.4 73.2 reduce-scatter.3
  513.2 61.1 all-gather.12
  644.2 74.9 reduce-scatter.7
  722.7 71.2 reduce-scatter.5
